TPU v7x, 32 devices: a whole 2x2x4 slice. The times are simulated.
32 devices in a mesh: expert: 4 (over y, x), shard: 8 (over z, core).
Axes of the slice: x: 2, y: 2, z: 4, core: 2. Of those that a mesh axis runs over, the one named last changes fastest.
Arguments:
- inputs: bfloat16 [4096, 1536], P(('expert', 'shard')), may hold values from -6 to 6
- cotangent: bfloat16 [4096, 1536], P(('expert', 'shard')), may hold values from -6 to 6
- routes: int32 [4096, 8], P(('expert', 'shard')), may hold values from 0 to 39, all different within a row; in each aligned block of 128 rows (0 to 127, 128 to 255, ...) at most 38 rows name the same one
- attn_gain: bfloat16 [1536], P('shard'), may hold values from 0.5 to 1.5
- w_query: bfloat16 [1536, 1536], P('shard'), may hold values from -0.22963966 to 0.22963966
- key_matrix: bfloat16 [1536, 512], P('shard'), may hold values from -0.22963966 to 0.22963966
- value_matrix: bfloat16 [1536, 512], P('shard'), may hold values from -0.15625 to 0.15625
- w_output: bfloat16 [1536, 1536], P('shard'), may hold values from -2.5 to 2.5
- moe_gain: bfloat16 [1536], P('shard'), may hold values from 0.5 to 1.5
- w_router: bfloat16 [1536, 40], P('shard'), may hold values from -0.38273277 to 0.38273277
- w_experts: bfloat16 [1536, 40, 1536], P('shard', 'expert'), may hold values from -0.25 to 0.25
Outputs:
- outputs: bfloat16 [4096, 1536], P(('expert', 'shard'))
- grad_inputs: float32 [4096, 1536], P(('expert', 'shard'))
- grad_attn_gain: float32 [1536], P('shard')
- grad_w_query: float32 [1536, 1536], P('shard')
- grad_w_key: float32 [1536, 512], P('shard')
- grad_w_value: float32 [1536, 512], P('shard')
- grad_w_output: float32 [1536, 1536], P('shard')
- grad_moe_gain: float32 [1536], P('shard')
- grad_w_router: float32 [1536, 40], P('shard')
- grad_w_experts: float32 [1536, 40, 1536], P('shard', 'expert')
Inputs may be any that keep to these rules, and one draw needn't show every extreme that they name: `routes`: each token names 8 different experts. Among the 128 tokens of one device at most 38 name the same expert, and 38 is reached. Every expert is named by some token.
All inputs are finite; a program needn't handle non-finite values.
Results may differ from a plain program's by a relative error of at most 0.028.
Values may be sent and summed in bfloat16 or wider, within the bound.
A program may use at most 320 MiB of HBM per device.

v0:
```python
import jax
import jax.numpy as jnp
from jax import lax
from jax.sharding import PartitionSpec as P

MODEL_WIDTH = 1536
QUERY_HEADS = 24
KEY_VALUE_HEADS = 8
HEAD_SIZE = 64
FF = 512
E = 40
TOP = 8
DEVICE_TOKENS = 64
CAP = 38


EPSILON = 1e-06
ROPE_BASE = 10000.0
MASKED = -1e30


def angle_tables(positions):
    half_width = HEAD_SIZE // 2
    frequency = jnp.power(
        ROPE_BASE, -(jnp.arange(half_width, dtype=jnp.float32) * (2.0 / HEAD_SIZE))
    )
    angles = positions[:, None] * frequency[None, :]
    return (jnp.cos(angles), jnp.sin(angles))


def apply_rotation(values, cosine_table, sines_table):
    half_width = values.shape[-1] // 2
    first_half, second_half = (values[..., :half_width], values[..., half_width:])
    cosine_table, sines_table = (cosine_table[:, None, :], sines_table[:, None, :])
    return jnp.concatenate(
        [
            first_half * cosine_table - second_half * sines_table,
            second_half * cosine_table + first_half * sines_table,
        ],
        axis=-1,
    )


def reverse_rotation(values, cosine_table, sines_table):
    half_width = values.shape[-1] // 2
    first_half, second_half = (values[..., :half_width], values[..., half_width:])
    cosine_table, sines_table = (cosine_table[:, None, :], sines_table[:, None, :])
    return jnp.concatenate(
        [
            first_half * cosine_table + second_half * sines_table,
            second_half * cosine_table - first_half * sines_table,
        ],
        axis=-1,
    )


def local(
    inputs,
    cotangent,
    routes,
    attn_gain,
    w_query,
    key_matrix,
    value_matrix,
    w_output,
    moe_gain,
    w_router,
    w_experts,
):
    rows_local = inputs.shape[0]
    group_count = lax.axis_size("expert")
    experts_here = E // group_count
    group_width = QUERY_HEADS // KEY_VALUE_HEADS
    key_value_width = KEY_VALUE_HEADS * HEAD_SIZE
    scale_factor = 1.0 / HEAD_SIZE
    sequence_count = rows_local // DEVICE_TOKENS
    gain_one, query_full, key_complete, value_full, output_full, router_full, gain_two = (
        lax.all_gather(attn_gain, "shard", axis=0, tiled=True),
        lax.all_gather(w_query, "shard", axis=0, tiled=True),
        lax.all_gather(key_matrix, "shard", axis=0, tiled=True),
        lax.all_gather(value_matrix, "shard", axis=0, tiled=True),
        lax.all_gather(w_output, "shard", axis=0, tiled=True),
        lax.all_gather(w_router, "shard", axis=0, tiled=True),
        lax.all_gather(moe_gain, "shard", axis=0, tiled=True),
    )
    inputs_wide = inputs.astype(jnp.float32)
    r_one = lax.rsqrt(jnp.mean(inputs_wide * inputs_wide, axis=-1, keepdims=True) + EPSILON)
    z_one = inputs_wide * r_one
    normed_first = (z_one * gain_one.astype(jnp.float32)).astype(jnp.bfloat16)
    offset = lax.axis_index("shard") * DEVICE_TOKENS
    positions = offset + jnp.arange(DEVICE_TOKENS, dtype=jnp.int32)
    row_positions = jnp.tile(positions, sequence_count)
    cosine_table, sines_table = angle_tables(row_positions.astype(jnp.float32))
    query_rotated = apply_rotation(
        jnp.dot(normed_first, query_full, preferred_element_type=jnp.float32).reshape(
            rows_local, QUERY_HEADS, HEAD_SIZE
        ),
        cosine_table,
        sines_table,
    ).astype(jnp.bfloat16)
    keys_rot = apply_rotation(
        jnp.dot(normed_first, key_complete, preferred_element_type=jnp.float32).reshape(
            rows_local, KEY_VALUE_HEADS, HEAD_SIZE
        ),
        cosine_table,
        sines_table,
    ).astype(jnp.bfloat16)
    values_narrow = jnp.dot(normed_first, value_full, preferred_element_type=jnp.float32).astype(
        jnp.bfloat16
    )
    kv_local = jnp.concatenate(
        [keys_rot.reshape(rows_local, key_value_width), values_narrow], axis=1
    ).reshape(sequence_count, DEVICE_TOKENS, 2 * key_value_width)
    kv_all = lax.all_gather(kv_local, "shard", axis=1, tiled=True)
    seq_length = kv_all.shape[1]
    block_of_keys = min(512, seq_length)
    total_of_block = (offset + DEVICE_TOKENS + block_of_keys - 1) // block_of_keys
    query_four_dims = query_rotated.reshape(
        sequence_count, DEVICE_TOKENS, KEY_VALUE_HEADS, group_width, HEAD_SIZE
    )

    def scores_for(block_index):
        start_row = block_index * block_of_keys
        key_value_slice = lax.dynamic_slice_in_dim(kv_all, start_row, block_of_keys, 1)
        keys_block = key_value_slice[..., :key_value_width].reshape(
            sequence_count, block_of_keys, KEY_VALUE_HEADS, HEAD_SIZE
        )
        values_block = key_value_slice[..., key_value_width:].reshape(
            sequence_count, block_of_keys, KEY_VALUE_HEADS, HEAD_SIZE
        )
        scores = (
            jnp.einsum(
                "nqjgd,nkjd->njgqk", query_four_dims, keys_block, preferred_element_type=jnp.float32
            )
            * scale_factor
        )
        key_pos = start_row + jnp.arange(block_of_keys, dtype=jnp.int32)
        allowed = key_pos[None, :] <= positions[:, None]
        return (jnp.where(allowed, scores, MASKED), keys_block, values_block)

    def stats_step(block_index, loop_state):
        running_max, running_sum = loop_state
        scores = scores_for(block_index)[0]
        new_max = jnp.maximum(running_max, jnp.max(scores, axis=-1))
        running_sum = running_sum * jnp.exp(running_max - new_max) + jnp.sum(
            jnp.exp(scores - new_max[..., None]), axis=-1
        )
        return (new_max, running_sum)

    statistics_shape = (sequence_count, KEY_VALUE_HEADS, group_width, DEVICE_TOKENS)
    start_stats = (
        jnp.full(statistics_shape, MASKED, jnp.float32),
        jnp.zeros(statistics_shape, jnp.float32),
    )
    run_max, run_sum = lax.fori_loop(0, total_of_block, stats_step, start_stats)
    log_total = run_max + jnp.log(run_sum)

    def mixing_step(block_index, mixed_sum):
        scores, keys_block, values_block = scores_for(block_index)
        attn_probs = jnp.exp(scores - log_total[..., None]).astype(jnp.bfloat16)
        return mixed_sum + jnp.einsum(
            "njgqk,nkjd->nqjgd", attn_probs, values_block, preferred_element_type=jnp.float32
        )

    attention_mixed = lax.fori_loop(
        0,
        total_of_block,
        mixing_step,
        jnp.zeros(
            (sequence_count, DEVICE_TOKENS, KEY_VALUE_HEADS, group_width, HEAD_SIZE), jnp.float32
        ),
    )
    attention_mixed = attention_mixed.reshape(rows_local, QUERY_HEADS * HEAD_SIZE).astype(
        jnp.bfloat16
    )
    h_one = inputs_wide + jnp.dot(attention_mixed, output_full, preferred_element_type=jnp.float32)
    r_two = lax.rsqrt(jnp.mean(h_one * h_one, axis=-1, keepdims=True) + EPSILON)
    z_two = h_one * r_two
    n_two = (z_two * gain_two.astype(jnp.float32)).astype(jnp.bfloat16)
    logits = jnp.dot(n_two, router_full, preferred_element_type=jnp.float32)
    expert_ids = jnp.arange(E, dtype=jnp.int32)
    route_picks = (routes[:, :, None] == expert_ids[None, None, :]).astype(jnp.float32)
    chosen = jnp.sum(route_picks * logits[:, None, :], axis=-1)
    weights = jax.nn.softmax(chosen, axis=-1)
    flat_routes = routes.reshape(-1)
    route_hits = (flat_routes[:, None] == expert_ids[None, :]).astype(jnp.int32)
    route_ranks = jnp.sum(jnp.cumsum(route_hits, axis=0) * route_hits, axis=1) - 1
    targets = flat_routes * CAP + route_ranks
    token_of = jnp.arange(rows_local * TOP, dtype=jnp.int32) // TOP
    outgoing = jnp.zeros((E * CAP, MODEL_WIDTH), jnp.bfloat16).at[targets].set(n_two[token_of])
    arrived = lax.all_to_all(
        outgoing.reshape(group_count, experts_here, CAP, MODEL_WIDTH),
        "expert",
        split_axis=0,
        concat_axis=0,
        tiled=True,
    )
    expert_full = lax.all_gather(w_experts, "shard", axis=0, tiled=True)
    gate_and_up = expert_full[:, :, : 2 * FF]
    down_part = expert_full[:, :, 2 * FF :]
    both_parts = jnp.einsum(
        "sjcd,djf->sjcf", arrived, gate_and_up, preferred_element_type=jnp.float32
    )
    gate_part = both_parts[..., :FF]
    upper_part = both_parts[..., FF:]
    sigmoid_gate = jax.nn.sigmoid(gate_part)
    activated = (gate_part * sigmoid_gate * upper_part).astype(jnp.bfloat16)
    produced = jnp.einsum(
        "sjcf,djf->sjcd", activated, down_part, preferred_element_type=jnp.float32
    ).astype(jnp.bfloat16)
    returned = lax.all_to_all(produced, "expert", split_axis=0, concat_axis=0, tiled=True).reshape(
        E * CAP, MODEL_WIDTH
    )
    route_out = returned[targets].reshape(rows_local, TOP, MODEL_WIDTH).astype(jnp.float32)
    moe_sum = jnp.sum(weights[:, :, None] * route_out, axis=1)
    outputs = (h_one + moe_sum).astype(jnp.bfloat16)
    dy_wide = cotangent.astype(jnp.float32)
    d_routes = (
        (weights[:, :, None] * dy_wide[:, None, :])
        .astype(jnp.bfloat16)
        .reshape(rows_local * TOP, MODEL_WIDTH)
    )
    d_outgoing = jnp.zeros((E * CAP, MODEL_WIDTH), jnp.bfloat16).at[targets].set(d_routes)
    d_arrived = lax.all_to_all(
        d_outgoing.reshape(group_count, experts_here, CAP, MODEL_WIDTH),
        "expert",
        split_axis=0,
        concat_axis=0,
        tiled=True,
    )
    d_weights = jnp.sum(dy_wide[:, None, :] * route_out, axis=-1)
    d_chosen = weights * (d_weights - jnp.sum(weights * d_weights, axis=-1, keepdims=True))
    d_logits = jnp.sum(route_picks * d_chosen[:, :, None], axis=1).astype(jnp.bfloat16)
    grad_router = jnp.einsum("td,te->de", n_two, d_logits, preferred_element_type=jnp.float32)
    d_act = jnp.einsum("sjcd,djf->sjcf", d_arrived, down_part, preferred_element_type=jnp.float32)
    d_gate_up = jnp.concatenate(
        [
            d_act * upper_part * sigmoid_gate * (1.0 + gate_part * (1.0 - sigmoid_gate)),
            d_act * gate_part * sigmoid_gate,
        ],
        axis=-1,
    ).astype(jnp.bfloat16)
    d_rows = jnp.einsum(
        "sjcf,djf->sjcd", d_gate_up, gate_and_up, preferred_element_type=jnp.float32
    ).astype(jnp.bfloat16)
    d_returned = lax.all_to_all(d_rows, "expert", split_axis=0, concat_axis=0, tiled=True).reshape(
        E * CAP, MODEL_WIDTH
    )
    d_n_two = jnp.einsum(
        "te,de->td", d_logits, router_full, preferred_element_type=jnp.float32
    ) + jnp.sum(
        d_returned[targets].reshape(rows_local, TOP, MODEL_WIDTH).astype(jnp.float32), axis=1
    )
    first_part = jnp.einsum(
        "sjcd,sjcf->djf", arrived, d_gate_up, preferred_element_type=jnp.float32
    )
    second = jnp.einsum("sjcd,sjcf->djf", d_arrived, activated, preferred_element_type=jnp.float32)
    grad_experts = lax.psum_scatter(
        jnp.concatenate([first_part, second], axis=2).astype(jnp.bfloat16),
        "shard",
        scatter_dimension=0,
        tiled=True,
    ).astype(jnp.float32)
    grad_gain_two = jnp.sum(d_n_two * z_two, axis=0)
    dz_two = d_n_two * gain_two.astype(jnp.float32)
    dh_one = dy_wide + r_two * (dz_two - z_two * jnp.mean(dz_two * z_two, axis=-1, keepdims=True))
    dh_narrow = dh_one.astype(jnp.bfloat16)
    grad_output = jnp.einsum(
        "tk,td->kd", attention_mixed, dh_narrow, preferred_element_type=jnp.float32
    )
    mixed_gradient = jnp.einsum(
        "td,kd->tk", dh_narrow, output_full, preferred_element_type=jnp.float32
    ).astype(jnp.bfloat16)
    grad_four_dims = mixed_gradient.reshape(
        sequence_count, DEVICE_TOKENS, KEY_VALUE_HEADS, group_width, HEAD_SIZE
    )
    row_difference = jnp.sum(
        grad_four_dims.astype(jnp.float32)
        * attention_mixed.reshape(
            sequence_count, DEVICE_TOKENS, KEY_VALUE_HEADS, group_width, HEAD_SIZE
        ).astype(jnp.float32),
        axis=-1,
    )
    row_difference = jnp.transpose(row_difference, (0, 2, 3, 1))

    def grad_step(block_index, loop_state):
        d_query_sum, d_key_rows = loop_state
        scores, keys_block, values_block = scores_for(block_index)
        attn_probs = jnp.exp(scores - log_total[..., None])
        d_probs = jnp.einsum(
            "nqjgd,nkjd->njgqk", grad_four_dims, values_block, preferred_element_type=jnp.float32
        )
        d_scores = (attn_probs * (d_probs - row_difference[..., None])).astype(jnp.bfloat16)
        d_query_sum = (
            d_query_sum
            + jnp.einsum(
                "njgqk,nkjd->nqjgd", d_scores, keys_block, preferred_element_type=jnp.float32
            )
            * scale_factor
        )
        key_grad = (
            jnp.einsum(
                "njgqk,nqjgd->nkjd", d_scores, query_four_dims, preferred_element_type=jnp.float32
            )
            * scale_factor
        )
        value_grad = jnp.einsum(
            "njgqk,nqjgd->nkjd",
            attn_probs.astype(jnp.bfloat16),
            grad_four_dims,
            preferred_element_type=jnp.float32,
        )
        update = jnp.concatenate(
            [
                key_grad.reshape(sequence_count, block_of_keys, key_value_width),
                value_grad.reshape(sequence_count, block_of_keys, key_value_width),
            ],
            axis=2,
        )
        d_key_rows = lax.dynamic_update_slice_in_dim(
            d_key_rows, update, block_index * block_of_keys, 1
        )
        return (d_query_sum, d_key_rows)

    start_grads = (
        jnp.zeros(
            (sequence_count, DEVICE_TOKENS, KEY_VALUE_HEADS, group_width, HEAD_SIZE), jnp.float32
        ),
        jnp.zeros((sequence_count, seq_length, 2 * key_value_width), jnp.float32),
    )
    d_query_sum, d_key_rows = lax.fori_loop(0, total_of_block, grad_step, start_grads)
    owned_keys = (
        lax.psum_scatter(d_key_rows.astype(jnp.bfloat16), "shard", scatter_dimension=1, tiled=True)
        .astype(jnp.float32)
        .reshape(rows_local, 2 * key_value_width)
    )
    d_query = (
        reverse_rotation(
            d_query_sum.reshape(rows_local, QUERY_HEADS, HEAD_SIZE), cosine_table, sines_table
        )
        .reshape(rows_local, QUERY_HEADS * HEAD_SIZE)
        .astype(jnp.bfloat16)
    )
    key_gradient = (
        reverse_rotation(
            owned_keys[:, :key_value_width].reshape(rows_local, KEY_VALUE_HEADS, HEAD_SIZE),
            cosine_table,
            sines_table,
        )
        .reshape(rows_local, key_value_width)
        .astype(jnp.bfloat16)
    )
    value_gradient = owned_keys[:, key_value_width:].astype(jnp.bfloat16)
    grad_query = jnp.einsum("td,tk->dk", normed_first, d_query, preferred_element_type=jnp.float32)
    grad_key = jnp.einsum(
        "td,tk->dk", normed_first, key_gradient, preferred_element_type=jnp.float32
    )
    grad_value = jnp.einsum(
        "td,tk->dk", normed_first, value_gradient, preferred_element_type=jnp.float32
    )
    d_n_one = (
        jnp.einsum("tk,dk->td", d_query, query_full, preferred_element_type=jnp.float32)
        + jnp.einsum("tk,dk->td", key_gradient, key_complete, preferred_element_type=jnp.float32)
        + jnp.einsum("tk,dk->td", value_gradient, value_full, preferred_element_type=jnp.float32)
    )
    grad_gain_one = jnp.sum(d_n_one * z_one, axis=0)
    dz_one = d_n_one * gain_one.astype(jnp.float32)
    grad_inputs = dh_one + r_one * (
        dz_one - z_one * jnp.mean(dz_one * z_one, axis=-1, keepdims=True)
    )
    totals = (
        lax.psum_scatter(
            grad_gain_one.astype(jnp.bfloat16), "shard", scatter_dimension=0, tiled=True
        ).astype(jnp.float32),
        lax.psum_scatter(
            grad_query.astype(jnp.bfloat16), "shard", scatter_dimension=0, tiled=True
        ).astype(jnp.float32),
        lax.psum_scatter(
            grad_key.astype(jnp.bfloat16), "shard", scatter_dimension=0, tiled=True
        ).astype(jnp.float32),
        lax.psum_scatter(
            grad_value.astype(jnp.bfloat16), "shard", scatter_dimension=0, tiled=True
        ).astype(jnp.float32),
        lax.psum_scatter(
            grad_output.astype(jnp.bfloat16), "shard", scatter_dimension=0, tiled=True
        ).astype(jnp.float32),
        lax.psum_scatter(
            grad_router.astype(jnp.bfloat16), "shard", scatter_dimension=0, tiled=True
        ).astype(jnp.float32),
        lax.psum_scatter(
            grad_gain_two.astype(jnp.bfloat16), "shard", scatter_dimension=0, tiled=True
        ).astype(jnp.float32),
    )
    totals = (
        lax.psum(totals[0].astype(jnp.bfloat16), "expert").astype(jnp.float32),
        lax.psum(totals[1].astype(jnp.bfloat16), "expert").astype(jnp.float32),
        lax.psum(totals[2].astype(jnp.bfloat16), "expert").astype(jnp.float32),
        lax.psum(totals[3].astype(jnp.bfloat16), "expert").astype(jnp.float32),
        lax.psum(totals[4].astype(jnp.bfloat16), "expert").astype(jnp.float32),
        lax.psum(totals[5].astype(jnp.bfloat16), "expert").astype(jnp.float32),
        lax.psum(totals[6].astype(jnp.bfloat16), "expert").astype(jnp.float32),
    )
    return (
        outputs,
        grad_inputs,
        totals[0],
        totals[1],
        totals[2],
        totals[3],
        totals[4],
        totals[6],
        totals[5],
        grad_experts,
    )


def solution(mesh):
    return jax.shard_map(
        local,
        mesh=mesh,
        in_specs=(
            P(("expert", "shard"), None),
            P(("expert", "shard"), None),
            P(("expert", "shard"), None),
            P("shard"),
            P("shard", None),
            P("shard", None),
            P("shard", None),
            P("shard", None),
            P("shard"),
            P("shard", None),
            P("shard", "expert", None),
        ),
        out_specs=(
            P(("expert", "shard"), None),
            P(("expert", "shard"), None),
            P("shard"),
            P("shard", None),
            P("shard", None),
            P("shard", None),
            P("shard", None),
            P("shard"),
            P("shard", None),
            P("shard", "expert", None),
        ),
        check_vma=False,
    )
```

profile of v0, /device:TPU:10, one launch (start us, length us, event | category | flops | bytes accessed | tf_op | source)
XLA Modules:
  0.0 1622.2 jit_solution(8283196650302339188)
XLA Ops:
  12.5 13.5 all-reduce.5
  38.8 23.4 %all-gather.10.cloned.1.call-done = bf16[1536,512]{1,0:T(8,128)(2,1)} async-done(((bf16[192,512]{1,0:T(8,128)(2,1)}), bf16[1536,512]{1,0:T(8,128)(2,1)}) %all-gather.10.cloned.1.call-update) | async-done | bytes 1572880 | tf_op jit(solution)/shard_map/all_gather | solution.py:81
  67.2 11.3 reduce-window.6
  79.0 14.6 all-gather.12.cloned.1.call-done
  96.5 47.9 %all-gather.14.cloned.1.call-done = bf16[1536,1536]{1,0:T(8,128)(2,1)} async-done(((bf16[192,1536]{1,0:T(8,128)(2,1)}), bf16[1536,1536]{1,0:T(8,128)(2,1)}) %all-gather.14.cloned.1.call-update) | async-done | bytes 4718608 | tf_op jit(solution)/shard_map/all_gather | solution.py:79
  169.1 26.7 %all-gather.16.cloned.1.call-done = bf16[1536,1536]{1,0:T(8,128)(2,1)} async-done(((bf16[192,1536]{1,0:T(8,128)(2,1)}), bf16[1536,1536]{1,0:T(8,128)(2,1)}) %all-gather.16.cloned.1.call-update) | async-done | bytes 4718608 | tf_op jit(solution)/shard_map/all_gather | solution.py:82
  200.2 18.8 %scatter_custom_fusion = bf16[1520,1536]{1,0:T(8,128)(2,1)} fusion(s32[1024]{0:T(1024)S(1)} %bitcast.308, bf16[128,1536]{1,0:T(8,128)(2,1)S(1)} %multiply_convert_fusion.1, s32[1024]{0:T(1024)S(1)} %broadcast_clamp_fusion.1, bf16[]{:T(256)} %constant.110.clone.1), kind=kCustom, calls=%fused_computation.88 | custom fusion | bytes 4669442 | tf_op jit(solution)/shard_map/scatter | solution.py:190
  231.7 34.2 %all-gather = bf16[8,192,40]{1,2,0:T(8,128)(2,1)S(1)} all-gather(bf16[1,192,40]{1,2,0:T(8,128)(2,1)S(1)} %bitcast.307), channel_id=1, replica_groups=mesh['expert'=4,'shard'=8] {'shard'}, dimensions={0}, use_global_device_ids=true | all-gather | bytes 138240 | tf_op jit(solution)/shard_map/all_gather | solution.py:83
  268.0 8.7 scatter_custom_fusion.1
  292.9 304.9 %all-gather.18.cloned.1.call-done = bf16[1536,10,1536]{2,0,1:T(8,128)(2,1)} async-done(((bf16[192,10,1536]{2,0,1:T(8,128)(2,1)}), bf16[1536,10,1536]{2,0,1:T(8,128)(2,1)}) %all-gather.18.cloned.1.call-update) | async-done | bytes 47185936 | tf_op jit(solution)/shard_map/all_gather | solution.py:198
  597.9 17.0 %fusion.59 = f32[4,10,38,1024]{3,2,0,1:T(8,128)} fusion(bf16[1536,10,1536]{2,0,1:T(8,128)(2,1)} %all-gather.18.cloned.1.call-done, bf16[4,10,38,1536]{3,2,1,0:T(8,128)(2,1)} %all-to-all-done), kind=kOutput, calls=%fused_computation.94 | convolution fusion | flops 4781506560 | bytes 42598400 | tf_op jit(solution)/shard_map/sjcd,djf->sjcf/dot_general | solution.py:201
  614.9 12.6 fusion.50
  627.5 17.9 %convert_bitcast_fusion = bf16[4,10,38,1536]{3,2,0,1:T(8,128)(2,1)} fusion(bf16[1536,10,1536]{2,0,1:T(8,128)(2,1)} %all-gather.18.cloned.1.call-done, bf16[4,10,38,512]{3,2,0,1:T(8,128)(2,1)} %get-tuple-element.446, bf16[4,10,38,512]{3,2,0,1:T(8,128)(2,1)} %get-tuple-element.445), kind=kOutput, calls=%fused_computation.71 | convolution fusion | flops 4790067200 | bytes 39403520 | tf_op jit(solution)/shard_map/sjcf,djf->sjcd/dot_general | solution.py:243
  655.7 9.1 convert_bitcast_fusion.1
  667.5 43.5 %all-to-all-done.3 = bf16[4,10,38,1536]{3,2,1,0:T(8,128)(2,1)} async-done(((bf16[4,10,38,1536]{3,2,1,0:T(8,128)(2,1)}), bf16[4,10,38,1536]{3,2,1,0:T(8,128)(2,1)}, u32[]{:S(2)}, u32[]{:S(2)}) %all-to-all-start.3) | async-done | bytes 4669472 | tf_op jit(solution)/shard_map/all_to_all | solution.py:246
  724.7 10.2 gather_fusion.1
  739.7 31.2 %all-to-all-done.1 = bf16[4,10,38,1536]{3,2,1,0:T(8,128)(2,1)} async-done(((bf16[4,10,38,1536]{3,2,1,0:T(8,128)(2,1)}), bf16[4,10,38,1536]{3,2,1,0:T(8,128)(2,1)}, u32[]{:S(2)}, u32[]{:S(2)}) %all-to-all-start.1) | async-done | bytes 4669472 | tf_op jit(solution)/shard_map/all_to_all | solution.py:211
  777.6 10.2 gather_fusion
  814.0 9.3 while.39
  827.5 32.2 %reduce-scatter.12.cloned.1.call-done = bf16[2,64,1024]{2,1,0:T(8,128)(2,1)} async-done(((bf16[2,512,1024]{2,1,0:T(8,128)(2,1)}), bf16[2,64,1024]{2,1,0:T(8,128)(2,1)}) %reduce-scatter.12.cloned.1.call-update) | async-done | bytes 262160 | tf_op jit(solution)/shard_map/reduce_scatter | solution.py:333
  878.4 16.1 fusion.37
  895.6 10.4 fusion.40
  906.0 25.0 %reduce-scatter.18.cloned.1.call-done = bf16[192,512]{1,0:T(8,128)(2,1)} async-done(((bf16[1536,512]{1,0:T(8,128)(2,1)}), bf16[192,512]{1,0:T(8,128)(2,1)}) %reduce-scatter.18.cloned.1.call-update) | async-done | bytes 196624 | tf_op jit(solution)/shard_map/reduce_scatter | solution.py:381
  931.0 56.4 %reduce-scatter.20.cloned.1.call-done = bf16[192,1536]{1,0:T(8,128)(2,1)} async-done(((bf16[1536,1536]{1,0:T(8,128)(2,1)}), bf16[192,1536]{1,0:T(8,128)(2,1)}) %reduce-scatter.20.cloned.1.call-update) | async-done | bytes 589840 | tf_op jit(solution)/shard_map/reduce_scatter | solution.py:384
  987.4 56.2 %reduce-scatter.14.cloned.1.call-done = bf16[192,1536]{1,0:T(8,128)(2,1)} async-done(((bf16[1536,1536]{1,0:T(8,128)(2,1)}), bf16[192,1536]{1,0:T(8,128)(2,1)}) %reduce-scatter.14.cloned.1.call-update) | async-done | bytes 589840 | tf_op jit(solution)/shard_map/reduce_scatter | solution.py:375
  1043.7 33.0 %pad_maximum_fusion.1 = bf16[1536,10,1536]{0,2,1:T(8,128)(2,1)} fusion(bf16[1536,10,512]{0,2,1:T(8,128)(2,1)} %fusion.40, bf16[1536,10,1024]{0,2,1:T(8,128)(2,1)} %fusion.37), kind=kLoop, calls=%fused_computation.52 | loop fusion | flops 94371840 | bytes 94371840 | tf_op jit(solution)/shard_map/concatenate | solution.py:259
  1076.8 55.5 %copy.182 = bf16[1536,15360]{1,0:T(8,128)(2,1)} copy(bf16[1536,15360]{0,1:T(8,128)(2,1)} %bitcast.286) | data formatting | bytes 94371840
  1142.8 19.4 %all-reduce.4 = (bf16[1536]{0:T(1024)(128)(2,1)S(1)}, bf16[1536]{0:T(1024)(128)(2,1)S(1)}) all-reduce(bf16[1536]{0:T(1024)(128)(2,1)S(1)} %get-tuple-element.378, bf16[1536]{0:T(1024)(128)(2,1)S(1)} %copy-done.31), channel_id=3, replica_groups=mesh['expert'=4,'shard'=8] {'shard'}, use_global_device_ids=true, to_apply=%region_28.29.clone | all-reduce | flops 3072 | bytes 12288
  1162.3 14.4 all-reduce.6
  1187.6 407.1 %reduce-scatter.24.cloned.1.call-done = bf16[192,15360]{1,0:T(8,128)(2,1)} async-done(((bf16[1536,15360]{1,0:T(8,128)(2,1)}), bf16[192,15360]{1,0:T(8,128)(2,1)}) %reduce-scatter.24.cloned.1.call-update) | async-done | bytes 5898256
  1594.7 9.6 copy.183
  1604.3 10.9 copy.161
  (251 shorter events, 213.4 us)
Async XLA Ops:
  7.2 28.9 %all-gather.8.cloned.1.call-start = ((), (), s32[]{:S(2)}) async-start(), calls=%async_computation.11 | async-start | bytes 1769472 | tf_op jit(solution)/shard_map/all_gather | solution.py:80
  7.9 54.2 %all-gather.10.cloned.1.call-start = ((), (), s32[]{:S(2)}) async-start(), calls=%async_computation.12 | async-start | bytes 1769472 | tf_op jit(solution)/shard_map/all_gather | solution.py:81
  8.7 85.0 %all-gather.12.cloned.1.call-start = ((), (), s32[]{:S(2)}) async-start(), calls=%async_computation.13 | async-start | bytes 2359296 | tf_op jit(solution)/shard_map/all_gather | solution.py:114
  26.0 118.3 %copy-start.15 = (f32[1536]{0:T(1024)}, f32[1536]{0:T(1024)S(1)}, u32[]{:S(2)}) copy-start(f32[1536]{0:T(1024)S(1)} %convert_element_type.192) | copy-start | bytes 18436
  27.2 117.1 %copy-start.26 = (f32[128]{0:T(128)}, f32[128]{0:T(128)S(1)}, u32[]{:S(2)}) copy-start(f32[128]{0:T(128)S(1)} %add_rsqrt_fusion.1) | copy-start | bytes 1540
  27.4 121.3 %copy-start.19 = (f32[128,32]{0,1:T(8,128)}, f32[128,32]{0,1:T(8,128)S(1)}, u32[]{:S(2)}) copy-start(f32[128,32]{0,1:T(8,128)S(1)} %get-tuple-element.458) | copy-start | bytes 49156
  27.4 121.3 %copy-start.21 = (f32[128,32]{0,1:T(8,128)}, f32[128,32]{0,1:T(8,128)S(1)}, u32[]{:S(2)}) copy-start(f32[128,32]{0,1:T(8,128)S(1)} %get-tuple-element.459) | copy-start | bytes 49156
  64.9 79.5 %all-gather.14.cloned.1.call-start = ((), (), s32[]{:S(2)}) async-start(), calls=%async_computation.14 | async-start | bytes 5308416 | tf_op jit(solution)/shard_map/all_gather | solution.py:79
  65.5 130.4 %all-gather.16.cloned.1.call-start = ((), (), s32[]{:S(2)}) async-start(), calls=%async_computation.15 | async-start | bytes 5308416 | tf_op jit(solution)/shard_map/all_gather | solution.py:82
  66.0 78.3 %copy-start.3 = (bf16[128,1536]{1,0:T(8,128)(2,1)S(1)}, bf16[128,1536]{1,0:T(8,128)(2,1)}, u32[]{:S(2)}) copy-start(bf16[128,1536]{1,0:T(8,128)(2,1)} %param.17) | copy-start | bytes 1179652
  66.1 531.8 %all-gather.18.cloned.1.call-start = ((), (), s32[]{:S(2)}) async-start(), calls=%async_computation.16 | async-start | bytes 53084160 | tf_op jit(solution)/shard_map/all_gather | solution.py:198
  168.0 51.0 %copy-start.9 = (bf16[2,64,8,3,64]{1,0,4,3,2:T(2,128)(2,1)}, bf16[2,64,8,3,64]{1,0,4,3,2:T(2,128)(2,1)S(1)}, u32[]{:S(2)}) copy-start(bf16[2,64,8,3,64]{1,0,4,3,2:T(2,128)(2,1)S(1)} %copy.136) | copy-start | bytes 1179652
  225.8 40.3 %copy-start.14 = (bf16[128,1536]{1,0:T(8,128)(2,1)S(1)}, bf16[128,1536]{1,0:T(8,128)(2,1)}, u32[]{:S(2)}) copy-start(bf16[128,1536]{1,0:T(8,128)(2,1)} %param.18) | copy-start | bytes 1179652
  225.8 61.1 %all-to-all-start = ((bf16[4,10,38,1536]{3,2,1,0:T(8,128)(2,1)}), bf16[4,10,38,1536]{3,2,1,0:T(8,128)(2,1)}, u32[]{:S(2)}, u32[]{:S(2)}) async-start(bf16[4,10,38,1536]{3,2,1,0:T(8,128)(2,1)} %reshape.414), calls=%async_computation | async-start | bytes 9830400 | tf_op jit(solution)/shard_map/all_to_all | solution.py:191
  287.0 327.9 %all-to-all-start.2 = ((bf16[4,10,38,1536]{3,2,1,0:T(8,128)(2,1)}), bf16[4,10,38,1536]{3,2,1,0:T(8,128)(2,1)}, u32[]{:S(2)}, u32[]{:S(2)}) async-start(bf16[4,10,38,1536]{3,2,1,0:T(8,128)(2,1)} %reshape.416), calls=%async_computation.2 | async-start | bytes 9830400 | tf_op jit(solution)/shard_map/all_to_all | solution.py:224
  650.4 60.5 %all-to-all-start.3 = ((bf16[4,10,38,1536]{3,2,1,0:T(8,128)(2,1)}), bf16[4,10,38,1536]{3,2,1,0:T(8,128)(2,1)}, u32[]{:S(2)}, u32[]{:S(2)}) async-start(bf16[4,10,38,1536]{3,2,1,0:T(8,128)(2,1)} %copy.150), calls=%async_computation.3 | async-start | bytes 9830400 | tf_op jit(solution)/shard_map/all_to_all | solution.py:246
  711.0 60.0 %all-to-all-start.1 = ((bf16[4,10,38,1536]{3,2,1,0:T(8,128)(2,1)}), bf16[4,10,38,1536]{3,2,1,0:T(8,128)(2,1)}, u32[]{:S(2)}, u32[]{:S(2)}) async-start(bf16[4,10,38,1536]{3,2,1,0:T(8,128)(2,1)} %copy.145), calls=%async_computation.1 | async-start | bytes 9830400 | tf_op jit(solution)/shard_map/all_to_all | solution.py:211
  716.5 143.2 %reduce-scatter.12.cloned.1.call-start = ((), (), s32[]{:S(2)}) async-start(), calls=%async_computation.17 | async-start | bytes 2359296 | tf_op jit(solution)/shard_map/reduce_scatter | solution.py:333
  823.4 37.5 %copy-start.20 = (f32[128,32]{0,1:T(8,128)S(1)}, f32[128,32]{0,1:T(8,128)}, u32[]{:S(2)}) copy-start(f32[128,32]{0,1:T(8,128)} %copy-done.19) | copy-start | bytes 49156
  823.4 37.5 %copy-start.22 = (f32[128,32]{0,1:T(8,128)S(1)}, f32[128,32]{0,1:T(8,128)}, u32[]{:S(2)}) copy-start(f32[128,32]{0,1:T(8,128)} %copy-done.21) | copy-start | bytes 49156
  823.4 37.6 %copy-start.4 = (bf16[128,1536]{1,0:T(8,128)(2,1)S(1)}, bf16[128,1536]{1,0:T(8,128)(2,1)}, u32[]{:S(2)}) copy-start(bf16[128,1536]{1,0:T(8,128)(2,1)} %param.17) | copy-start | bytes 1179652
  823.4 37.6 %copy-start.16 = (f32[1536]{0:T(1024)S(1)}, f32[1536]{0:T(1024)}, u32[]{:S(2)}) copy-start(f32[1536]{0:T(1024)} %copy-done.15) | copy-start | bytes 18436
  823.4 37.6 %copy-start.27 = (f32[128]{0:T(128)S(1)}, f32[128]{0:T(128)}, u32[]{:S(2)}) copy-start(f32[128]{0:T(128)} %copy-done.26) | copy-start | bytes 1540
  827.5 37.3 %copy-start.7 = (f32[128,1536]{1,0:T(8,128)S(1)}, f32[128,1536]{1,0:T(8,128)}, u32[]{:S(2)}) copy-start(f32[128,1536]{1,0:T(8,128)} %copy-done.6) | copy-start | bytes 2359300
  827.5 37.3 %copy-start.11 = (bf16[128,1536]{0,1:T(8,128)(2,1)S(1)}, bf16[128,1536]{0,1:T(8,128)(2,1)}, u32[]{:S(2)}) copy-start(bf16[128,1536]{0,1:T(8,128)(2,1)} %convert_element_type.199) | copy-start | bytes 1179652
  827.5 78.5 %reduce-scatter.16.cloned.1.call-start = ((), (), s32[]{:S(2)}) async-start(), calls=%async_computation.19 | async-start | bytes 1769472 | tf_op jit(solution)/shard_map/reduce_scatter | solution.py:378
  862.8 68.2 %reduce-scatter.18.cloned.1.call-start = ((), (), s32[]{:S(2)}) async-start(), calls=%async_computation.20 | async-start | bytes 1769472 | tf_op jit(solution)/shard_map/reduce_scatter | solution.py:381
  864.8 122.7 %reduce-scatter.20.cloned.1.call-start = ((), (), s32[]{:S(2)}) async-start(), calls=%async_computation.21 | async-start | bytes 5308416 | tf_op jit(solution)/shard_map/reduce_scatter | solution.py:384
  868.4 175.3 %reduce-scatter.14.cloned.1.call-start = ((), (), s32[]{:S(2)}) async-start(), calls=%async_computation.18 | async-start | bytes 5308416 | tf_op jit(solution)/shard_map/reduce_scatter | solution.py:375
  878.1 259.8 %reduce-scatter.22.cloned.1.call-start = ((), (), s32[]{:S(2)}) async-start(), calls=%async_computation.22 | async-start | bytes 442368
  895.6 284.1 %all-reduce.10.cloned.1.call-start = ((), (), s32[]{:S(2)}) async-start(), calls=%async_computation.24 | async-start | bytes 3145728 | tf_op jit(solution)/shard_map/psum | solution.py:396
  1043.7 551.0 %reduce-scatter.24.cloned.1.call-start = ((), (), s32[]{:S(2)}) async-start(), calls=%async_computation.23 | async-start | bytes 53084160
  (19 other events, 214.5 us)
Sparse Core Ops, SparseCore 0:
  9.6 26.4 all-gather.7
  37.7 24.3 all-gather.9
  65.0 28.5 all-gather.11
  95.1 49.1 all-gather.13
  145.8 49.9 all-gather.15
  197.3 400.5 all-gather.17
  827.6 32.0 reduce-scatter.11
  862.9 33.1 reduce-scatter.15
  898.4 32.5 reduce-scatter.17
  933.2 54.1 reduce-scatter.19
  990.3 53.3 reduce-scatter.13
  1046.3 28.7 reduce-scatter.21
  1078.5 62.5 all-reduce.9
  1143.4 451.3 reduce-scatter.23
where the time goes:
time: 1640 us; the launch traced here: 1620 us
  waiting for transfers between devices  1080 us (66%)
  local copies, waits for them, and re-layouts  193 us (12%)
  matrix products  137 us (8%)
  other arithmetic  86.2 us (5%)
  blocking collectives  81.6 us (5%)
  starting transfers between devices  23.5 us (1%)
  between operations  16.5 us (1%)
    unnamed x16, waiting for transfers between devices  410 us
    all_gather x1, waiting for transfers between devices, local(): expert_full = lax.all_gather(w_experts, 'shard', axis=0, tiled=True)  305 us
    unnamed x80, local copies, waits for them, and re-layouts  94.3 us
    reduce_scatter x1, waiting for transfers between devices, local(): lax.psum_scatter(grad_output.astype(jnp.bfloat16), 'shard', scatter_dimen...  56.4 us
    reduce_scatter x1, waiting for transfers between devices, local(): lax.psum_scatter(grad_query.astype(jnp.bfloat16), 'shard', scatter_dimens...  56.2 us
    all_gather x1, waiting for transfers between devices, local(): lax.all_gather(w_query, 'shard', axis=0, tiled=True)  47.9 us
    all_to_all x1, waiting for transfers between devices, local(): lax.all_to_all(d_rows, 'expert', split_axis=0, concat_axis=0, tiled=True)  43.5 us
    all_gather x1, blocking collectives, local(): lax.all_gather(w_router, 'shard', axis=0, tiled=True)  34.2 us
  transfers between devices with their start and end apart: 18, of which 14 were waited for; matrix products, arithmetic and copies ran while one was open for 18% of the time, Pallas kernels for 0%

commit v1 on v0

--- a/solution.py
+++ b/solution.py
@@ -1,6 +1,10 @@
+import functools
+
 import jax
 import jax.numpy as jnp
 from jax import lax
+from jax.experimental import pallas as pl
+from jax.experimental.pallas import tpu as pltpu
 from jax.sharding import PartitionSpec as P
 
 MODEL_WIDTH = 1536
@@ -17,6 +21,7 @@
 EPSILON = 1e-06
 ROPE_BASE = 10000.0
 MASKED = -1e30
+LANES = 128
 
 
 def angle_tables(positions):
@@ -54,7 +59,7 @@
     )
 
 
-def local(
+def general(
     inputs,
     cotangent,
     routes,
@@ -414,9 +419,896 @@
     )
 
 
+def divides(shards, groups):
+    experts_here = E // groups
+    if groups != 4 or shards % 2 or shards < 4:
+        return False
+    if KEY_VALUE_HEADS % shards or shards > experts_here:
+        return False
+    extra = experts_here % shards
+    return extra == 0 or (shards % extra == 0 and FF % (shards // extra) == 0)
+
+
+def packed_experts(w_experts, shards):
+    rows, experts_here, _ = w_experts.shape
+    whole, extra = divmod(experts_here, shards)
+    parts = [w_experts[:, : whole * shards].reshape(rows, shards, whole * 3 * FF)]
+    if extra:
+        cuts = shards // extra
+        width = FF // cuts
+        cut = w_experts[:, whole * shards :].reshape(rows, extra, 3, cuts, width)
+        parts.append(jnp.transpose(cut, (0, 1, 3, 2, 4)).reshape(rows, shards, 3 * width))
+    return jnp.transpose(jnp.concatenate(parts, axis=2), (1, 0, 2))
+
+
+def unpacked_experts(blocks, experts_here):
+    shards, rows, _ = blocks.shape
+    whole, extra = divmod(experts_here, shards)
+    blocks = jnp.transpose(blocks, (1, 0, 2))
+    parts = [blocks[:, :, : whole * 3 * FF].reshape(rows, shards * whole, 3 * FF)]
+    if extra:
+        cuts = shards // extra
+        width = FF // cuts
+        cut = blocks[:, :, whole * 3 * FF :].reshape(rows, extra, cuts, 3, width)
+        parts.append(jnp.transpose(cut, (0, 1, 3, 2, 4)).reshape(rows, extra, 3 * FF))
+    return jnp.concatenate(parts, axis=1)
+
+
+def rotated(values, cosine, sine):
+    half = HEAD_SIZE // 2
+    first, second = values[..., :half], values[..., half:]
+    return jnp.concatenate([first * cosine - second * sine, second * cosine + first * sine], axis=-1)
+
+
+def alternating(depth):
+    order = []
+    low, high = 0, depth - 1
+    while low <= high:
+        order.append(high)
+        if low != high:
+            order.append(low)
+        low, high = low + 1, high - 1
+    return order
+
+
+def sent(source, target, send, receive, group, shard):
+    return pltpu.make_async_remote_copy(
+        src_ref=source,
+        dst_ref=target,
+        send_sem=send,
+        recv_sem=receive,
+        device_id=(group, shard),
+        device_id_type=pl.DeviceIdType.MESH,
+    )
+
+
+class Place:
+    def __init__(self, shards, groups):
+        self.group, self.shard = lax.axis_index("expert"), lax.axis_index("shard")
+        self.shards, self.groups = shards, groups
+        self.depth = shards // 2
+        self.spot, self.core = self.shard // 2, self.shard % 2
+        self.first = self.group + 1 - 2 * (self.group % 2)
+        self.second = (self.group + 2) % 4
+        self.corner = (self.first + 2) % 4
+        self.partner = self.shard + 1 - 2 * self.core
+
+    def greet(self, wide, whole_line):
+        barrier = pltpu.get_barrier_semaphore()
+
+        def signal(group, shard):
+            pl.semaphore_signal(
+                barrier, inc=1, device_id=(group, shard), device_id_type=pl.DeviceIdType.MESH
+            )
+
+        more = 2 if wide else 0
+        if wide:
+            signal(self.first, self.shard)
+            signal(self.second, self.shard)
+        if whole_line:
+            for i in range(1, self.shards):
+                signal(self.group, (self.shard + i) % self.shards)
+            pl.semaphore_wait(barrier, more + self.shards - 1)
+            return
+        signal(self.group, self.partner)
+        inside = (self.spot > 0) & (self.spot < self.depth - 1)
+
+        @pl.when(self.spot > 0)
+        def _():
+            signal(self.group, self.shard - 2)
+
+        @pl.when(self.spot < self.depth - 1)
+        def _():
+            signal(self.group, self.shard + 2)
+
+        @pl.when(inside)
+        def _():
+            pl.semaphore_wait(barrier, more + 3)
+
+        @pl.when(jnp.logical_not(inside))
+        def _():
+            pl.semaphore_wait(barrier, more + 2)
+
+
+class Exchange:
+    @staticmethod
+    def scratch(array):
+        n = array.shape[0]
+        dma = pltpu.SemaphoreType.DMA
+        return [pltpu.VMEM(array.shape[1:], array.dtype), dma((2,)), dma((n,)), dma((n,))]
+
+    def __init__(self, at, source, target, stage, own, out, come):
+        self.at, self.source, self.target = at, source, target
+        self.stage, self.own, self.out, self.come = stage, own, out, come
+
+    def copy(self, i):
+        at = self.at
+        to = (at.shard + i) % at.shards
+        return sent(
+            self.source.at[to],
+            self.target.at[at.shard],
+            self.out.at[i],
+            self.come.at[i],
+            at.group,
+            to,
+        )
+
+    def keep(self, i):
+        here = self.at.shard
+        if i == 0:
+            return pltpu.make_async_copy(self.source.at[here], self.stage, self.own.at[0])
+        return pltpu.make_async_copy(self.stage, self.target.at[here], self.own.at[1])
+
+    def start(self):
+        self.keep(0).start()
+        for i in range(self.at.shards - 1, 0, -1):
+            self.copy(i).start()
+        self.keep(0).wait()
+        self.keep(1).start()
+
+    def finish(self):
+        self.keep(1).wait()
+        for i in range(1, self.at.shards):
+            self.copy(i).wait()
+
+
+class Gather:
+    @staticmethod
+    def scratch(array, wide, shards):
+        steps = shards // 2 - 1
+        marks = 1 + 2 * steps
+        dma = pltpu.SemaphoreType.DMA
+        turns = 2 if wide else 1
+        return [
+            dma((1,)),
+            dma((2 * steps,)),
+            dma((2 * steps,)),
+            dma((turns, marks)),
+            dma((turns, marks)),
+            dma((turns, marks)),
+            dma((turns, marks)),
+            dma((5 if wide else 1, marks)),
+            dma((5 if wide else 1, marks)),
+        ]
+
+    def __init__(self, at, wide, block, out, *sems):
+        self.at, self.wide, self.block, self.out = at, wide, block, out
+        self.own, self.z_out, self.z_in, self.p_out, self.p_in = sems[:5]
+        self.h_out, self.h_in, self.c_out, self.c_in = sems[5:]
+        self.steps = at.depth - 1
+        self.events = [(0, 0)]
+        for t in range(self.steps):
+            self.events += [(1, t), (2, t)]
+
+    def when(self, event, body):
+        kind, t = event
+        if kind == 0:
+            body()
+        elif kind == 1:
+            pl.when(self.at.spot - 1 - t >= 0)(body)
+        else:
+            pl.when(self.at.spot + 1 + t < self.at.depth)(body)
+
+    def origin(self, event):
+        kind, t = event
+        return self.at.shard + (0, -2 * (t + 1), 2 * (t + 1))[kind]
+
+    def slot(self, group, shard):
+        index = group * self.at.shards + shard if self.wide else shard
+        return self.out.at[:, index]
+
+    def half(self, ref, which):
+        rows = ref.shape[1]
+        cut = rows // 32 * 16
+        return ref.at[:, pl.ds(0, cut)] if which == 0 else ref.at[:, pl.ds(cut, rows - cut)]
+
+    def line(self, step, direction, shard):
+        at = self.at
+        k = direction * self.steps + step
+        ref = self.slot(at.group, shard)
+        source = self.block if step == 0 else ref
+        to = at.shard + (2, -2)[direction]
+        return sent(source, ref, self.z_out.at[k], self.z_in.at[k], at.group, to)
+
+    def side(self, k, which):
+        at, event = self.at, self.events[k]
+        ref = self.slot(at.group, self.origin(event))
+        source = self.block if event[0] == 0 else ref
+        group = (at.first, at.second)[which]
+        return sent(source, ref, self.p_out.at[which, k], self.p_in.at[which, k], group, at.shard)
+
+    def turn(self, k, which):
+        at = self.at
+        shard = self.origin(self.events[k])
+        held = self.half(self.slot((at.first, at.second)[which], shard), which)
+        group = (at.second, at.first)[which]
+        return sent(held, held, self.h_out.at[which, k], self.h_in.at[which, k], group, at.shard)
+
+    def across(self, k, kind):
+        at, event = self.at, self.events[k]
+        shard = self.origin(event)
+        if kind < 3:
+            ref = self.slot((at.group, at.first, at.second)[kind], shard)
+        else:
+            ref = self.half(self.slot(at.corner, shard), kind - 3)
+        source = self.block if kind == 0 and event[0] == 0 else ref
+        return sent(
+            source, ref, self.c_out.at[kind, k], self.c_in.at[kind, k], at.group, at.partner
+        )
+
+    def keep(self):
+        here = self.slot(self.at.group, self.at.shard)
+        return pltpu.make_async_copy(self.block, here, self.own.at[0])
+
+    def onward(self, event, act):
+        kind, t = event
+        for direction in range(2):
+            if kind and direction != kind - 1:
+                continue
+            step = 0 if kind == 0 else t + 1
+            if step >= self.steps:
+                continue
+            ahead = self.at.spot < self.at.depth - 1 if direction == 0 else self.at.spot > 0
+            pl.when(ahead)(
+                lambda step=step, direction=direction: act(
+                    self.line(step, direction, self.origin(event))
+                )
+            )
+
+    def lines(self, k):
+        event = self.events[k]
+
+        def body():
+            kind, t = event
+            if kind:
+                self.line(t, kind - 1, self.origin(event)).wait_recv()
+            self.onward(event, lambda copy: copy.start())
+            if self.wide:
+                self.side(k, 0).start()
+                self.side(k, 1).start()
+            self.across(k, 0).start()
+            if kind == 0:
+                self.keep().start()
+
+        self.when(event, body)
+
+    def sides(self, k):
+        def body():
+            for which in range(2):
+                self.side(k, which).wait_recv()
+                self.turn(k, which).start()
+                self.across(k, 1 + which).start()
+
+        if self.wide:
+            self.when(self.events[k], body)
+
+    def turns(self, k):
+        def body():
+            for which in range(2):
+                self.turn(k, which).wait_recv()
+                self.across(k, 3 + which).start()
+
+        if self.wide:
+            self.when(self.events[k], body)
+
+    def finish(self, k):
+        event = self.events[k]
+
+        def body():
+            if event[0] == 0:
+                self.keep().wait()
+            self.onward(event, lambda copy: copy.wait_send())
+            for kind in range(5 if self.wide else 1):
+                copy = self.across(k, kind)
+                copy.wait_send()
+                copy.wait_recv()
+            if self.wide:
+                for which in range(2):
+                    self.side(k, which).wait_send()
+                    self.turn(k, which).wait_send()
+
+        self.when(event, body)
+
+
+class Reduce:
+    @staticmethod
+    def scratch(parts, wide, shards):
+        depth = shards // 2
+        block = (parts.shape[0],) + parts.shape[2:]
+        kinds = 4 if wide else 1
+        dma = pltpu.SemaphoreType.DMA
+        out = [
+            pltpu.VMEM((kinds, depth) + block, parts.dtype),
+            pltpu.VMEM((kinds, depth) + block, parts.dtype),
+            pltpu.VMEM((2, depth) + block, parts.dtype),
+            dma((kinds, depth)),
+            dma((kinds, depth)),
+            dma((kinds, depth)),
+            dma((2, depth)),
+            dma((2, depth)),
+        ]
+        if wide:
+            cut = block[1] // 32 * 16
+            out += [
+                pltpu.VMEM((depth, block[0], cut, block[2]), parts.dtype),
+                pltpu.VMEM((depth, block[0], block[1] - cut, block[2]), parts.dtype),
+                pltpu.VMEM((2, depth) + block, parts.dtype),
+                dma((2, depth)),
+                dma((2, depth)),
+                dma((2, depth)),
+                dma((2, depth)),
+            ]
+        return out
+
+    def __init__(self, at, wide, parts, total, *scratch):
+        self.at, self.wide, self.parts, self.total = at, wide, parts, total
+        self.mine, self.accs, self.z_buf, self.own = scratch[:4]
+        self.c_out, self.c_in, self.z_out, self.z_in = scratch[4:8]
+        if wide:
+            self.h_buf, self.p_buf = scratch[8:10], scratch[10]
+            self.h_out, self.h_in, self.p_out, self.p_in = scratch[11:]
+        self.order = alternating(at.depth)
+        self.kinds = (3, 1, 2, 0) if wide else (0,)
+        self.columns = (at.group, at.first, at.second, at.corner)
+
+    def place(self, kind, q, core):
+        shard = 2 * q + core
+        return self.columns[kind] * self.at.shards + shard if self.wide else shard
+
+    def load(self, kind, q):
+        return pltpu.make_async_copy(
+            self.parts.at[:, self.place(kind, q, self.at.core)],
+            self.mine.at[kind, q],
+            self.own.at[kind, q],
+        )
+
+    def across(self, kind, q):
+        return sent(
+            self.parts.at[:, self.place(kind, q, 1 - self.at.core)],
+            self.accs.at[kind, q],
+            self.c_out.at[kind, q],
+            self.c_in.at[kind, q],
+            self.at.group,
+            self.at.partner,
+        )
+
+    def span(self, which):
+        rows = self.accs.shape[3]
+        cut = rows // 32 * 16
+        return pl.ds(0, cut) if which == 0 else pl.ds(cut, rows - cut)
+
+    def turn(self, q, which):
+        return sent(
+            self.accs.at[3, q, :, self.span(which)],
+            self.h_buf[which].at[q],
+            self.h_out.at[which, q],
+            self.h_in.at[which, q],
+            (self.at.first, self.at.second)[which],
+            self.at.shard,
+        )
+
+    def side(self, q, which):
+        return sent(
+            self.accs.at[1 + which, q],
+            self.p_buf.at[which, q],
+            self.p_out.at[which, q],
+            self.p_in.at[which, q],
+            (self.at.first, self.at.second)[which],
+            self.at.shard,
+        )
+
+    def line(self, q, direction):
+        return sent(
+            self.accs.at[0, q],
+            self.z_buf.at[direction, q],
+            self.z_out.at[direction, q],
+            self.z_in.at[direction, q],
+            self.at.group,
+            self.at.shard + (2, -2)[direction],
+        )
+
+    def add(self, kind, q, *others):
+        value = self.accs[kind, q].astype(jnp.float32)
+        for other in others:
+            value = value + other.astype(jnp.float32)
+        self.accs[kind, q] = value.astype(self.accs.dtype)
+
+    def pair(self, kind, q):
+        self.load(kind, q).wait()
+        self.across(kind, q).wait_recv()
+        self.add(kind, q, self.mine[kind, q])
+
+    def begin(self):
+        for kind in self.kinds:
+            for q in self.order:
+                self.load(kind, q).start()
+                self.across(kind, q).start()
+
+    def corners(self):
+        for q in self.order:
+            self.pair(3, q)
+            self.turn(q, 0).start()
+            self.turn(q, 1).start()
+
+    def sides(self):
+        for q in self.order:
+            for which in range(2):
+                kind = 2 - which
+                self.pair(kind, q)
+                self.turn(q, which).wait_recv()
+                span = self.span(which)
+                value = self.accs[kind, q, :, span].astype(jnp.float32)
+                value = value + self.h_buf[which][q].astype(jnp.float32)
+                self.accs[kind, q, :, span] = value.astype(self.accs.dtype)
+                self.side(q, kind - 1).start()
+
+    def lines(self):
+        at = self.at
+        for q in self.order:
+            self.pair(0, q)
+            if self.wide:
+                self.side(q, 0).wait_recv()
+                self.side(q, 1).wait_recv()
+                self.add(0, q, self.p_buf[0, q], self.p_buf[1, q])
+            for direction in range(2):
+
+                @pl.when(q > at.spot if direction == 0 else q < at.spot)
+                def _(q=q, direction=direction):
+                    @pl.when(at.spot > 0 if direction == 0 else at.spot < at.depth - 1)
+                    def _():
+                        self.line(q, direction).wait_recv()
+                        self.add(0, q, self.z_buf[direction, q])
+
+                    self.line(q, direction).start()
+
+    def finish(self):
+        at, total = self.at, self.total
+        for q in range(at.depth):
+
+            @pl.when(q == at.spot)
+            def _(q=q):
+                total[...] = self.accs[0, q].astype(jnp.float32)
+                for direction in range(2):
+                    if q > 0 if direction == 0 else q < at.depth - 1:
+                        self.line(q, direction).wait_recv()
+                        total[...] = total[...] + self.z_buf[direction, q].astype(jnp.float32)
+
+            for kind in self.kinds:
+                self.across(kind, q).wait_send()
+            if self.wide:
+                for which in range(2):
+                    self.turn(q, which).wait_send()
+                    self.side(q, which).wait_send()
+            for direction in range(2):
+
+                @pl.when(q > at.spot if direction == 0 else q < at.spot)
+                def _(q=q, direction=direction):
+                    self.line(q, direction).wait_send()
+
+
+def cut_refs(refs, sizes):
+    out, start = [], 0
+    for size in sizes:
+        out.append(refs[start : start + size])
+        start += size
+    return out
+
+
+def gather_body(shards, groups, wides, swaps, sizes, *refs):
+    count = len(wides) + swaps
+    ins, outs = refs[:count], refs[count : 2 * count]
+    scratch = cut_refs(refs[2 * count :], sizes)
+    at = Place(shards, groups)
+    at.greet(any(wides), swaps > 0)
+    gathers = [Gather(at, wide, ins[i], outs[i], *scratch[i]) for i, wide in enumerate(wides)]
+    moves = [Exchange(at, ins[i], outs[i], *scratch[i]) for i in range(len(wides), count)]
+    marks = range(len(gathers[0].events))
+    for k in marks:
+        for g in gathers:
+            g.lines(k)
+    for m in moves:
+        m.start()
+    for step in (Gather.sides, Gather.turns, Gather.finish):
+        for k in marks:
+            for g in gathers:
+                step(g, k)
+    for m in moves:
+        m.finish()
+
+
+def gathered(arrays, wides, shards, groups, identity, swapped=()):
+    shapes = [
+        jax.ShapeDtypeStruct(
+            (a.shape[0], shards * (groups if wide else 1)) + a.shape[1:], a.dtype
+        )
+        for a, wide in zip(arrays, wides)
+    ] + [jax.ShapeDtypeStruct(a.shape, a.dtype) for a in swapped]
+    moved = sum(s.size * s.dtype.itemsize for s in shapes)
+    scratch = [Gather.scratch(a, wide, shards) for a, wide in zip(arrays, wides)]
+    scratch += [Exchange.scratch(a) for a in swapped]
+    return pl.pallas_call(
+        functools.partial(
+            gather_body,
+            shards,
+            groups,
+            tuple(wides),
+            len(swapped),
+            tuple(len(s) for s in scratch),
+        ),
+        out_shape=shapes,
+        in_specs=[pl.BlockSpec(memory_space=pltpu.VMEM)] * len(arrays)
+        + [pl.BlockSpec(memory_space=pl.ANY)] * len(swapped),
+        out_specs=[pl.BlockSpec(memory_space=pl.ANY)] * len(shapes),
+        scratch_shapes=[s for some in scratch for s in some],
+        compiler_params=pltpu.CompilerParams(collective_id=identity, has_side_effects=True),
+        cost_estimate=pl.CostEstimate(flops=0, bytes_accessed=20 * moved, transcendentals=0),
+    )(*arrays, *swapped)
+
+
+def reduce_body(shards, groups, wides, swaps, sizes, *refs):
+    count = len(wides) + swaps
+    ins, outs = refs[:count], refs[count : 2 * count]
+    scratch = cut_refs(refs[2 * count :], sizes)
+    at = Place(shards, groups)
+    at.greet(any(wides), swaps > 0)
+    sums = [Reduce(at, wide, ins[i], outs[i], *scratch[i]) for i, wide in enumerate(wides)]
+    moves = [Exchange(at, ins[i], outs[i], *scratch[i]) for i in range(len(wides), count)]
+    for r in sums:
+        r.begin()
+    for m in moves:
+        m.start()
+    for r in sums:
+        if r.wide:
+            r.corners()
+    for r in sums:
+        if not r.wide:
+            r.lines()
+    for r in sums:
+        if r.wide:
+            r.sides()
+            r.lines()
+    for r in sums:
+        r.finish()
+    for m in moves:
+        m.finish()
+
+
+def reduced(arrays, wides, shards, groups, identity, swapped=()):
+    shapes = [
+        jax.ShapeDtypeStruct((a.shape[0],) + a.shape[2:], jnp.float32) for a in arrays
+    ] + [jax.ShapeDtypeStruct(a.shape, a.dtype) for a in swapped]
+    moved = sum(a.size * a.dtype.itemsize for a in (*arrays, *swapped))
+    scratch = [Reduce.scratch(a, wide, shards) for a, wide in zip(arrays, wides)]
+    scratch += [Exchange.scratch(a) for a in swapped]
+    return pl.pallas_call(
+        functools.partial(
+            reduce_body,
+            shards,
+            groups,
+            tuple(wides),
+            len(swapped),
+            tuple(len(s) for s in scratch),
+        ),
+        out_shape=shapes,
+        in_specs=[pl.BlockSpec(memory_space=pl.ANY)] * (len(arrays) + len(swapped)),
+        out_specs=[pl.BlockSpec(memory_space=pltpu.VMEM)] * len(arrays)
+        + [pl.BlockSpec(memory_space=pl.ANY)] * len(swapped),
+        scratch_shapes=[s for some in scratch for s in some],
+        compiler_params=pltpu.CompilerParams(
+            collective_id=identity, has_side_effects=True, vmem_limit_bytes=60 * 1024 * 1024
+        ),
+        cost_estimate=pl.CostEstimate(flops=0, bytes_accessed=20 * moved, transcendentals=0),
+    )(*arrays, *swapped)
+
+
+def local(
+    inputs,
+    cotangent,
+    routes,
+    attn_gain,
+    w_query,
+    key_matrix,
+    value_matrix,
+    w_output,
+    moe_gain,
+    w_router,
+    w_experts,
+):
+    f32, bf16 = jnp.float32, jnp.bfloat16
+    both = ("expert", "shard")
+    shards, groups = lax.axis_size("shard"), lax.axis_size("expert")
+    shard, group = lax.axis_index("shard"), lax.axis_index("expert")
+    tokens = inputs.shape[0]
+    own_rows = attn_gain.shape[0]
+    sequences = tokens // DEVICE_TOKENS
+    length = shards * DEVICE_TOKENS
+    experts_here = E // groups
+    heads = KEY_VALUE_HEADS // shards
+    ratio = QUERY_HEADS // KEY_VALUE_HEADS
+    query_width, key_width = heads * ratio * HEAD_SIZE, heads * HEAD_SIZE
+    scale = 1.0 / HEAD_SIZE
+
+    small = jnp.concatenate([w_router, attn_gain[:, None], moe_gain[:, None]], axis=1)
+    small = jnp.pad(small, ((0, 0), (0, LANES - E - 2)))
+    qkv_cut = jnp.transpose(
+        jnp.concatenate(
+            [
+                w_query.reshape(own_rows, shards, query_width),
+                key_matrix.reshape(own_rows, shards, key_width),
+                value_matrix.reshape(own_rows, shards, key_width),
+            ],
+            axis=2,
+        ),
+        (1, 0, 2),
+    )
+    group_inputs, small_all, routes_all, c_all, qkv_own = gathered(
+        [
+            inputs.reshape(sequences, DEVICE_TOKENS, MODEL_WIDTH),
+            small[None],
+            jnp.transpose(routes)[None],
+            cotangent[None],
+        ],
+        (False, False, True, True),
+        shards,
+        groups,
+        0,
+        [qkv_cut],
+    )
+    qkv_own = qkv_own.reshape(MODEL_WIDTH, query_width + 2 * key_width)
+    r_all = jnp.transpose(routes_all[0], (0, 2, 1))
+    c_all = c_all[0]
+    small = small_all.reshape(MODEL_WIDTH, LANES)
+    router, gain_one, gain_two = small[:, :E], small[:, E].astype(f32), small[:, E + 1].astype(f32)
+
+    group_wide = group_inputs.reshape(sequences * length, MODEL_WIDTH).astype(f32)
+    r_group = lax.rsqrt(jnp.mean(group_wide * group_wide, axis=-1, keepdims=True) + EPSILON)
+    z_group = group_wide * r_group
+    normed = (z_group * gain_one).astype(bf16)
+    qkv = jnp.dot(normed, qkv_own, preferred_element_type=f32)
+    cosine, sine = angle_tables(jnp.arange(length, dtype=f32))
+    q_shape = (sequences, length, heads, ratio, HEAD_SIZE)
+    k_shape = (sequences, length, heads, HEAD_SIZE)
+    query = rotated(
+        qkv[:, :query_width].reshape(q_shape),
+        cosine[:, None, None, :],
+        sine[:, None, None, :],
+    ).astype(bf16)
+    keys = rotated(
+        qkv[:, query_width : query_width + key_width].reshape(k_shape),
+        cosine[:, None, :],
+        sine[:, None, :],
+    ).astype(bf16)
+    values = qkv[:, query_width + key_width :].reshape(k_shape).astype(bf16)
+    places = jnp.arange(length, dtype=jnp.int32)
+    allowed = places[None, :] <= places[:, None]
+    scores = jnp.einsum("nqjgd,nkjd->njgqk", query, keys, preferred_element_type=f32) * scale
+    scores = jnp.where(allowed, scores, MASKED)
+    top = jnp.max(scores, axis=-1, keepdims=True)
+    log_total = top + jnp.log(jnp.sum(jnp.exp(scores - top), axis=-1, keepdims=True))
+    probs = jnp.exp(scores - log_total)
+    mixed = jnp.einsum(
+        "njgqk,nkjd->nqjgd", probs.astype(bf16), values, preferred_element_type=f32
+    ).astype(bf16)
+    mixed_rows = mixed.reshape(sequences * length, query_width)
+    projected = jnp.dot(mixed_rows, w_output, preferred_element_type=f32).astype(bf16)
+    line_shape = (sequences, shards, DEVICE_TOKENS, MODEL_WIDTH)
+    attended = reduced([projected.reshape(line_shape)], (False,), shards, groups, 1)[0]
+    attended = attended.reshape(tokens, MODEL_WIDTH)
+    inputs_wide = inputs.astype(f32)
+    h_one = inputs_wide + attended
+    r_two = lax.rsqrt(jnp.mean(h_one * h_one, axis=-1, keepdims=True) + EPSILON)
+    z_two = h_one * r_two
+    n_two = (z_two * gain_two).astype(bf16)
+
+    blocks = groups * shards
+    n_all, experts_own = gathered(
+        [n_two[None]], (True,), shards, groups, 2, [packed_experts(w_experts, shards)]
+    )
+    n_all = n_all[0]
+    experts_own = experts_own.reshape(MODEL_WIDTH, -1)
+
+    def weights_of(rows, picks_of):
+        logits = jnp.einsum("...d,de->...e", rows, router, preferred_element_type=f32)
+        picks = (picks_of[..., None] == jnp.arange(E, dtype=jnp.int32)).astype(f32)
+        chosen = jnp.sum(picks * logits[..., None, :], axis=-1)
+        return jax.nn.softmax(chosen, axis=-1), picks
+
+    w_all, _ = weights_of(n_all, r_all)
+    whole, extra = divmod(experts_here, shards)
+    owned = [(group * experts_here + shard * whole + i, i * 3 * FF, FF) for i in range(whole)]
+    if extra:
+        cuts = shards // extra
+        owned.append(
+            (group * experts_here + whole * shards + shard // cuts, whole * 3 * FF, FF // cuts)
+        )
+    slots = -(-CAP // 8) * 8
+    lower = (jnp.arange(tokens)[:, None] <= jnp.arange(tokens)[None, :]).astype(bf16)
+    picked, slot_weights = [], []
+    for expert, _, _ in owned:
+        hit = jnp.any(r_all == expert, axis=-1)
+        rank = jnp.einsum("bt,tu->bu", hit.astype(bf16), lower, preferred_element_type=f32)
+        place = jnp.where(hit, rank.astype(jnp.int32) - 1, -1)
+        pick = place[:, None, :] == jnp.arange(slots, dtype=jnp.int32)[None, :, None]
+        weight = jnp.sum(jnp.where(r_all == expert, w_all, 0.0), axis=-1)
+        picked.append(pick)
+        slot_weights.append(jnp.sum(jnp.where(pick, weight[:, None, :], 0.0), axis=-1))
+    selection = jnp.concatenate(picked, axis=1).astype(bf16)
+    n_sent = jnp.einsum("bct,btd->bcd", selection, n_all, preferred_element_type=f32).astype(bf16)
+    c_sent = jnp.einsum("bct,btd->bcd", selection, c_all, preferred_element_type=f32).astype(bf16)
+    produced, d_rows, grads = [], [], []
+    d_weights = jnp.zeros((blocks, tokens, TOP), f32)
+    for i, (expert, start, width) in enumerate(owned):
+        a = n_sent[:, i * slots : (i + 1) * slots].reshape(blocks * slots, MODEL_WIDTH)
+        c = c_sent[:, i * slots : (i + 1) * slots].reshape(blocks * slots, MODEL_WIDTH)
+        gate_up = experts_own[:, start : start + 2 * width]
+        down = experts_own[:, start + 2 * width : start + 3 * width]
+        both_parts = jnp.dot(a, gate_up, preferred_element_type=f32)
+        d_plain = jnp.dot(c, down, preferred_element_type=f32)
+        gate, up = both_parts[:, :width], both_parts[:, width:]
+        sig = jax.nn.sigmoid(gate)
+        act = gate * sig * up
+        w = slot_weights[i].reshape(-1, 1)
+        d_slot = jnp.sum(act * d_plain, axis=-1).reshape(blocks, slots)
+        d_token = jnp.sum(jnp.where(picked[i], d_slot[:, :, None], 0.0), axis=1)
+        d_weights = d_weights + jnp.where(r_all == expert, d_token[:, :, None], 0.0)
+        act_w = (act * w).astype(bf16)
+        da = d_plain * w
+        d_gu = jnp.concatenate(
+            [da * up * sig * (1.0 + gate * (1.0 - sig)), da * gate * sig], axis=1
+        ).astype(bf16)
+        produced.append(
+            jnp.einsum("rf,df->rd", act_w, down, preferred_element_type=f32)
+            .astype(bf16)
+            .reshape(blocks, slots, MODEL_WIDTH)
+        )
+        d_rows.append(
+            jnp.einsum("rf,df->rd", d_gu, gate_up, preferred_element_type=f32)
+            .astype(bf16)
+            .reshape(blocks, slots, MODEL_WIDTH)
+        )
+        grads.append(jnp.einsum("rd,rf->df", a, d_gu, preferred_element_type=f32))
+        grads.append(jnp.einsum("rd,rf->df", c, act_w, preferred_element_type=f32))
+    d_sums = jnp.einsum(
+        "bct,bcd->btd", selection, jnp.concatenate(d_rows, axis=1), preferred_element_type=f32
+    ).astype(bf16)
+    high = d_weights.astype(bf16)
+    low = (d_weights - high.astype(f32)).astype(bf16)
+    pad_rows = 16
+    carried = jnp.stack([high, low], axis=1).reshape(blocks, 2, tokens * TOP)
+    carried = jnp.pad(carried, ((0, 0), (0, pad_rows - 2), (0, MODEL_WIDTH - tokens * TOP)))
+    grads = jnp.concatenate(grads, axis=1).astype(bf16).reshape(shards, own_rows, -1)
+    back, grads = reduced(
+        [jnp.concatenate([d_sums, carried], axis=1)[None]], (True,), shards, groups, 3, [grads]
+    )
+    back = back[0]
+    grad_experts = unpacked_experts(grads, experts_here).astype(f32)
+    o_sums = jnp.einsum(
+        "bct,bcd->btd", selection, jnp.concatenate(produced, axis=1), preferred_element_type=f32
+    ).astype(bf16)
+
+    weights, picks = weights_of(n_two, routes)
+    carried_back = back[tokens : tokens + 2, : tokens * TOP]
+    d_weights = (carried_back[0] + carried_back[1]).reshape(tokens, TOP)
+    d_chosen = weights * (d_weights - jnp.sum(weights * d_weights, axis=-1, keepdims=True))
+    d_logits = jnp.sum(picks * d_chosen[:, :, None], axis=1).astype(bf16)
+    grad_router = jnp.einsum("td,te->de", n_two, d_logits, preferred_element_type=f32)
+    d_n_two = jnp.einsum("te,de->td", d_logits, router, preferred_element_type=f32) + back[
+        :tokens
+    ]
+    grad_gain_two = jnp.sum(d_n_two * z_two, axis=0)
+    dz_two = d_n_two * gain_two
+    dh_one = cotangent.astype(f32) + r_two * (
+        dz_two - z_two * jnp.mean(dz_two * z_two, axis=-1, keepdims=True)
+    )
+
+    dh_group = gathered(
+        [dh_one.astype(bf16).reshape(sequences, DEVICE_TOKENS, MODEL_WIDTH)],
+        (False,),
+        shards,
+        groups,
+        4,
+    )[0].reshape(sequences * length, MODEL_WIDTH)
+    grad_output = jnp.einsum("tk,td->kd", mixed_rows, dh_group, preferred_element_type=f32)
+    d_mixed = (
+        jnp.einsum("td,kd->tk", dh_group, w_output, preferred_element_type=f32)
+        .astype(bf16)
+        .reshape(q_shape)
+    )
+    delta = jnp.sum(d_mixed.astype(f32) * mixed.astype(f32), axis=-1)
+    delta = jnp.transpose(delta, (0, 2, 3, 1))[..., None]
+    d_probs = jnp.einsum("nqjgd,nkjd->njgqk", d_mixed, values, preferred_element_type=f32)
+    d_scores = (probs * (d_probs - delta)).astype(bf16)
+    d_query = jnp.einsum("njgqk,nkjd->nqjgd", d_scores, keys, preferred_element_type=f32) * scale
+    d_keys = jnp.einsum("njgqk,nqjgd->nkjd", d_scores, query, preferred_element_type=f32) * scale
+    d_values = jnp.einsum(
+        "njgqk,nqjgd->nkjd", probs.astype(bf16), d_mixed, preferred_element_type=f32
+    )
+    d_qkv = jnp.concatenate(
+        [
+            rotated(d_query, cosine[:, None, None, :], -sine[:, None, None, :])
+            .astype(bf16)
+            .reshape(sequences * length, query_width),
+            rotated(d_keys, cosine[:, None, :], -sine[:, None, :])
+            .astype(bf16)
+            .reshape(sequences * length, key_width),
+            d_values.astype(bf16).reshape(sequences * length, key_width),
+        ],
+        axis=1,
+    )
+    d_normed = jnp.einsum("tk,dk->td", d_qkv, qkv_own, preferred_element_type=f32)
+    grad_gain_one = jnp.sum(d_normed * z_group, axis=0)
+    grad_qkv = jnp.einsum("td,tk->dk", normed, d_qkv, preferred_element_type=f32)
+    grad_small = jnp.concatenate(
+        [grad_router, grad_gain_one[:, None], grad_gain_two[:, None]], axis=1
+    ).astype(bf16)
+    grad_small = jnp.pad(grad_small, ((0, 0), (0, LANES - E - 2)))
+    d_n_one, grad_small, moe_sum, grad_qkv = reduced(
+        [
+            d_normed.astype(bf16).reshape(line_shape),
+            grad_small.reshape(1, shards, own_rows, LANES),
+            o_sums[None],
+        ],
+        (False, False, True),
+        shards,
+        groups,
+        5,
+        [grad_qkv.astype(bf16).reshape(shards, own_rows, -1)],
+    )
+    d_n_one = d_n_one.reshape(tokens, MODEL_WIDTH)
+    outputs = (h_one + moe_sum[0]).astype(bf16)
+    grad_qkv, grad_output, grad_small = lax.psum(
+        (grad_qkv, grad_output.astype(bf16), grad_small[0].astype(bf16)), "expert"
+    )
+    grad_small = grad_small.astype(f32)
+
+    def columns(start, width):
+        part = jnp.transpose(grad_qkv[:, :, start : start + width], (1, 0, 2))
+        return part.reshape(own_rows, shards * width).astype(f32)
+
+    r_one = lax.rsqrt(jnp.mean(inputs_wide * inputs_wide, axis=-1, keepdims=True) + EPSILON)
+    z_one = inputs_wide * r_one
+    dz_one = d_n_one * gain_one
+    grad_inputs = dh_one + r_one * (
+        dz_one - z_one * jnp.mean(dz_one * z_one, axis=-1, keepdims=True)
+    )
+    return (
+        outputs,
+        grad_inputs,
+        grad_small[:, E],
+        columns(0, query_width),
+        columns(query_width, key_width),
+        columns(query_width + key_width, key_width),
+        grad_output.astype(f32),
+        grad_small[:, E + 1],
+        grad_small[:, :E],
+        grad_experts,
+    )
+
+
 def solution(mesh):
+    fits = divides(mesh.shape["shard"], mesh.shape["expert"])
     return jax.shard_map(
-        local,
+        local if fits else general,
         mesh=mesh,
         in_specs=(
             P(("expert", "shard"), None),

time: 1640 us -> 963 us (0.59)
  waiting for transfers between devices: 1080 us -> 13.1 us
  Pallas kernels: 0 us -> 616 us
  local copies, waits for them, and re-layouts: 193 us -> 94.1 us
  blocking collectives: 81.6 us -> 16 us
  starting transfers between devices: 23.5 us -> 0.04 us
  other arithmetic: 86.2 us -> 68.8 us
    pallas_call x0 -> x6, Pallas kernels: none -> 616 us  [the longest x3 341 us: reduced(): pl.pallas_call(functools.partial(reduce_body, shards, groups, tuple(wides...]
    all_gather x6 -> x0, waiting for transfers between devices: 426 us -> none  [the longest x1 305 us: local(): expert_full = lax.all_gather(w_experts, 'shard', axis=0, tiled=True)]
    unnamed x16 -> x1, waiting for transfers between devices: 410 us -> 0.02 us
    reduce_scatter x5 -> x0, waiting for transfers between devices: 170 us -> none  [the longest x1 56.4 us: local(): lax.psum_scatter(grad_output.astype(jnp.bfloat16), 'shard', scatter_dimen...]
    unnamed x80 -> x177, local copies, waits for them, and re-layouts: 94.3 us -> 5.81 us
    all_to_all x4 -> x0, waiting for transfers between devices: 78.3 us -> none  [the longest x1 43.5 us: local(): lax.all_to_all(d_rows, 'expert', split_axis=0, concat_axis=0, tiled=True)]
    all_gather x1 -> x0, blocking collectives: 34.2 us -> none  [local(): lax.all_gather(w_router, 'shard', axis=0, tiled=True)]
    unnamed x2 -> x0, blocking collectives: 32.9 us -> none
  transfers between devices with their start and end apart: 18 -> 1, of which waited for: 14 -> 1; matrix products, arithmetic and copies ran while one was open for 18% -> 4% of each run, Pallas kernels for 0% -> 0%
where the time goes in v1:
time: 963 us; the launch traced here: 956 us
  Pallas kernels  616 us (64%)
  matrix products  132 us (14%)
  local copies, waits for them, and re-layouts  94.1 us (10%)
  other arithmetic  68.8 us (7%)
  blocking collectives  16 us (2%)
  between operations  15.7 us (2%)
  waiting for transfers between devices  13.1 us (1%)
    pallas_call x3, Pallas kernels, reduced(): pl.pallas_call(functools.partial(reduce_body, shards, groups, tuple(wides...  341 us
    pallas_call x3, Pallas kernels, gathered(): pl.pallas_call(functools.partial(gather_body, shards, groups, tuple(wides...  275 us
  transfers between devices with their start and end apart: 1, of which 1 were waited for; matrix products, arithmetic and copies ran while one was open for 4% of the time, Pallas kernels for 0%

profile of v1, /device:TPU:10, one launch (start us, length us, event | category | flops | bytes accessed | tf_op | source)
XLA Modules:
  0.0 955.7 jit_solution(11656676338505602083)
XLA Ops:
  7.4 4.9 slice.135
  16.3 92.0 %shard_map.186 = (bf16[2,8,64,1536]{3,2,1,0:T(8,128)(2,1)}, bf16[1,8,192,128]{3,2,1,0:T(8,128)(2,1)}, s32[1,32,8,128]{3,2,1,0:T(8,128)}, bf16[1,32,128,1536]{3,2,1,0:T(8,128)(2,1)}, bf16[8,192,320]{2,1,0:T(8,128)(2,1)}) custom-call(bf16[2,64,1536]{2,1,0:T(8,128)(2,1)} %bitcast.296, bf16[1,192,128]{2,1,0:T(8,128)(2,1)} %fusion.97.refs_1_, ...), custom_call_target="tpu_custom_call" | custom-call | bytes 344719360 | tf_op jit(solution)/shard_map/pallas_call | solution.py:949
  129.1 50.6 %shard_map.187 = f32[2,64,1536]{2,1,0:T(8,128)} custom-call(bf16[2,8,64,1536]{3,2,1,0:T(8,128)(2,1)} %bitcast.281), custom_call_target="tpu_custom_call" | custom-call | bytes 62914560 | tf_op jit(solution)/shard_map/pallas_call | solution.py:1003
  195.5 5.6 maximum_bitcast_fusion.1.refs_1_
  201.1 151.5 %shard_map.188 = (bf16[1,32,128,1536]{3,2,1,0:T(8,128)(2,1)}, bf16[8,192,1920]{2,1,0:T(8,128)(2,1)}) custom-call(bf16[1,128,1536]{2,1,0:T(8,128)(2,1)} %fusion.153.refs_0_, bf16[8,192,1920]{2,1,0:T(8,128)(2,1)} %maximum_bitcast_fusion.1.refs_1_), custom_call_target="tpu_custom_call" | custom-call | bytes 369623040 | tf_op jit(solution)/shard_map/pallas_call | solution.py:949
  352.6 7.8 fusion.4
  361.3 5.3 fusion.20
  366.6 6.9 fusion.17
  376.9 6.3 copy.141
  383.1 6.3 copy.137
  390.4 5.1 fusion.118
  415.5 6.3 copy.139
  428.4 6.6 copy.135
  435.1 8.0 fusion.31
  443.1 8.0 multiply_reduce_fusion.2
  451.7 4.7 multiply_convert_fusion.4
  456.4 5.8 convolution_convert_fusion.4
  465.8 5.8 convolution_convert_fusion.2
  471.6 6.7 fusion.37
  479.8 8.6 convolution_convert_fusion.1
  488.4 13.0 %maximum_bitcast_fusion.refs_0_ = bf16[1,32,144,1536]{3,2,1,0:T(8,128)(2,1)} fusion(bf16[32,16,1536]{2,1,0:T(8,128)(2,1)S(1)} %fusion.40, bf16[32,128,1536]{2,1,0:T(8,128)(2,1)} %convolution_convert_fusion.1), kind=kLoop, calls=%fused_computation.2 | loop fusion | flops 28311552 | bytes 28311552 | tf_op jit(solution)/shard_map/broadcast_in_dim | solution.py:1201
  504.4 184.5 %shard_map.189 = (f32[1,144,1536]{2,1,0:T(8,128)}, bf16[8,192,1920]{2,1,0:T(8,128)(2,1)}) custom-call(bf16[1,32,144,1536]{3,2,1,0:T(8,128)(2,1)} %maximum_bitcast_fusion.refs_0_, bf16[8,192,1920]{2,1,0:T(8,128)(2,1)} %pad_maximum_fusion.refs_1_), custom_call_target="tpu_custom_call" | custom-call | bytes 401080320 | tf_op jit(solution)/shard_map/pallas_call | solution.py:1003
  694.8 31.5 %shard_map.190 = bf16[2,8,64,1536]{3,2,1,0:T(8,128)(2,1)} custom-call(bf16[2,64,1536]{2,1,0:T(8,128)(2,1)} %bitcast.318), custom_call_target="tpu_custom_call" | custom-call | bytes 62914560 | tf_op jit(solution)/shard_map/pallas_call | solution.py:949
  733.8 4.6 fusion.53
  738.7 4.9 fusion.26
  747.6 5.0 multiply_reduce_fusion
  759.5 8.5 fusion.8.refs_2_
  768.8 105.7 %shard_map.191 = (f32[2,64,1536]{2,1,0:T(8,128)}, f32[1,192,128]{2,1,0:T(8,128)}, f32[1,128,1536]{2,1,0:T(8,128)}, bf16[8,192,320]{2,1,0:T(8,128)(2,1)}) custom-call(bf16[2,8,64,1536]{3,2,1,0:T(8,128)(2,1)} %bitcast.312, bf16[1,8,192,128]{3,2,1,0:T(8,128)(2,1)} %bitcast.319, bf16[1,32,128,1536]{3,2,1,0:T(8,128)(2,1)} %fusion.8.refs_2_, ...), custom_call_target="tpu_custom_call" | custom-call | bytes 342097920 | tf_op jit(solution)/shard_map/pallas_call | solution.py:1003
  877.0 5.0 slice.198
  882.0 16.0 %psum.21 = bf16[192,128]{1,0:T(8,128)(2,1)S(1)} all-reduce(bf16[192,128]{1,0:T(8,128)(2,1)S(1)} %convert_bitcast_fusion.3), channel_id=1, replica_groups=mesh['expert'=4,'shard'=8] {'expert'}, use_global_device_ids=true, to_apply=%region_28.29 | all-reduce | flops 24576 | bytes 98304 | tf_op jit(solution)/shard_map/psum | solution.py:1279
  917.2 7.6 maximum_convert_fusion
  924.8 13.1 %all-reduce.6.cloned.1.call-done = (bf16[8,192,320]{2,1,0:T(8,128)(2,1)}, bf16[192,1536]{1,0:T(8,128)(2,1)}) async-done(((bf16[8,192,320]{2,1,0:T(8,128)(2,1)}, bf16[192,1536]{1,0:T(8,128)(2,1)}), (bf16[8,192,320]{2,1,0:T(8,128)(2,1)}, bf16[192,1536]{1,0:T(8,128)(2,1)})) %all-reduce.6.cloned.1.call-update) | async-done | bytes 1572880 | tf_op jit(solution)/shard_map/psum | solution.py:1279
  (307 shorter events, 138.0 us)
Async XLA Ops:
  7.2 119.1 %copy-start = (bf16[192,1536]{1,0:T(8,128)(2,1)S(1)}, bf16[192,1536]{1,0:T(8,128)(2,1)}, u32[]{:S(2)}) copy-start(bf16[192,1536]{1,0:T(8,128)(2,1)} %param.18) | copy-start | bytes 1769476
  7.2 930.7 %all-reduce.6.cloned.1.call-start = ((), (), s32[]{:S(2)}) async-start(), calls=%async_computation | async-start | bytes 3538944 | tf_op jit(solution)/shard_map/psum | solution.py:1279
  7.3 116.6 %copy-start.31 = (pred[512,512]{0,1:T(8,128)(4,1)}, pred[512,512]{0,1:T(8,128)(4,1)S(1)}, u32[]{:S(2)}) copy-start(pred[512,512]{0,1:T(8,128)(4,1)S(1)} %iota_compare_fusion.3) | copy-start | bytes 786436
  126.2 53.5 %copy-start.9 = (bf16[128,1536]{1,0:T(8,128)(2,1)S(1)}, bf16[128,1536]{1,0:T(8,128)(2,1)}, u32[]{:S(2)}) copy-start(bf16[128,1536]{1,0:T(8,128)(2,1)} %param.11) | copy-start | bytes 1179652
  129.1 54.3 %slice-start = ((bf16[192,10,1536]{2,0,1:T(8,128)(2,1)}), bf16[192,2,1536]{2,0,1:T(8,128)(2,1)S(1)}, s32[]{:S(2)}) async-start(bf16[192,10,1536]{2,0,1:T(8,128)(2,1)} %param.21), calls=%async_computation.1 | async-start | bytes 2359296 | tf_op jit(solution)/shard_map/slice | solution.py:439
  181.6 10.3 %copy-start.64 = (f32[128]{0:T(128)}, f32[128]{0:T(128)S(1)}, u32[]{:S(2)}) copy-start(f32[128]{0:T(128)S(1)} %get-tuple-element.131) | copy-start | bytes 1540
  184.5 8.8 copy-start.42
  201.1 151.5 %copy-start.7 = (bf16[1,8,192,128]{3,2,1,0:T(8,128)(2,1)S(1)}, bf16[1,8,192,128]{3,2,1,0:T(8,128)(2,1)}, u32[]{:S(2)}) copy-start(bf16[1,8,192,128]{3,2,1,0:T(8,128)(2,1)} %get-tuple-element.24) | copy-start | bytes 1179652
  352.6 7.8 copy-start.59
  352.6 7.8 copy-start.61
  352.6 8.6 copy-start.1
  383.1 6.6 copy-start.62
  399.2 6.6 copy-start.54
  435.0 8.0 copy-start.2
  443.0 8.0 copy-start.13
  443.1 8.1 copy-start.60
  451.7 14.1 %slice-start.1 = ((s8[5898240]{0:T(1024)(128)(4,1)}), s8[4194304]{0:T(1024)(128)(4,1)S(1)}, s32[]{:S(2)}) async-start(s8[5898240]{0:T(1024)(128)(4,1)} %bitcast.339), calls=%async_computation.2 | async-start | bytes 8388608
  456.4 9.4 slice-start.2
  471.6 6.8 copy-start.55
  471.6 8.2 copy-start.23
  488.4 13.0 %copy-start.22 = (bf16[8,192,1024]{2,1,0:T(8,128)(2,1)S(1)}, bf16[8,192,1024]{2,1,0:T(8,128)(2,1)}, u32[]{:S(2)}) copy-start(bf16[8,192,1024]{2,1,0:T(8,128)(2,1)} %fusion.37) | copy-start | bytes 9437188
  488.4 13.0 %copy-start.28 = (bf16[8,192,512]{2,1,0:T(8,128)(2,1)S(1)}, bf16[8,192,512]{2,1,0:T(8,128)(2,1)}, u32[]{:S(2)}) copy-start(bf16[8,192,512]{2,1,0:T(8,128)(2,1)} %convolution_convert_fusion.10) | copy-start | bytes 4718596
  488.4 13.0 %copy-start.33 = (bf16[8,192,256]{2,1,0:T(8,128)(2,1)S(1)}, bf16[8,192,256]{2,1,0:T(8,128)(2,1)}, u32[]{:S(2)}) copy-start(bf16[8,192,256]{2,1,0:T(8,128)(2,1)} %convolution_convert_fusion.11) | copy-start | bytes 2359300
  488.4 13.0 %copy-start.43 = (bf16[8,192,128]{2,1,0:T(8,128)(2,1)S(1)}, bf16[8,192,128]{2,1,0:T(8,128)(2,1)}, u32[]{:S(2)}) copy-start(bf16[8,192,128]{2,1,0:T(8,128)(2,1)} %convolution_convert_fusion.13) | copy-start | bytes 1179652
  504.4 185.5 %copy-start.70 = (f32[128]{0:T(128)S(1)}, f32[128]{0:T(128)}, u32[]{:S(2)}) copy-start(f32[128]{0:T(128)} %copy-done.69) | copy-start | bytes 1540
  504.4 185.5 %copy-start.72 = (f32[128]{0:T(128)S(1)}, f32[128]{0:T(128)}, u32[]{:S(2)}) copy-start(f32[128]{0:T(128)} %fusion.103) | copy-start | bytes 1540
  504.4 185.6 %copy-start.65 = (f32[128]{0:T(128)S(1)}, f32[128]{0:T(128)}, u32[]{:S(2)}) copy-start(f32[128]{0:T(128)} %copy-done.64) | copy-start | bytes 1540
  690.0 36.4 %copy-start.12 = (bf16[24,8,2,512]{3,1,2,0:T(8,128)(2,1)S(1)}, bf16[24,8,2,512]{3,1,2,0:T(8,128)(2,1)}, u32[]{:S(2)}) copy-start(bf16[24,8,2,512]{3,1,2,0:T(8,128)(2,1)} %copy-done.11) | copy-start | bytes 1179652
  901.0 11.1 %copy-start.10 = (bf16[128,1536]{1,0:T(8,128)(2,1)S(1)}, bf16[128,1536]{1,0:T(8,128)(2,1)}, u32[]{:S(2)}) copy-start(bf16[128,1536]{1,0:T(8,128)(2,1)} %param.11) | copy-start | bytes 1179652
  901.0 11.1 %copy-start.71 = (f32[128]{0:T(128)S(1)}, f32[128]{0:T(128)}, u32[]{:S(2)}) copy-start(f32[128]{0:T(128)} %get-tuple-element.130) | copy-start | bytes 1540
  905.2 9.3 copy-start.20
  905.2 9.3 copy-start.66
  (50 other events, 200.4 us)
Sparse Core Ops, SparseCore 0:
  874.7 63.1 all-reduce.5

commit v2 on v1

--- a/solution.py
+++ b/solution.py
@@ -429,31 +429,6 @@
     return extra == 0 or (shards % extra == 0 and FF % (shards // extra) == 0)
 
 
-def packed_experts(w_experts, shards):
-    rows, experts_here, _ = w_experts.shape
-    whole, extra = divmod(experts_here, shards)
-    parts = [w_experts[:, : whole * shards].reshape(rows, shards, whole * 3 * FF)]
-    if extra:
-        cuts = shards // extra
-        width = FF // cuts
-        cut = w_experts[:, whole * shards :].reshape(rows, extra, 3, cuts, width)
-        parts.append(jnp.transpose(cut, (0, 1, 3, 2, 4)).reshape(rows, shards, 3 * width))
-    return jnp.transpose(jnp.concatenate(parts, axis=2), (1, 0, 2))
-
-
-def unpacked_experts(blocks, experts_here):
-    shards, rows, _ = blocks.shape
-    whole, extra = divmod(experts_here, shards)
-    blocks = jnp.transpose(blocks, (1, 0, 2))
-    parts = [blocks[:, :, : whole * 3 * FF].reshape(rows, shards * whole, 3 * FF)]
-    if extra:
-        cuts = shards // extra
-        width = FF // cuts
-        cut = blocks[:, :, whole * 3 * FF :].reshape(rows, extra, cuts, 3, width)
-        parts.append(jnp.transpose(cut, (0, 1, 3, 2, 4)).reshape(rows, extra, 3 * FF))
-    return jnp.concatenate(parts, axis=1)
-
-
 def rotated(values, cosine, sine):
     half = HEAD_SIZE // 2
     first, second = values[..., :half], values[..., half:]
@@ -493,7 +468,7 @@
         self.corner = (self.first + 2) % 4
         self.partner = self.shard + 1 - 2 * self.core
 
-    def greet(self, wide, whole_line):
+    def greet(self, wide, whole_line, corner=False):
         barrier = pltpu.get_barrier_semaphore()
 
         def signal(group, shard):
@@ -501,10 +476,12 @@
                 barrier, inc=1, device_id=(group, shard), device_id_type=pl.DeviceIdType.MESH
             )
 
-        more = 2 if wide else 0
+        more = (2 if wide else 0) + (1 if corner else 0)
         if wide:
             signal(self.first, self.shard)
             signal(self.second, self.shard)
+        if corner:
+            signal(self.corner, self.shard)
         if whole_line:
             for i in range(1, self.shards):
                 signal(self.group, (self.shard + i) % self.shards)
@@ -532,44 +509,186 @@
 
 class Exchange:
     @staticmethod
-    def scratch(array):
-        n = array.shape[0]
+    def scratch(block, dtype, pieces, n):
         dma = pltpu.SemaphoreType.DMA
-        return [pltpu.VMEM(array.shape[1:], array.dtype), dma((2,)), dma((n,)), dma((n,))]
-
-    def __init__(self, at, source, target, stage, own, out, come):
+        return [pltpu.VMEM(block, dtype), dma((2, pieces)), dma((n, pieces)), dma((n, pieces))]
+
+    def __init__(self, at, plan, source, target, stage, own, out, come):
         self.at, self.source, self.target = at, source, target
         self.stage, self.own, self.out, self.come = stage, own, out, come
-
-    def copy(self, i):
+        self.take, self.give, self.parts = plan.take, plan.give, plan.parts
+
+    def copies(self, i):
         at = self.at
         to = (at.shard + i) % at.shards
+        for k, (taken, given) in enumerate(zip(self.take(to), self.give(at.shard))):
+            yield sent(
+                self.source.at[taken],
+                self.target.at[given],
+                self.out.at[i, k],
+                self.come.at[i, k],
+                at.group,
+                to,
+            )
+
+    def keep(self, way):
+        here = self.at.shard
+        for k, (taken, given) in enumerate(zip(self.take(here), self.give(here))):
+            held = self.stage.at[self.parts[k]]
+            if way == 0:
+                yield pltpu.make_async_copy(self.source.at[taken], held, self.own.at[0, k])
+            else:
+                yield pltpu.make_async_copy(held, self.target.at[given], self.own.at[1, k])
+
+    def start(self):
+        for copy in self.keep(0):
+            copy.start()
+        for i in range(self.at.shards - 1, 0, -1):
+            for copy in self.copies(i):
+                copy.start()
+        for copy in self.keep(0):
+            copy.wait()
+        for copy in self.keep(1):
+            copy.start()
+
+    def wait(self):
+        for copy in self.keep(1):
+            copy.wait()
+        for i in range(1, self.at.shards):
+            for copy in self.copies(i):
+                copy.wait()
+
+
+class Rows:
+    def __init__(self, array):
+        self.shape, self.block, self.count = array.shape, array.shape[1:], 1
+        self.parts = [...]
+
+    def take(self, i):
+        return [i]
+
+    def give(self, me):
+        return [me]
+
+
+class Experts:
+    def __init__(self, array, shards, experts_here, back, thirds=(0, 3)):
+        self.shards, self.back, self.first = shards, back, thirds[0]
+        self.thirds = thirds[1] - thirds[0]
+        self.whole, self.extra = divmod(experts_here, shards)
+        self.cuts = shards // self.extra if self.extra else 1
+        self.width = FF // self.cuts
+        rows = array.shape[1]
+        held = 3 * (FF * self.whole + (self.width if self.extra else 0))
+        moved = held * self.thirds // 3
+        self.shape = (experts_here, rows, self.thirds * FF) if back else (shards, rows, held)
+        self.block = (rows, moved)
+        self.parts = [(slice(None), cut) for cut in self.inside(0, self.thirds)]
+        self.count = len(self.parts)
+
+    def inside(self, first, thirds):
+        cuts = [
+            pl.ds((i * thirds + first) * FF, self.thirds * FF) for i in range(self.whole)
+        ]
+        if self.extra:
+            start = self.whole * thirds * FF
+            cuts += [
+                pl.ds(start + (first + k) * self.width, self.width) for k in range(self.thirds)
+            ]
+        return cuts
+
+    def owner(self, i):
+        return [(i, slice(None), cut) for cut in self.inside(self.first, 3)]
+
+    def outside(self, i):
+        first = 0 if self.back else self.first
+        cuts = [
+            (i * self.whole + k, slice(None), pl.ds(first * FF, self.thirds * FF))
+            for k in range(self.whole)
+        ]
+        if self.extra:
+            expert = self.whole * self.shards + i // self.cuts
+            for k in range(self.thirds):
+                start = pl.multiple_of((first + k) * FF + i % self.cuts * self.width, 128)
+                cuts.append((expert, slice(None), pl.ds(start, self.width)))
+        return cuts
+
+    def take(self, i):
+        return self.owner(i) if self.back else self.outside(i)
+
+    def give(self, me):
+        return self.outside(me) if self.back else self.owner(me)
+
+
+class Across:
+    @staticmethod
+    def scratch(shape, dtype):
+        block = (shape[0] // 4,) + shape[1:]
+        dma = pltpu.SemaphoreType.DMA
+        return [pltpu.VMEM((4,) + block, dtype), pltpu.VMEM(block, dtype)] + [
+            dma((4,)) for _ in range(4)
+        ]
+
+    def __init__(self, at, source, target, held, mine, r_out, r_in, g_out, g_in):
+        self.at, self.source, self.target, self.held, self.mine = at, source, target, held, mine
+        self.r_out, self.r_in, self.g_out, self.g_in = r_out, r_in, g_out, g_in
+        self.size = mine.shape[0]
+
+    def part(self, ref, group):
+        return ref.at[pl.ds(group * self.size, self.size)]
+
+    def peer(self, i):
+        return (self.at.first, self.at.second, self.at.corner)[i - 1]
+
+    def out(self, i):
         return sent(
-            self.source.at[to],
-            self.target.at[at.shard],
-            self.out.at[i],
-            self.come.at[i],
-            at.group,
-            to,
-        )
-
-    def keep(self, i):
-        here = self.at.shard
-        if i == 0:
-            return pltpu.make_async_copy(self.source.at[here], self.stage, self.own.at[0])
-        return pltpu.make_async_copy(self.stage, self.target.at[here], self.own.at[1])
+            self.part(self.source, self.peer(i)),
+            self.held.at[i],
+            self.r_out.at[i],
+            self.r_in.at[i],
+            self.peer(i),
+            self.at.shard,
+        )
+
+    def back(self, i):
+        return sent(
+            self.mine,
+            self.part(self.target, self.at.group),
+            self.g_out.at[i],
+            self.g_in.at[i],
+            self.peer(i),
+            self.at.shard,
+        )
+
+    def own(self, way):
+        if way == 0:
+            here = self.part(self.source, self.at.group)
+            return pltpu.make_async_copy(here, self.held.at[0], self.r_in.at[0])
+        here = self.part(self.target, self.at.group)
+        return pltpu.make_async_copy(self.mine, here, self.g_in.at[0])
 
     def start(self):
-        self.keep(0).start()
-        for i in range(self.at.shards - 1, 0, -1):
-            self.copy(i).start()
-        self.keep(0).wait()
-        self.keep(1).start()
-
-    def finish(self):
-        self.keep(1).wait()
-        for i in range(1, self.at.shards):
-            self.copy(i).wait()
+        self.own(0).start()
+        for i in (3, 1, 2):
+            self.out(i).start()
+
+    def turn(self):
+        self.own(0).wait()
+        for i in range(1, 4):
+            self.out(i).wait_recv()
+        total = self.held[0].astype(jnp.float32)
+        for i in range(1, 4):
+            total = total + self.held[i].astype(jnp.float32)
+        self.mine[...] = total.astype(self.mine.dtype)
+        self.own(1).start()
+        for i in (3, 1, 2):
+            self.back(i).start()
+
+    def wait(self):
+        self.own(1).wait()
+        for i in range(1, 4):
+            self.out(i).wait_send()
+            self.back(i).wait()
 
 
 class Gather:
@@ -862,24 +981,23 @@
                 self.accs[kind, q, :, span] = value.astype(self.accs.dtype)
                 self.side(q, kind - 1).start()
 
-    def lines(self):
+    def lines(self, q):
         at = self.at
-        for q in self.order:
-            self.pair(0, q)
-            if self.wide:
-                self.side(q, 0).wait_recv()
-                self.side(q, 1).wait_recv()
-                self.add(0, q, self.p_buf[0, q], self.p_buf[1, q])
-            for direction in range(2):
-
-                @pl.when(q > at.spot if direction == 0 else q < at.spot)
-                def _(q=q, direction=direction):
-                    @pl.when(at.spot > 0 if direction == 0 else at.spot < at.depth - 1)
-                    def _():
-                        self.line(q, direction).wait_recv()
-                        self.add(0, q, self.z_buf[direction, q])
-
-                    self.line(q, direction).start()
+        self.pair(0, q)
+        if self.wide:
+            self.side(q, 0).wait_recv()
+            self.side(q, 1).wait_recv()
+            self.add(0, q, self.p_buf[0, q], self.p_buf[1, q])
+        for direction in range(2):
+
+            @pl.when(q > at.spot if direction == 0 else q < at.spot)
+            def _(direction=direction):
+                @pl.when(at.spot > 0 if direction == 0 else at.spot < at.depth - 1)
+                def _():
+                    self.line(q, direction).wait_recv()
+                    self.add(0, q, self.z_buf[direction, q])
+
+                self.line(q, direction).start()
 
     def finish(self):
         at, total = self.at, self.total
@@ -914,14 +1032,17 @@
     return out
 
 
-def gather_body(shards, groups, wides, swaps, sizes, *refs):
-    count = len(wides) + swaps
+def gather_body(shards, groups, wides, plans, sizes, *refs):
+    count = len(wides) + len(plans)
     ins, outs = refs[:count], refs[count : 2 * count]
     scratch = cut_refs(refs[2 * count :], sizes)
     at = Place(shards, groups)
-    at.greet(any(wides), swaps > 0)
+    at.greet(any(wides), len(plans) > 0)
     gathers = [Gather(at, wide, ins[i], outs[i], *scratch[i]) for i, wide in enumerate(wides)]
-    moves = [Exchange(at, ins[i], outs[i], *scratch[i]) for i in range(len(wides), count)]
+    moves = [
+        Exchange(at, plan, ins[i], outs[i], *scratch[i])
+        for i, plan in enumerate(plans, len(wides))
+    ]
     marks = range(len(gathers[0].events))
     for k in marks:
         for g in gathers:
@@ -933,27 +1054,22 @@
             for g in gathers:
                 step(g, k)
     for m in moves:
-        m.finish()
-
-
-def gathered(arrays, wides, shards, groups, identity, swapped=()):
+        m.wait()
+
+
+def gathered(arrays, wides, shards, groups, identity, swapped=(), plans=()):
     shapes = [
         jax.ShapeDtypeStruct(
             (a.shape[0], shards * (groups if wide else 1)) + a.shape[1:], a.dtype
         )
         for a, wide in zip(arrays, wides)
-    ] + [jax.ShapeDtypeStruct(a.shape, a.dtype) for a in swapped]
+    ] + [jax.ShapeDtypeStruct(p.shape, a.dtype) for a, p in zip(swapped, plans)]
     moved = sum(s.size * s.dtype.itemsize for s in shapes)
     scratch = [Gather.scratch(a, wide, shards) for a, wide in zip(arrays, wides)]
-    scratch += [Exchange.scratch(a) for a in swapped]
+    scratch += [Exchange.scratch(p.block, a.dtype, p.count, shards) for a, p in zip(swapped, plans)]
     return pl.pallas_call(
         functools.partial(
-            gather_body,
-            shards,
-            groups,
-            tuple(wides),
-            len(swapped),
-            tuple(len(s) for s in scratch),
+            gather_body, shards, groups, tuple(wides), tuple(plans), tuple(len(s) for s in scratch)
         ),
         out_shape=shapes,
         in_specs=[pl.BlockSpec(memory_space=pltpu.VMEM)] * len(arrays)
@@ -965,60 +1081,394 @@
     )(*arrays, *swapped)
 
 
-def reduce_body(shards, groups, wides, swaps, sizes, *refs):
-    count = len(wides) + swaps
-    ins, outs = refs[:count], refs[count : 2 * count]
-    scratch = cut_refs(refs[2 * count :], sizes)
+def halved(array, wide):
+    block = array.size // array.shape[1] * array.dtype.itemsize
+    return not wide and array.shape[0] == 2 and block > 200_000
+
+
+def reduce_body(shards, groups, wides, halves, plans, sums, sizes, *refs):
+    given = len(wides) + len(plans)
+    count = given + sum(1 for kind, _ in sums if kind == "in")
+    results = given + len(sums)
+    ins, outs = refs[:count], refs[count : count + results]
+    scratch = cut_refs(refs[count + results :], sizes)
     at = Place(shards, groups)
-    at.greet(any(wides), swaps > 0)
-    sums = [Reduce(at, wide, ins[i], outs[i], *scratch[i]) for i, wide in enumerate(wides)]
-    moves = [Exchange(at, ins[i], outs[i], *scratch[i]) for i in range(len(wides), count)]
-    for r in sums:
+    at.greet(any(wides) or len(sums) > 0, len(plans) > 0, len(sums) > 0)
+    reductions = []
+    for i, wide in enumerate(wides):
+        if halves[i]:
+            for j in range(2):
+                half = pl.ds(j, 1)
+                reductions.append(
+                    Reduce(at, wide, ins[i].at[half], outs[i].at[half], *scratch.pop(0))
+                )
+        else:
+            reductions.append(Reduce(at, wide, ins[i], outs[i], *scratch.pop(0)))
+    moves = [
+        Exchange(at, plan, ins[i], outs[i], *scratch.pop(0))
+        for i, plan in enumerate(plans, len(wides))
+    ]
+    totals = []
+    for i, (kind, which) in enumerate(sums, given):
+        source = {"in": ins, "sum": outs, "swap": outs}[kind]
+        source = source[which + (0 if kind == "sum" else given if kind == "in" else len(wides))]
+        totals.append(Across(at, source, outs[i], *scratch.pop(0)))
+    flat = [r for r in reductions if not r.wide]
+    wide_ones = [r for r in reductions if r.wide]
+    order = reductions[0].order
+    late = [i for i in range(len(moves)) if flat and ("swap", i) not in sums]
+
+    def swapped_sums():
+        for (kind, which), s in zip(sums, totals):
+            if kind == "swap":
+                moves[which].wait()
+                s.start()
+
+    for r in reductions:
         r.begin()
-    for m in moves:
-        m.start()
-    for r in sums:
-        if r.wide:
-            r.corners()
-    for r in sums:
-        if not r.wide:
-            r.lines()
-    for r in sums:
-        if r.wide:
-            r.sides()
-            r.lines()
-    for r in sums:
+    for i, m in enumerate(moves):
+        if i not in late:
+            m.start()
+    for (kind, _), s in zip(sums, totals):
+        if kind == "in":
+            s.start()
+    for r in wide_ones:
+        r.corners()
+    for step, q in enumerate(order):
+        for r in flat:
+            r.lines(q)
+        if step == min(1, len(order) - 1):
+            for i in late:
+                moves[i].start()
+        if step == min(2, len(order) - 1):
+            swapped_sums()
+    for r in flat:
         r.finish()
-    for m in moves:
-        m.finish()
-
-
-def reduced(arrays, wides, shards, groups, identity, swapped=()):
+    for (kind, _), s in zip(sums, totals):
+        if kind == "sum":
+            s.start()
+    for r in wide_ones:
+        r.sides()
+    for s in totals:
+        s.turn()
+    for r in wide_ones:
+        for q in order:
+            r.lines(q)
+    for r in wide_ones:
+        r.finish()
+    for s in totals:
+        s.wait()
+    for i, m in enumerate(moves):
+        if ("swap", i) not in sums:
+            m.wait()
+
+
+def reduced(arrays, wides, shards, groups, identity, swapped=(), plans=(), sums=(), terms=()):
     shapes = [
         jax.ShapeDtypeStruct((a.shape[0],) + a.shape[2:], jnp.float32) for a in arrays
-    ] + [jax.ShapeDtypeStruct(a.shape, a.dtype) for a in swapped]
-    moved = sum(a.size * a.dtype.itemsize for a in (*arrays, *swapped))
-    scratch = [Reduce.scratch(a, wide, shards) for a, wide in zip(arrays, wides)]
-    scratch += [Exchange.scratch(a) for a in swapped]
+    ] + [jax.ShapeDtypeStruct(p.shape, a.dtype) for a, p in zip(swapped, plans)]
+    for kind, which in sums:
+        if kind == "in":
+            source = terms[which]
+        else:
+            source = shapes[which + (0 if kind == "sum" else len(arrays))]
+        shapes.append(jax.ShapeDtypeStruct(source.shape, source.dtype))
+    operands = (*arrays, *swapped, *terms)
+    moved = sum(a.size * a.dtype.itemsize for a in operands)
+    halves = tuple(halved(a, wide) for a, wide in zip(arrays, wides))
+    scratch = []
+    for a, wide, half in zip(arrays, wides, halves):
+        block = jax.ShapeDtypeStruct((1,) + a.shape[1:] if half else a.shape, a.dtype)
+        scratch += [Reduce.scratch(block, wide, shards)] * (2 if half else 1)
+    scratch += [Exchange.scratch(p.block, a.dtype, p.count, shards) for a, p in zip(swapped, plans)]
+    scratch += [Across.scratch(a.shape, a.dtype) for a in shapes[len(arrays) + len(swapped) :]]
     return pl.pallas_call(
         functools.partial(
             reduce_body,
             shards,
             groups,
             tuple(wides),
-            len(swapped),
+            halves,
+            tuple(plans),
+            tuple(sums),
             tuple(len(s) for s in scratch),
         ),
         out_shape=shapes,
-        in_specs=[pl.BlockSpec(memory_space=pl.ANY)] * (len(arrays) + len(swapped)),
+        in_specs=[pl.BlockSpec(memory_space=pl.ANY)] * len(operands),
         out_specs=[pl.BlockSpec(memory_space=pltpu.VMEM)] * len(arrays)
-        + [pl.BlockSpec(memory_space=pl.ANY)] * len(swapped),
+        + [pl.BlockSpec(memory_space=pl.ANY)] * (len(shapes) - len(arrays)),
         scratch_shapes=[s for some in scratch for s in some],
         compiler_params=pltpu.CompilerParams(
-            collective_id=identity, has_side_effects=True, vmem_limit_bytes=60 * 1024 * 1024
+            collective_id=identity, has_side_effects=True, vmem_limit_bytes=64 * 1024 * 1024 - 65536
         ),
         cost_estimate=pl.CostEstimate(flops=0, bytes_accessed=20 * moved, transcendentals=0),
-    )(*arrays, *swapped)
+    )(*operands)
+
+
+PAIR = 256
+TILE = 320
+
+
+def experts_body(
+    shape,
+    ids,
+    routes,
+    router,
+    n_from,
+    c_from,
+    w_from,
+    y_to,
+    d_to,
+    g_to,
+    rows_n,
+    rows_c,
+    weights,
+    picks,
+    slot_w,
+    slot_d,
+    act_rows,
+    gu_rows,
+    y_rows,
+    d_rows,
+    n_buf,
+    c_buf,
+    y_buf,
+    d_buf,
+    g_buf,
+    n_sem,
+    c_sem,
+    w_sem,
+    y_sem,
+    d_sem,
+    g_sem,
+):
+    units, pairs, slots, tokens, extra = shape
+    f32, bf16 = jnp.float32, jnp.bfloat16
+    whole = 2 * slots
+    chunk = weights.shape[0] // w_from.shape[0]
+
+    def bring(p, slot):
+        return (
+            pltpu.make_async_copy(n_from.at[pl.ds(2 * p, 2)], n_buf.at[slot], n_sem.at[slot]),
+            pltpu.make_async_copy(c_from.at[pl.ds(2 * p, 2)], c_buf.at[slot], c_sem.at[slot]),
+        )
+
+    def weight_copy(i):
+        return pltpu.make_async_copy(
+            w_from.at[i], weights.at[pl.ds(i * chunk, chunk)], w_sem.at[i]
+        )
+
+    for copy in bring(0, 0):
+        copy.start()
+    for i in range(w_from.shape[0]):
+        weight_copy(i).start()
+    row = lax.broadcasted_iota(jnp.int32, (PAIR, PAIR), 0)
+    column = lax.broadcasted_iota(jnp.int32, (PAIR, PAIR), 1)
+    upto = ((row <= column) & (row // tokens == column // tokens)).astype(bf16)
+    names = lax.broadcasted_iota(jnp.int32, (router.shape[0], PAIR), 0)
+    lanes = lax.broadcasted_iota(jnp.int32, (1, PAIR), 1)
+    places = lax.broadcasted_iota(jnp.int32, (whole, PAIR), 0)
+    sixteen = lax.broadcasted_iota(jnp.int32, (16, PAIR), 0)
+
+    def dispatch(p, _):
+        slot = p % 2
+        for copy in bring(p, slot):
+            copy.wait()
+
+        @pl.when(p + 1 < pairs)
+        def _():
+            for copy in bring(p + 1, 1 - slot):
+                copy.start()
+
+        n = n_buf[slot].reshape(PAIR, n_buf.shape[3])
+        c = c_buf[slot].reshape(PAIR, c_buf.shape[3])
+        named = routes[p]
+        logits = lax.dot_general(
+            router[...], n, (((1,), (1,)), ((), ())), preferred_element_type=f32
+        )
+        hit = names == named[0:1]
+        for j in range(1, TOP):
+            hit = hit | (names == named[j : j + 1])
+        masked = jnp.where(hit, logits, MASKED)
+        top = jnp.max(masked, axis=0, keepdims=True)
+        raised = jnp.where(hit, jnp.exp(masked - top), 0.0)
+        share = raised / jnp.sum(raised, axis=0, keepdims=True)
+        hits = []
+        for u in range(len(units)):
+            mine = hit & (names == ids[u])
+            hits.append(jnp.sum(jnp.where(mine, 1.0, 0.0), axis=0, keepdims=True))
+        both = jnp.zeros((16, PAIR), f32)
+        for u in range(len(units)):
+            both = jnp.where(sixteen == u, hits[u], both)
+        ranks = jnp.dot(both.astype(bf16), upto, preferred_element_type=f32)
+        for u in range(len(units)):
+            weight = jnp.sum(
+                jnp.where(hit & (names == ids[u]), share, 0.0), axis=0, keepdims=True
+            )
+            place = jnp.where(
+                hits[u] > 0.5,
+                ranks[u : u + 1].astype(jnp.int32) - 1 + lanes // tokens * slots,
+                -1,
+            )
+            pick = (places == place).astype(f32)
+            at = pl.ds(pl.multiple_of(p * whole, 16), whole)
+            slot_w[u, at] = jnp.sum(pick * weight, axis=1, keepdims=True)
+            pick = pick.astype(bf16)
+            picks[u, p] = pick
+            rows_n[u, at] = jnp.dot(pick, n, preferred_element_type=f32).astype(bf16)
+            rows_c[u, at] = jnp.dot(pick, c, preferred_element_type=f32).astype(bf16)
+        return 0
+
+    lax.fori_loop(0, pairs, dispatch, 0)
+    for i in range(w_from.shape[0]):
+        weight_copy(i).wait()
+    turned = (((1,), (1,)), ((), ()))
+    summed = (((0,), (0,)), ((), ()))
+    for u, (start, width) in enumerate(units):
+        gu = pl.ds(start, 2 * width)
+        down = pl.ds(start + 2 * width, width)
+
+        def tile(i, _, u=u, start=start, width=width, gu=gu, down=down):
+            at = pl.ds(pl.multiple_of(i * TILE, 16), TILE)
+            parts = jnp.dot(rows_n[u, at], weights[:, gu], preferred_element_type=f32)
+            plain = jnp.dot(rows_c[u, at], weights[:, down], preferred_element_type=f32)
+            gate, up = parts[:, :width], parts[:, width:]
+            sig = jax.nn.sigmoid(gate)
+            act = gate * sig * up
+            w = slot_w[u, at]
+            slot_d[u, at] = jnp.sum(act * plain, axis=1, keepdims=True)
+            act_w = (act * w).astype(bf16)
+            da = plain * w
+            d_gate = (da * up * sig * (1.0 + gate * (1.0 - sig))).astype(bf16)
+            d_up = (da * gate * sig).astype(bf16)
+            act_rows[u, at, :width] = act_w
+            gu_rows[u, at, :width] = d_gate
+            gu_rows[u, at, width : 2 * width] = d_up
+            y_rows[u, at] = lax.dot_general(
+                act_w, weights[:, down], turned, preferred_element_type=f32
+            ).astype(bf16)
+            d_rows[u, at] = lax.dot_general(
+                gu_rows[u, at, : 2 * width], weights[:, gu], turned, preferred_element_type=f32
+            ).astype(bf16)
+            return 0
+
+        lax.fori_loop(0, pairs * whole // TILE, tile, 0)
+
+    deep = 256
+
+    def grad_copy(i):
+        return pltpu.make_async_copy(
+            g_buf.at[pl.ds(i * chunk, chunk)], g_to.at[i], g_sem.at[i]
+        )
+
+    def grads(i, _):
+        at = pl.ds(pl.multiple_of(i * deep, deep), deep)
+        for u, (start, width) in enumerate(units):
+            g_buf[at, start : start + 2 * width] = lax.dot_general(
+                rows_n[u, :, at], gu_rows[u, :, : 2 * width], summed, preferred_element_type=f32
+            ).astype(bf16)
+            g_buf[at, start + 2 * width : start + 3 * width] = lax.dot_general(
+                rows_c[u, :, at], act_rows[u, :, :width], summed, preferred_element_type=f32
+            ).astype(bf16)
+        return 0
+
+    lax.fori_loop(0, weights.shape[0] // deep, grads, 0)
+    for i in range(g_to.shape[0]):
+        grad_copy(i).start()
+
+    def put(p, slot):
+        return (
+            pltpu.make_async_copy(y_buf.at[slot], y_to.at[pl.ds(2 * p, 2)], y_sem.at[slot]),
+            pltpu.make_async_copy(d_buf.at[slot], d_to.at[pl.ds(2 * p, 2)], d_sem.at[slot]),
+        )
+
+    d_buf[:, :, tokens:] = jnp.zeros((2, 2, extra, d_buf.shape[3]), bf16)
+
+    def combine(p, _):
+        slot = p % 2
+
+        @pl.when(p >= 2)
+        def _():
+            for copy in put(p - 2, slot):
+                copy.wait()
+
+        at = pl.ds(pl.multiple_of(p * whole, 16), whole)
+        y = jnp.zeros((PAIR, y_rows.shape[2]), f32)
+        d = jnp.zeros((PAIR, y_rows.shape[2]), f32)
+        d_w = jnp.zeros((TOP, PAIR), f32)
+        for u in range(len(units)):
+            pick = picks[u, p]
+            y = y + lax.dot_general(pick, y_rows[u, at], summed, preferred_element_type=f32)
+            d = d + lax.dot_general(pick, d_rows[u, at], summed, preferred_element_type=f32)
+            back = jnp.sum(pick.astype(f32) * slot_d[u, at], axis=0, keepdims=True)
+            d_w = d_w + jnp.where(routes[p] == ids[u], back, 0.0)
+        high = d_w.astype(bf16)
+        low = (d_w - high.astype(f32)).astype(bf16)
+        y_buf[slot] = y.astype(bf16).reshape(y_buf.shape[1:])
+        d_buf[slot, :, :tokens] = d.astype(bf16).reshape(2, tokens, d.shape[1])
+        both = jnp.concatenate([high.astype(f32), low.astype(f32)], axis=0).astype(bf16)
+        for i in range(2):
+            d_buf[slot, i, tokens:, :tokens] = both[:, i * tokens : (i + 1) * tokens]
+        for copy in put(p, slot):
+            copy.start()
+        return 0
+
+    lax.fori_loop(0, pairs, combine, 0)
+    for p in range(pairs - 2, pairs):
+        for copy in put(p, p % 2):
+            copy.wait()
+    for i in range(g_to.shape[0]):
+        grad_copy(i).wait()
+
+
+def experts(ids, routes, router, n_all, c_all, owned, units, slots, extra):
+    blocks, tokens, width = n_all.shape
+    pairs = blocks // 2
+    rows = pairs * 2 * slots
+    count = len(units)
+    hidden = max(w for _, w in units)
+    bf16, f32 = jnp.bfloat16, jnp.float32
+    shards, own_rows, columns = owned.shape
+    dma = pltpu.SemaphoreType.DMA
+    any_space, vmem = pl.BlockSpec(memory_space=pl.ANY), pl.BlockSpec(memory_space=pltpu.VMEM)
+    flops = 2 * rows * width * sum(w for _, w in units) * 9
+    return pl.pallas_call(
+        functools.partial(experts_body, (tuple(units), pairs, slots, tokens, extra)),
+        out_shape=[
+            jax.ShapeDtypeStruct((blocks, tokens, width), bf16),
+            jax.ShapeDtypeStruct((blocks, tokens + extra, width), bf16),
+            jax.ShapeDtypeStruct(owned.shape, bf16),
+        ],
+        in_specs=[pl.BlockSpec(memory_space=pltpu.SMEM), vmem, vmem] + [any_space] * 3,
+        out_specs=[any_space] * 3,
+        scratch_shapes=[
+            pltpu.VMEM((count, rows, width), bf16),
+            pltpu.VMEM((count, rows, width), bf16),
+            pltpu.VMEM((shards * own_rows, columns), bf16),
+            pltpu.VMEM((count, pairs, 2 * slots, PAIR), bf16),
+            pltpu.VMEM((count, rows, 1), f32),
+            pltpu.VMEM((count, rows, 1), f32),
+            pltpu.VMEM((count, rows, hidden), bf16),
+            pltpu.VMEM((count, rows, 2 * hidden), bf16),
+            pltpu.VMEM((count, rows, width), bf16),
+            pltpu.VMEM((count, rows, width), bf16),
+            pltpu.VMEM((2, 2, tokens, width), bf16),
+            pltpu.VMEM((2, 2, tokens, width), bf16),
+            pltpu.VMEM((2, 2, tokens, width), bf16),
+            pltpu.VMEM((2, 2, tokens + extra, width), bf16),
+            pltpu.VMEM((shards * own_rows, columns), bf16),
+            dma((2,)),
+            dma((2,)),
+            dma((shards,)),
+            dma((2,)),
+            dma((2,)),
+            dma((shards,)),
+        ],
+        compiler_params=pltpu.CompilerParams(vmem_limit_bytes=67_000_000),
+        cost_estimate=pl.CostEstimate(
+            flops=flops, bytes_accessed=60 * 1024 * 1024, transcendentals=rows * hidden
+        ),
+    )(ids, routes, router, n_all, c_all, owned)
 
 
 def local(
@@ -1061,23 +1511,22 @@
         ),
         (1, 0, 2),
     )
-    group_inputs, small_all, routes_all, c_all, qkv_own = gathered(
+    group_inputs, small_all, routes_all, qkv_own = gathered(
         [
             inputs.reshape(sequences, DEVICE_TOKENS, MODEL_WIDTH),
             small[None],
             jnp.transpose(routes)[None],
-            cotangent[None],
         ],
-        (False, False, True, True),
+        (False, False, True),
         shards,
         groups,
         0,
         [qkv_cut],
+        [Rows(qkv_cut)],
     )
     qkv_own = qkv_own.reshape(MODEL_WIDTH, query_width + 2 * key_width)
-    r_all = jnp.transpose(routes_all[0], (0, 2, 1))
-    c_all = c_all[0]
     small = small_all.reshape(MODEL_WIDTH, LANES)
+    router_pad = jnp.where(jnp.arange(LANES) < E, small, 0)
     router, gain_one, gain_two = small[:, :E], small[:, E].astype(f32), small[:, E + 1].astype(f32)
 
     group_wide = group_inputs.reshape(sequences * length, MODEL_WIDTH).astype(f32)
@@ -1121,19 +1570,19 @@
     n_two = (z_two * gain_two).astype(bf16)
 
     blocks = groups * shards
-    n_all, experts_own = gathered(
-        [n_two[None]], (True,), shards, groups, 2, [packed_experts(w_experts, shards)]
-    )
+    experts_cut = jnp.transpose(w_experts, (1, 0, 2))
+    n_all, c_all, experts_own = gathered(
+        [n_two[None], cotangent[None]],
+        (True, True),
+        shards,
+        groups,
+        2,
+        [experts_cut],
+        [Experts(experts_cut, shards, experts_here, False)],
+    )
+    c_all = c_all[0]
     n_all = n_all[0]
-    experts_own = experts_own.reshape(MODEL_WIDTH, -1)
-
-    def weights_of(rows, picks_of):
-        logits = jnp.einsum("...d,de->...e", rows, router, preferred_element_type=f32)
-        picks = (picks_of[..., None] == jnp.arange(E, dtype=jnp.int32)).astype(f32)
-        chosen = jnp.sum(picks * logits[..., None, :], axis=-1)
-        return jax.nn.softmax(chosen, axis=-1), picks
-
-    w_all, _ = weights_of(n_all, r_all)
+
     whole, extra = divmod(experts_here, shards)
     owned = [(group * experts_here + shard * whole + i, i * 3 * FF, FF) for i in range(whole)]
     if extra:
@@ -1142,73 +1591,37 @@
             (group * experts_here + whole * shards + shard // cuts, whole * 3 * FF, FF // cuts)
         )
     slots = -(-CAP // 8) * 8
-    lower = (jnp.arange(tokens)[:, None] <= jnp.arange(tokens)[None, :]).astype(bf16)
-    picked, slot_weights = [], []
-    for expert, _, _ in owned:
-        hit = jnp.any(r_all == expert, axis=-1)
-        rank = jnp.einsum("bt,tu->bu", hit.astype(bf16), lower, preferred_element_type=f32)
-        place = jnp.where(hit, rank.astype(jnp.int32) - 1, -1)
-        pick = place[:, None, :] == jnp.arange(slots, dtype=jnp.int32)[None, :, None]
-        weight = jnp.sum(jnp.where(r_all == expert, w_all, 0.0), axis=-1)
-        picked.append(pick)
-        slot_weights.append(jnp.sum(jnp.where(pick, weight[:, None, :], 0.0), axis=-1))
-    selection = jnp.concatenate(picked, axis=1).astype(bf16)
-    n_sent = jnp.einsum("bct,btd->bcd", selection, n_all, preferred_element_type=f32).astype(bf16)
-    c_sent = jnp.einsum("bct,btd->bcd", selection, c_all, preferred_element_type=f32).astype(bf16)
-    produced, d_rows, grads = [], [], []
-    d_weights = jnp.zeros((blocks, tokens, TOP), f32)
-    for i, (expert, start, width) in enumerate(owned):
-        a = n_sent[:, i * slots : (i + 1) * slots].reshape(blocks * slots, MODEL_WIDTH)
-        c = c_sent[:, i * slots : (i + 1) * slots].reshape(blocks * slots, MODEL_WIDTH)
-        gate_up = experts_own[:, start : start + 2 * width]
-        down = experts_own[:, start + 2 * width : start + 3 * width]
-        both_parts = jnp.dot(a, gate_up, preferred_element_type=f32)
-        d_plain = jnp.dot(c, down, preferred_element_type=f32)
-        gate, up = both_parts[:, :width], both_parts[:, width:]
-        sig = jax.nn.sigmoid(gate)
-        act = gate * sig * up
-        w = slot_weights[i].reshape(-1, 1)
-        d_slot = jnp.sum(act * d_plain, axis=-1).reshape(blocks, slots)
-        d_token = jnp.sum(jnp.where(picked[i], d_slot[:, :, None], 0.0), axis=1)
-        d_weights = d_weights + jnp.where(r_all == expert, d_token[:, :, None], 0.0)
-        act_w = (act * w).astype(bf16)
-        da = d_plain * w
-        d_gu = jnp.concatenate(
-            [da * up * sig * (1.0 + gate * (1.0 - sig)), da * gate * sig], axis=1
-        ).astype(bf16)
-        produced.append(
-            jnp.einsum("rf,df->rd", act_w, down, preferred_element_type=f32)
-            .astype(bf16)
-            .reshape(blocks, slots, MODEL_WIDTH)
-        )
-        d_rows.append(
-            jnp.einsum("rf,df->rd", d_gu, gate_up, preferred_element_type=f32)
-            .astype(bf16)
-            .reshape(blocks, slots, MODEL_WIDTH)
-        )
-        grads.append(jnp.einsum("rd,rf->df", a, d_gu, preferred_element_type=f32))
-        grads.append(jnp.einsum("rd,rf->df", c, act_w, preferred_element_type=f32))
-    d_sums = jnp.einsum(
-        "bct,bcd->btd", selection, jnp.concatenate(d_rows, axis=1), preferred_element_type=f32
-    ).astype(bf16)
-    high = d_weights.astype(bf16)
-    low = (d_weights - high.astype(f32)).astype(bf16)
-    pad_rows = 16
-    carried = jnp.stack([high, low], axis=1).reshape(blocks, 2, tokens * TOP)
-    carried = jnp.pad(carried, ((0, 0), (0, pad_rows - 2), (0, MODEL_WIDTH - tokens * TOP)))
-    grads = jnp.concatenate(grads, axis=1).astype(bf16).reshape(shards, own_rows, -1)
-    back, grads = reduced(
-        [jnp.concatenate([d_sums, carried], axis=1)[None]], (True,), shards, groups, 3, [grads]
+    routes_pairs = jnp.transpose(
+        routes_all.reshape(blocks // 2, 2, TOP, tokens), (0, 2, 1, 3)
+    ).reshape(blocks // 2, TOP, 2 * tokens)
+    o_sums, d_sums, grads = experts(
+        jnp.stack([expert for expert, _, _ in owned]).astype(jnp.int32),
+        routes_pairs,
+        jnp.transpose(router_pad)[: -(-E // 16) * 16],
+        n_all,
+        c_all,
+        experts_own,
+        [(start, width) for _, start, width in owned],
+        slots,
+        2 * TOP,
+    )
+    back, moe_sum, gate_up = reduced(
+        [d_sums[None], o_sums[None]],
+        (True, True),
+        shards,
+        groups,
+        3,
+        [grads],
+        [Experts(grads, shards, experts_here, True, (0, 2))],
     )
     back = back[0]
-    grad_experts = unpacked_experts(grads, experts_here).astype(f32)
-    o_sums = jnp.einsum(
-        "bct,bcd->btd", selection, jnp.concatenate(produced, axis=1), preferred_element_type=f32
-    ).astype(bf16)
-
-    weights, picks = weights_of(n_two, routes)
-    carried_back = back[tokens : tokens + 2, : tokens * TOP]
-    d_weights = (carried_back[0] + carried_back[1]).reshape(tokens, TOP)
+    outputs = (h_one + moe_sum[0]).astype(bf16)
+
+    logits = jnp.dot(n_two, router, preferred_element_type=f32)
+    picks = (routes[:, :, None] == jnp.arange(E, dtype=jnp.int32)).astype(f32)
+    weights = jax.nn.softmax(jnp.sum(picks * logits[:, None, :], axis=-1), axis=-1)
+    carried = back[tokens:, :tokens]
+    d_weights = jnp.transpose(carried[:TOP] + carried[TOP:])
     d_chosen = weights * (d_weights - jnp.sum(weights * d_weights, axis=-1, keepdims=True))
     d_logits = jnp.sum(picks * d_chosen[:, :, None], axis=1).astype(bf16)
     grad_router = jnp.einsum("td,te->de", n_two, d_logits, preferred_element_type=f32)
@@ -1262,23 +1675,27 @@
         [grad_router, grad_gain_one[:, None], grad_gain_two[:, None]], axis=1
     ).astype(bf16)
     grad_small = jnp.pad(grad_small, ((0, 0), (0, LANES - E - 2)))
-    d_n_one, grad_small, moe_sum, grad_qkv = reduced(
+    grad_qkv = grad_qkv.astype(bf16).reshape(shards, own_rows, -1)
+    d_n_one, _, _, down, grad_qkv, grad_small, grad_output = reduced(
         [
             d_normed.astype(bf16).reshape(line_shape),
-            grad_small.reshape(1, shards, own_rows, LANES),
-            o_sums[None],
+            jnp.transpose(
+                grad_small.reshape(shards, groups, own_rows // groups, LANES), (1, 0, 2, 3)
+            ),
         ],
-        (False, False, True),
+        (False, False),
         shards,
         groups,
         5,
-        [grad_qkv.astype(bf16).reshape(shards, own_rows, -1)],
-    )
+        [grad_qkv, grads],
+        [Rows(grad_qkv), Experts(grads, shards, experts_here, True, (2, 3))],
+        [("swap", 0), ("sum", 1), ("in", 0)],
+        [grad_output.astype(bf16).reshape(groups, own_rows // groups, MODEL_WIDTH)],
+    )
+    grad_experts = jnp.transpose(jnp.concatenate([gate_up, down], axis=2), (1, 0, 2)).astype(f32)
+    grad_output = grad_output.reshape(own_rows, MODEL_WIDTH)
+    grad_small = grad_small.reshape(own_rows, LANES)
     d_n_one = d_n_one.reshape(tokens, MODEL_WIDTH)
-    outputs = (h_one + moe_sum[0]).astype(bf16)
-    grad_qkv, grad_output, grad_small = lax.psum(
-        (grad_qkv, grad_output.astype(bf16), grad_small[0].astype(bf16)), "expert"
-    )
     grad_small = grad_small.astype(f32)
 
     def columns(start, width):

time: 963 us -> 803 us (0.83)
  matrix products: 132 us -> 35.1 us
  Pallas kernels: 616 us -> 698 us
  local copies, waits for them, and re-layouts: 94.1 us -> 25.1 us
  other arithmetic: 68.8 us -> 38.5 us
  blocking collectives: 16 us -> 0 us
  between operations: 15.7 us -> 1.9 us
  waiting for transfers between devices: 13.1 us -> 0 us
    dot_general x20 -> x1, matrix products: 96 us -> 1.27 us  [local(): logits = jnp.dot(n_two, router, preferred_element_type=f32)]
    pallas_call x0 -> x1, Pallas kernels: none -> 72 us  [experts(): pl.pallas_call(functools.partial(experts_body, (tuple(units), pairs, slot...]
    dot_general x4 -> x0, local copies, waits for them, and re-layouts: 25.6 us -> none  [the longest x2 13 us: local(): grads.append(jnp.einsum('rd,rf->df', a, d_gu, preferred_element_type=f32))]
    slice x10 -> x1, local copies, waits for them, and re-layouts: 25.2 us -> 0.67 us  [local(): jnp.transpose(router_pad)[:-(-E // 16) * 16]]
    psum x1 -> x0, blocking collectives: 16 us -> none  [local(): lax.psum((grad_qkv, grad_output.astype(bf16), grad_small[0].astype(bf16))...]
    reshape x6 -> x2, local copies, waits for them, and re-layouts: 17.3 us -> 1.94 us  [the longest x1 1.16 us: local(): small = small_all.reshape(MODEL_WIDTH, LANES)]
    psum x1 -> x0, waiting for transfers between devices: 13.1 us -> none  [local(): lax.psum((grad_qkv, grad_output.astype(bf16), grad_small[0].astype(bf16))...]
    broadcast_in_dim x1 -> x0, other arithmetic: 13 us -> none  [local(): jnp.concatenate([d_sums, carried], axis=1)[None]]
  transfers between devices with their start and end apart: 1 -> 0, of which waited for: 1 -> 0; matrix products, arithmetic and copies ran while one was open for 4% -> 0% of each run, Pallas kernels for 0% -> 0%
where the time goes in v2:
time: 803 us; the launch traced here: 798 us
  Pallas kernels  698 us (87%)
  other arithmetic  38.5 us (5%)
  matrix products  35.1 us (4%)
  local copies, waits for them, and re-layouts  25.1 us (3%)
    pallas_call x3, Pallas kernels, reduced(): pl.pallas_call(functools.partial(reduce_body, shards, groups, tuple(wides...  353 us
    pallas_call x3, Pallas kernels, gathered(): pl.pallas_call(functools.partial(gather_body, shards, groups, tuple(wides...  272 us
    pallas_call x1, Pallas kernels, experts(): pl.pallas_call(functools.partial(experts_body, (tuple(units), pairs, slot...  72 us

profile of v2, /device:TPU:10, one launch (start us, length us, event | category | flops | bytes accessed | tf_op | source)
XLA Modules:
  0.0 798.1 jit_solution(11390007078194618278)
XLA Ops:
  6.3 1.7 reshape.449
  8.2 1.4 maximum_bitcast_fusion.refs_3_
  9.6 64.7 %shard_map.186 = (bf16[2,8,64,1536]{3,2,1,0:T(8,128)(2,1)}, bf16[1,8,192,128]{3,2,1,0:T(8,128)(2,1)}, s32[1,32,8,128]{3,2,1,0:T(8,128)}, bf16[8,192,320]{2,1,0:T(8,128)(2,1)}) custom-call(bf16[2,64,1536]{2,1,0:T(8,128)(2,1)} %bitcast.236, bf16[1,192,128]{2,1,0:T(8,128)(2,1)} %fusion.40.refs_1_, s32[1,8,128]{2,1,0:T(8,128)} %bitcast.267, ...), custom_call_target="tpu_custom_call" | custom-call | bytes 93061120 | tf_op jit(solution)/shard_map/pallas_call | solution.py:1070
  74.4 2.7 multiply_reduce_fusion.1
  77.8 2.3 convert_reduce_fusion
  81.5 1.2 fusion.56
  85.3 3.9 fusion.3
  89.3 4.3 exponential_reduce_fusion
  93.9 1.8 fusion.7
  96.2 2.7 convolution_convert_fusion
  98.9 39.3 %shard_map.187 = f32[2,64,1536]{2,1,0:T(8,128)} custom-call(bf16[2,8,64,1536]{3,2,1,0:T(8,128)(2,1)} %bitcast.225), custom_call_target="tpu_custom_call" | custom-call | bytes 62914560 | tf_op jit(solution)/shard_map/pallas_call | solution.py:1185
  138.2 1.5 multiply_reduce_fusion.4
  143.7 176.6 %shard_map.188 = (bf16[1,32,128,1536]{3,2,1,0:T(8,128)(2,1)}, bf16[1,32,128,1536]{3,2,1,0:T(8,128)(2,1)}, bf16[8,192,1920]{2,1,0:T(8,128)(2,1)}) custom-call(bf16[1,128,1536]{2,1,0:T(8,128)(2,1)} %fusion.75.refs_0_, bf16[1,128,1536]{2,1,0:T(8,128)(2,1)} %bitcast.241, bf16[10,192,1536]{2,1,0:T(8,128)(2,1)} %bitcast.237), custom_call_target="tpu_custom_call" | custom-call | bytes 621281280 | tf_op jit(solution)/shard_map/pallas_call | solution.py:1070
  320.3 72.0 %shard_map.189 = (bf16[32,128,1536]{2,1,0:T(8,128)(2,1)}, bf16[32,144,1536]{2,1,0:T(8,128)(2,1)}, bf16[8,192,1920]{2,1,0:T(8,128)(2,1)}) custom-call(s32[2]{0:T(128)} %pad_add_fusion.ids, s32[16,8,256]{2,1,0:T(8,128)} %bitcast.275, bf16[48,1536]{1,0:T(8,128)(2,1)} %slice.112.router, bf16[32,128,1536]{2,1,0:T(8,128)(2,1)} %bitcast.271, ...), custom_call_target="tpu_custom_call" | custom-call | flops 22649241600 | bytes 62914560 | tf_op jit(solution)/shard_map/pallas_call | solution.py:1435
  392.4 178.1 %shard_map.190 = (f32[1,144,1536]{2,1,0:T(8,128)}, f32[1,128,1536]{2,1,0:T(8,128)}, bf16[10,192,1024]{2,1,0:T(8,128)(2,1)}) custom-call(bf16[1,32,144,1536]{3,2,1,0:T(8,128)(2,1)} %bitcast.226, bf16[1,32,128,1536]{3,2,1,0:T(8,128)(2,1)} %bitcast.229, bf16[8,192,1920]{2,1,0:T(8,128)(2,1)} %get-tuple-element.37.refs_2_.refs_3_), custom_call_target="tpu_custom_call" | custom-call | bytes 652738560 | tf_op jit(solution)/shard_map/pallas_call | solution.py:1185
  570.5 1.4 multiply_convert_fusion.2
  571.9 1.3 fusion.22
  576.1 2.0 multiply_reduce_fusion.2
  579.2 31.1 %shard_map.191 = bf16[2,8,64,1536]{3,2,1,0:T(8,128)(2,1)} custom-call(bf16[2,64,1536]{2,1,0:T(8,128)(2,1)} %bitcast.252), custom_call_target="tpu_custom_call" | custom-call | bytes 62914560 | tf_op jit(solution)/shard_map/pallas_call | solution.py:1070
  610.3 3.1 convolution_convert_fusion.4
  614.8 5.0 fusion.5
  622.9 1.8 fusion.11
  625.1 4.6 multiply_reduce_fusion
  631.1 4.4 convolution_convert_fusion.1
  635.5 2.3 copy.151
  637.8 1.6 convolution_convert_fusion.2
  639.4 135.7 %shard_map.192 = (f32[2,64,1536]{2,1,0:T(8,128)}, f32[4,48,128]{2,1,0:T(8,128)}, bf16[8,192,320]{2,1,0:T(8,128)(2,1)}, bf16[10,192,512]{2,1,0:T(8,128)(2,1)}, bf...) custom-call(bf16[2,8,64,1536]{3,2,1,0:T(8,128)(2,1)} %bitcast.243, ...), custom_call_target="tpu_custom_call" | custom-call | bytes 220200960 | tf_op jit(solution)/shard_map/pallas_call | solution.py:1185
  775.1 1.6 fusion.14
  776.7 3.5 fusion.17
  782.1 1.5 reshape.477
  786.3 2.2 bitcast_convert_fusion
  789.8 8.1 %convert_bitcast_fusion = f32[192,10,1536]{2,0,1:T(8,128)} fusion(bf16[10,192,512]{2,1,0:T(8,128)(2,1)S(1)} %copy-done.11, bf16[10,192,1024]{2,1,0:T(8,128)(2,1)} %get-tuple-element.44), kind=kLoop, calls=%fused_computation | loop fusion | flops 11796480 | bytes 17694720 | tf_op jit(solution)/shard_map/convert_element_type | solution.py:1695
  (177 shorter events, 30.9 us)
Async XLA Ops:
  74.3 5.8 copy-start.2
  80.1 13.4 %copy-start.16 = (pred[512,512]{0,1:T(8,128)(4,1)}, pred[512,512]{0,1:T(8,128)(4,1)S(1)}, u32[]{:S(2)}) copy-start(pred[512,512]{0,1:T(8,128)(4,1)S(1)} %iota_compare_fusion) | copy-start | bytes 786436
  84.8 4.4 copy-start.12
  84.9 4.2 copy-start.19
  84.9 4.2 copy-start.21
  85.3 3.9 copy-start.28
  85.3 3.9 copy-start.30
  89.3 4.3 copy-start.35
  89.3 4.6 copy-start.6
  95.7 3.2 copy-start.14
  138.2 4.6 copy-start.26
  139.7 180.6 %copy-start = (f32[128,1536]{1,0:T(8,128)}, f32[128,1536]{1,0:T(8,128)S(1)}, u32[]{:S(2)}) copy-start(f32[128,1536]{1,0:T(8,128)S(1)} %get-tuple-element.81) | copy-start | bytes 2359300
  140.3 180.0 %copy-start.37 = (f32[128]{0:T(128)}, f32[128]{0:T(128)S(1)}, u32[]{:S(2)}) copy-start(f32[128]{0:T(128)S(1)} %get-tuple-element.112) | copy-start | bytes 1540
  570.5 7.6 copy-start.1
  570.5 7.6 copy-start.9
  570.5 7.6 copy-start.27
  570.5 7.6 copy-start.38
  578.1 32.2 %copy-start.24 = (bf16[192,1536]{1,0:T(8,128)(2,1)S(1)}, bf16[192,1536]{1,0:T(8,128)(2,1)}, u32[]{:S(2)}) copy-start(bf16[192,1536]{1,0:T(8,128)(2,1)} %param.18) | copy-start | bytes 1769476
  578.1 32.2 %copy-start.42 = (f32[128]{0:T(128)}, f32[128]{0:T(128)S(1)}, u32[]{:S(2)}) copy-start(f32[128]{0:T(128)S(1)} %broadcast_multiply_fusion.1) | copy-start | bytes 1540
  610.3 4.0 copy-start.15
  610.3 4.4 copy-start.17
  610.3 4.4 copy-start.36
  610.3 4.4 copy-start.40
  614.7 5.0 copy-start.29
  614.7 5.0 copy-start.31
  614.8 8.1 %slice-start = ((s8[6291456]{0:T(1024)(128)(4,1)}), s8[4194304]{0:T(1024)(128)(4,1)S(1)}, s32[]{:S(2)}) async-start(s8[6291456]{0:T(1024)(128)(4,1)} %bitcast.234), calls=%async_computation | async-start | bytes 8388608
  625.1 4.6 copy-start.32
  631.1 6.7 copy-start.4
  631.1 6.7 copy-start.8
  775.1 5.1 copy-start.18
  775.1 5.9 copy-start.10
  785.0 4.8 copy-start.11
  (15 other events, 25.1 us)

commit v3 on v2

--- a/solution.py
+++ b/solution.py
@@ -419,20 +419,11 @@
     )
 
 
-def divides(shards, groups):
-    experts_here = E // groups
-    if groups != 4 or shards % 2 or shards < 4:
+def fits(shards, groups):
+    if groups != 4 or shards != KEY_VALUE_HEADS or shards % 2 or E % groups:
         return False
-    if KEY_VALUE_HEADS % shards or shards > experts_here:
-        return False
-    extra = experts_here % shards
-    return extra == 0 or (shards % extra == 0 and FF % (shards // extra) == 0)
-
-
-def rotated(values, cosine, sine):
-    half = HEAD_SIZE // 2
-    first, second = values[..., :half], values[..., half:]
-    return jnp.concatenate([first * cosine - second * sine, second * cosine + first * sine], axis=-1)
+    extra = E // groups % shards
+    return E // groups > shards and extra > 0 and FF % (shards // extra * LANES) == 0
 
 
 def alternating(depth):
@@ -572,45 +563,45 @@
 
 
 class Experts:
-    def __init__(self, array, shards, experts_here, back, thirds=(0, 3)):
-        self.shards, self.back, self.first = shards, back, thirds[0]
-        self.thirds = thirds[1] - thirds[0]
+    def __init__(self, array, shards, experts_here, back, thirds=(0, 3), cut_thirds=(0, 3)):
+        self.back, self.thirds, self.cut_thirds = back, thirds, cut_thirds
         self.whole, self.extra = divmod(experts_here, shards)
+        self.shards = shards
         self.cuts = shards // self.extra if self.extra else 1
         self.width = FF // self.cuts
+        if not self.extra:
+            self.cut_thirds = (0, 0)
         rows = array.shape[1]
         held = 3 * (FF * self.whole + (self.width if self.extra else 0))
-        moved = held * self.thirds // 3
-        self.shape = (experts_here, rows, self.thirds * FF) if back else (shards, rows, held)
-        self.block = (rows, moved)
-        self.parts = [(slice(None), cut) for cut in self.inside(0, self.thirds)]
+        self.shape = (experts_here, rows, 3 * FF) if back else (shards, rows, held)
+        self.block = (rows, held)
+        self.parts = [cut for _, cut in self.owner_cuts()]
         self.count = len(self.parts)
 
-    def inside(self, first, thirds):
-        cuts = [
-            pl.ds((i * thirds + first) * FF, self.thirds * FF) for i in range(self.whole)
-        ]
-        if self.extra:
-            start = self.whole * thirds * FF
-            cuts += [
-                pl.ds(start + (first + k) * self.width, self.width) for k in range(self.thirds)
-            ]
-        return cuts
+    def owner_cuts(self):
+        cuts = []
+        first, last = self.thirds
+        for i in range(self.whole if last > first else 0):
+            cuts.append((i, pl.ds((3 * i + first) * FF, (last - first) * FF)))
+        start = self.whole * 3 * FF
+        for k in range(*self.cut_thirds):
+            cuts.append((k, pl.ds(start + k * self.width, self.width)))
+        return [(k, (slice(None), cut)) for k, cut in cuts]
 
     def owner(self, i):
-        return [(i, slice(None), cut) for cut in self.inside(self.first, 3)]
+        return [(i, *cut) for _, cut in self.owner_cuts()]
 
     def outside(self, i):
-        first = 0 if self.back else self.first
-        cuts = [
-            (i * self.whole + k, slice(None), pl.ds(first * FF, self.thirds * FF))
-            for k in range(self.whole)
-        ]
-        if self.extra:
+        cuts = []
+        first, last = self.thirds
+        for k in range(self.whole if last > first else 0):
+            cuts.append(
+                (i * self.whole + k, slice(None), pl.ds(first * FF, (last - first) * FF))
+            )
+        for k in range(*self.cut_thirds):
             expert = self.whole * self.shards + i // self.cuts
-            for k in range(self.thirds):
-                start = pl.multiple_of((first + k) * FF + i % self.cuts * self.width, 128)
-                cuts.append((expert, slice(None), pl.ds(start, self.width)))
+            start = pl.multiple_of(k * FF + i % self.cuts * self.width, 128)
+            cuts.append((expert, slice(None), pl.ds(start, self.width)))
         return cuts
 
     def take(self, i):
@@ -1217,6 +1208,7 @@
     n_from,
     c_from,
     w_from,
+    w_cut,
     y_to,
     d_to,
     g_to,
@@ -1253,15 +1245,22 @@
             pltpu.make_async_copy(c_from.at[pl.ds(2 * p, 2)], c_buf.at[slot], c_sem.at[slot]),
         )
 
-    def weight_copy(i):
-        return pltpu.make_async_copy(
-            w_from.at[i], weights.at[pl.ds(i * chunk, chunk)], w_sem.at[i]
-        )
+    split = units[-1][0]
+
+    def weight_copies(i):
+        here = pl.ds(i * chunk, chunk)
+        for k, (source, cut) in enumerate(
+            ((w_from, pl.ds(0, split)), (w_cut, pl.ds(split, weights.shape[1] - split)))
+        ):
+            yield pltpu.make_async_copy(
+                source.at[i, :, cut], weights.at[here, cut], w_sem.at[i, k]
+            )
 
     for copy in bring(0, 0):
         copy.start()
     for i in range(w_from.shape[0]):
-        weight_copy(i).start()
+        for copy in weight_copies(i):
+            copy.start()
     row = lax.broadcasted_iota(jnp.int32, (PAIR, PAIR), 0)
     column = lax.broadcasted_iota(jnp.int32, (PAIR, PAIR), 1)
     upto = ((row <= column) & (row // tokens == column // tokens)).astype(bf16)
@@ -1313,15 +1312,19 @@
             pick = (places == place).astype(f32)
             at = pl.ds(pl.multiple_of(p * whole, 16), whole)
             slot_w[u, at] = jnp.sum(pick * weight, axis=1, keepdims=True)
-            pick = pick.astype(bf16)
-            picks[u, p] = pick
-            rows_n[u, at] = jnp.dot(pick, n, preferred_element_type=f32).astype(bf16)
-            rows_c[u, at] = jnp.dot(pick, c, preferred_element_type=f32).astype(bf16)
+            picks[p, u * whole : (u + 1) * whole] = pick.astype(bf16)
+        at = pl.ds(pl.multiple_of(p * whole, 16), whole)
+        sent_n = jnp.dot(picks[p], n, preferred_element_type=f32).astype(bf16)
+        sent_c = jnp.dot(picks[p], c, preferred_element_type=f32).astype(bf16)
+        for u in range(len(units)):
+            rows_n[u, at] = sent_n[u * whole : (u + 1) * whole]
+            rows_c[u, at] = sent_c[u * whole : (u + 1) * whole]
         return 0
 
     lax.fori_loop(0, pairs, dispatch, 0)
     for i in range(w_from.shape[0]):
-        weight_copy(i).wait()
+        for copy in weight_copies(i):
+            copy.wait()
     turned = (((1,), (1,)), ((), ()))
     summed = (((0,), (0,)), ((), ()))
     for u, (start, width) in enumerate(units):
@@ -1393,13 +1396,14 @@
                 copy.wait()
 
         at = pl.ds(pl.multiple_of(p * whole, 16), whole)
-        y = jnp.zeros((PAIR, y_rows.shape[2]), f32)
-        d = jnp.zeros((PAIR, y_rows.shape[2]), f32)
+        pick = picks[p]
+        both = [y_rows[u, at] for u in range(len(units))]
+        y = lax.dot_general(pick, jnp.concatenate(both), summed, preferred_element_type=f32)
+        both = [d_rows[u, at] for u in range(len(units))]
+        d = lax.dot_general(pick, jnp.concatenate(both), summed, preferred_element_type=f32)
         d_w = jnp.zeros((TOP, PAIR), f32)
         for u in range(len(units)):
-            pick = picks[u, p]
-            y = y + lax.dot_general(pick, y_rows[u, at], summed, preferred_element_type=f32)
-            d = d + lax.dot_general(pick, d_rows[u, at], summed, preferred_element_type=f32)
+            pick = picks[p, u * whole : (u + 1) * whole]
             back = jnp.sum(pick.astype(f32) * slot_d[u, at], axis=0, keepdims=True)
             d_w = d_w + jnp.where(routes[p] == ids[u], back, 0.0)
         high = d_w.astype(bf16)
@@ -1421,7 +1425,7 @@
         grad_copy(i).wait()
 
 
-def experts(ids, routes, router, n_all, c_all, owned, units, slots, extra):
+def experts(ids, routes, router, n_all, c_all, owned, owned_cut, units, slots, extra):
     blocks, tokens, width = n_all.shape
     pairs = blocks // 2
     rows = pairs * 2 * slots
@@ -1439,13 +1443,13 @@
             jax.ShapeDtypeStruct((blocks, tokens + extra, width), bf16),
             jax.ShapeDtypeStruct(owned.shape, bf16),
         ],
-        in_specs=[pl.BlockSpec(memory_space=pltpu.SMEM), vmem, vmem] + [any_space] * 3,
+        in_specs=[pl.BlockSpec(memory_space=pltpu.SMEM), vmem, vmem] + [any_space] * 4,
         out_specs=[any_space] * 3,
         scratch_shapes=[
             pltpu.VMEM((count, rows, width), bf16),
             pltpu.VMEM((count, rows, width), bf16),
             pltpu.VMEM((shards * own_rows, columns), bf16),
-            pltpu.VMEM((count, pairs, 2 * slots, PAIR), bf16),
+            pltpu.VMEM((pairs, count * 2 * slots, PAIR), bf16),
             pltpu.VMEM((count, rows, 1), f32),
             pltpu.VMEM((count, rows, 1), f32),
             pltpu.VMEM((count, rows, hidden), bf16),
@@ -1459,7 +1463,7 @@
             pltpu.VMEM((shards * own_rows, columns), bf16),
             dma((2,)),
             dma((2,)),
-            dma((shards,)),
+            dma((shards, 2)),
             dma((2,)),
             dma((2,)),
             dma((shards,)),
@@ -1468,7 +1472,336 @@
         cost_estimate=pl.CostEstimate(
             flops=flops, bytes_accessed=60 * 1024 * 1024, transcendentals=rows * hidden
         ),
-    )(ids, routes, router, n_all, c_all, owned)
+    )(ids, routes, router, n_all, c_all, owned, owned_cut)
+
+
+def turned_lanes(values, cosine, sine):
+    lane = lax.broadcasted_iota(jnp.int32, values.shape, 1)
+    half = HEAD_SIZE // 2
+    other = jnp.where(
+        lane % HEAD_SIZE < half,
+        pltpu.roll(values, LANES - half, 1),
+        pltpu.roll(values, half, 1),
+    )
+    return values * cosine + other * sine
+
+
+def causal(rows, columns, first_row):
+    row = lax.broadcasted_iota(jnp.int32, (rows, columns), 0) + first_row
+    return lax.broadcasted_iota(jnp.int32, (rows, columns), 1) <= row
+
+
+NT = (((1,), (1,)), ((), ()))
+TN = (((0,), (0,)), ((), ()))
+
+
+def product(a, b, dims):
+    return lax.dot_general(a, b, dims, preferred_element_type=jnp.float32)
+
+
+def front_body(shards, groups, plans, sizes, *refs):
+    x, small, routes, w_output, cosine, sine, qkv_cut, experts_cut = refs[:8]
+    small_all, routes_all, qkv_own, piece, normed, turned, log_sums, mixed, attended = refs[8:17]
+    x_all, parts = refs[17:19]
+    scratch = cut_refs(refs[19:], sizes)
+    f32, bf16 = jnp.float32, jnp.bfloat16
+    at = Place(shards, groups)
+    at.greet(True, True)
+    gathers = [
+        Gather(at, False, x, x_all, *scratch[0]),
+        Gather(at, False, small, small_all, *scratch[1]),
+        Gather(at, True, routes, routes_all, *scratch[2]),
+    ]
+    qkv_move = Exchange(at, plans[0], qkv_cut, qkv_own, *scratch[3])
+    piece_move = Exchange(at, plans[1], experts_cut, piece, *scratch[4])
+    sums = [
+        Reduce(at, False, parts.at[pl.ds(j, 1)], attended.at[pl.ds(j, 1)], *scratch[5 + j])
+        for j in range(2)
+    ]
+    marks = range(len(gathers[0].events))
+    for k in marks:
+        for g in gathers:
+            g.lines(k)
+        if k == 0:
+            qkv_move.start()
+    piece_move.start()
+    for step in (Gather.sides, Gather.turns, Gather.finish):
+        for k in marks:
+            for g in gathers:
+                step(g, k)
+    qkv_move.wait()
+
+    width = x.shape[2]
+    length = shards * DEVICE_TOKENS
+    tile = 256
+    at_lane = lax.broadcasted_iota(jnp.int32, (16, LANES), 1)
+    at_row = lax.broadcasted_iota(jnp.int32, (16, LANES), 0)
+    one_hot = ((at_lane == E) & (at_row == 0)).astype(bf16)
+    gain = product(one_hot, small_all[0].reshape(width, LANES), NT)[0:1]
+    per = length // tile
+
+    def project(t, _):
+        j, i = t // per, t % per
+        count = tile // DEVICE_TOKENS
+        rows = x_all[j, pl.ds(i * count, count)].reshape(tile, width).astype(f32)
+        rate = lax.rsqrt(jnp.mean(rows * rows, axis=-1, keepdims=True) + EPSILON)
+        n = (rows * rate * gain).astype(bf16)
+        here = pl.ds(pl.multiple_of(i * tile, tile), tile)
+        normed[j, here] = n
+        qkv = jnp.dot(n, qkv_own[...].reshape(width, -1), preferred_element_type=f32)
+        for lanes in (0, LANES):
+            turned[j, here, lanes : lanes + LANES] = turned_lanes(
+                qkv[:, lanes : lanes + LANES], cosine[here], sine[here]
+            ).astype(bf16)
+        turned[j, here, 2 * LANES :] = qkv[:, 2 * LANES :].astype(bf16)
+        return 0
+
+    lax.fori_loop(0, 2 * per, project, 0)
+    ratio = QUERY_HEADS // KEY_VALUE_HEADS
+    scale = 1.0 / HEAD_SIZE
+    for j in range(2):
+        key = turned[j, :, ratio * HEAD_SIZE : (ratio + 1) * HEAD_SIZE]
+        value = turned[j, :, (ratio + 1) * HEAD_SIZE :]
+        for i in range(per):
+            here = slice(i * tile, (i + 1) * tile)
+            seen = (i + 1) * tile
+            outs, logs = [], []
+            for h in range(ratio):
+                query = turned[j, here, h * HEAD_SIZE : (h + 1) * HEAD_SIZE]
+                scores = product(query, key[:seen], NT) * scale
+                scores = jnp.where(causal(tile, seen, i * tile), scores, MASKED)
+                top = jnp.max(scores, axis=-1, keepdims=True)
+                raised = jnp.exp(scores - top)
+                total = jnp.sum(raised, axis=-1, keepdims=True)
+                logs.append(top + jnp.log(total))
+                probs = (raised * (1.0 / total)).astype(bf16)
+                outs.append(jnp.dot(probs, value[:seen], preferred_element_type=f32))
+            mixed[j, here] = jnp.concatenate(outs, axis=1).astype(bf16)
+            for h in range(ratio):
+                log_sums[j, here, h : h + 1] = logs[h]
+            out = jnp.dot(mixed[j, here], w_output[...], preferred_element_type=f32).astype(bf16)
+            count = tile // DEVICE_TOKENS
+            parts[j, i * count : (i + 1) * count] = out.reshape(count, DEVICE_TOKENS, width)
+        sums[j].begin()
+    for q in sums[0].order:
+        for s in sums:
+            s.lines(q)
+    for s in sums:
+        s.finish()
+    piece_move.wait()
+
+
+def front(x, small, routes, w_output, cosine, sine, qkv_cut, experts_cut, shards, groups, plans):
+    f32, bf16 = jnp.float32, jnp.bfloat16
+    sequences, rows, width = x.shape
+    length = shards * rows
+    block = jax.ShapeDtypeStruct((1, shards, rows, width), bf16)
+    scratch = [
+        Gather.scratch(x, False, shards),
+        Gather.scratch(small, False, shards),
+        Gather.scratch(routes, True, shards),
+        Exchange.scratch(plans[0].block, bf16, plans[0].count, shards),
+        Exchange.scratch(plans[1].block, bf16, plans[1].count, shards),
+        Reduce.scratch(block, False, shards),
+        Reduce.scratch(block, False, shards),
+    ]
+    any_space, vmem = pl.BlockSpec(memory_space=pl.ANY), pl.BlockSpec(memory_space=pltpu.VMEM)
+    columns = qkv_cut.shape[2]
+    queries = w_output.shape[0]
+    return pl.pallas_call(
+        functools.partial(
+            front_body, shards, groups, tuple(plans), tuple(len(s) for s in scratch)
+        ),
+        out_shape=[
+            jax.ShapeDtypeStruct((1, shards) + small.shape[1:], bf16),
+            jax.ShapeDtypeStruct((1, shards * groups) + routes.shape[1:], routes.dtype),
+            jax.ShapeDtypeStruct(plans[0].shape, bf16),
+            jax.ShapeDtypeStruct(plans[1].shape, bf16),
+            jax.ShapeDtypeStruct((sequences, length, width), bf16),
+            jax.ShapeDtypeStruct((sequences, length, columns), bf16),
+            jax.ShapeDtypeStruct((sequences, length, LANES), f32),
+            jax.ShapeDtypeStruct((sequences, length, queries), bf16),
+            jax.ShapeDtypeStruct((sequences, rows, width), f32),
+        ],
+        in_specs=[vmem] * 6 + [any_space] * 2,
+        out_specs=[vmem, any_space, vmem, any_space, vmem, vmem, vmem, vmem, vmem],
+        scratch_shapes=[
+            pltpu.VMEM((sequences, shards, rows, width), bf16),
+            pltpu.VMEM((sequences, shards, rows, width), bf16),
+        ]
+        + [s for some in scratch for s in some],
+        compiler_params=pltpu.CompilerParams(
+            collective_id=0, has_side_effects=True, vmem_limit_bytes=60 * 1024 * 1024
+        ),
+        cost_estimate=pl.CostEstimate(
+            flops=4 * 10**9, bytes_accessed=100 * 10**6, transcendentals=3 * 10**6
+        ),
+    )(x, small, routes, w_output, cosine, sine, qkv_cut, experts_cut)
+
+
+def rear_body(shards, groups, plans, sizes, *refs):
+    dh, w_output, normed, qkv_own, turned, log_sums, mixed, cosine, sine = refs[:9]
+    grad_small, grads, _ = refs[9:12]
+    d_normed, small_line, qkv_sum, small_sum, output_sum, experts_out = refs[12:18]
+    dh_all, parts, d_qkv, d_keys, d_values, grad_qkv, swapped, grad_output = refs[18:26]
+    scratch = cut_refs(refs[26:], sizes)
+    f32, bf16 = jnp.float32, jnp.bfloat16
+    at = Place(shards, groups)
+    at.greet(True, True, True)
+    gather = Gather(at, False, dh, dh_all, *scratch[0])
+    experts_move = Exchange(at, plans[0], grads, experts_out, *scratch[1])
+    qkv_move = Exchange(at, plans[1], grad_qkv, swapped, *scratch[2])
+    sums = [
+        Reduce(at, False, parts.at[pl.ds(j, 1)], d_normed.at[pl.ds(j, 1)], *scratch[3 + j])
+        for j in range(2)
+    ]
+    small = Reduce(at, False, grad_small, small_line, *scratch[5])
+    of_qkv = Across(at, swapped, qkv_sum, *scratch[6])
+    of_small = Across(at, small_line, small_sum, *scratch[7])
+    of_output = Across(at, grad_output, output_sum, *scratch[8])
+    small.begin()
+    marks = range(len(gather.events))
+    for k in marks:
+        gather.lines(k)
+    for q in small.order:
+        small.lines(q)
+    experts_move.start()
+    small.finish()
+    of_small.start()
+    for k in marks:
+        gather.finish(k)
+
+    width = dh.shape[2]
+    length = shards * DEVICE_TOKENS
+    tile = 256
+    ratio = QUERY_HEADS // KEY_VALUE_HEADS
+    scale = 1.0 / HEAD_SIZE
+    total = jnp.zeros((ratio * HEAD_SIZE, width), f32)
+    for j in range(2):
+        total = total + product(mixed[j], dh_all[j].reshape(length, width), TN)
+    grad_output[...] = total.astype(bf16).reshape(grad_output.shape)
+    of_output.start()
+    for j in range(2):
+        d_mixed = product(dh_all[j].reshape(length, width), w_output[...], NT).astype(bf16)
+        key = turned[j, :, ratio * HEAD_SIZE : (ratio + 1) * HEAD_SIZE]
+        value = turned[j, :, (ratio + 1) * HEAD_SIZE :]
+        d_keys[...] = jnp.zeros_like(d_keys)
+        d_values[...] = jnp.zeros_like(d_values)
+        d_queries = []
+        for i in range(length // tile):
+            here = slice(i * tile, (i + 1) * tile)
+            seen = (i + 1) * tile
+            row = []
+            for h in range(ratio):
+                head = slice(h * HEAD_SIZE, (h + 1) * HEAD_SIZE)
+                query = turned[j, here, head]
+                d_out = d_mixed[here, head]
+                scores = product(query, key[:seen], NT) * scale
+                scores = jnp.where(causal(tile, seen, i * tile), scores, MASKED)
+                probs = jnp.exp(scores - log_sums[j, here, h : h + 1])
+                delta = jnp.sum(
+                    d_out.astype(f32) * mixed[j, here, head].astype(f32), axis=-1, keepdims=True
+                )
+                d_scores = probs * (product(d_out, value[:seen], NT) - delta)
+                d_scores = d_scores.astype(bf16)
+                row.append(jnp.dot(d_scores, key[:seen], preferred_element_type=f32) * scale)
+                d_keys[:seen] = d_keys[:seen] + product(d_scores, query, TN) * scale
+                d_values[:seen] = d_values[:seen] + product(probs.astype(bf16), d_out, TN)
+            d_queries.append(jnp.concatenate(row, axis=1))
+        d_query = jnp.concatenate(d_queries, axis=0)
+        last = jnp.concatenate([d_query[:, LANES:], d_keys[...]], axis=1)
+        d_qkv[j, :, :LANES] = turned_lanes(d_query[:, :LANES], cosine[...], -sine[...]).astype(bf16)
+        d_qkv[j, :, LANES : 2 * LANES] = turned_lanes(last, cosine[...], -sine[...]).astype(bf16)
+        d_qkv[j, :, 2 * LANES :] = d_values[...].astype(bf16)
+        out = product(d_qkv[j], qkv_own[...].reshape(width, -1), NT).astype(bf16)
+        parts[j] = out.reshape(shards, DEVICE_TOKENS, width)
+        sums[j].begin()
+    cut = 2 * grad_qkv.shape[1]
+    for i in range(width // cut):
+        here = slice(i * cut, (i + 1) * cut)
+        value = product(normed[0, :, here], d_qkv[0], TN) + product(
+            normed[1, :, here], d_qkv[1], TN
+        )
+        grad_qkv[2 * i : 2 * i + 2] = value.astype(bf16).reshape(2, cut // 2, -1)
+    qkv_move.start()
+    order = sums[0].order
+    for step, q in enumerate(order):
+        for s in sums:
+            s.lines(q)
+        if step == min(1, len(order) - 1):
+            of_small.turn()
+            of_output.turn()
+        if step == min(2, len(order) - 1):
+            qkv_move.wait()
+            of_qkv.start()
+    for s in sums:
+        s.finish()
+    of_qkv.turn()
+    for s in (of_small, of_output, of_qkv):
+        s.wait()
+    experts_move.wait()
+
+
+def rear(
+    dh, w_output, normed, qkv_own, turned, log_sums, mixed, cosine, sine, grad_small, grads, held,
+    shards, groups, plan,
+):
+    f32, bf16 = jnp.float32, jnp.bfloat16
+    sequences, rows, width = dh.shape
+    length = shards * rows
+    queries = w_output.shape[0]
+    block = jax.ShapeDtypeStruct((1, shards, rows, width), bf16)
+    small_shape = grad_small.shape[:1] + grad_small.shape[2:]
+    output_shape = (groups, queries // groups, width)
+    qkv_plan = Rows(qkv_own)
+    scratch = [
+        Gather.scratch(dh, False, shards),
+        Exchange.scratch(plan.block, bf16, plan.count, shards),
+        Exchange.scratch(qkv_plan.block, bf16, qkv_plan.count, shards),
+        Reduce.scratch(block, False, shards),
+        Reduce.scratch(block, False, shards),
+        Reduce.scratch(grad_small, False, shards),
+        Across.scratch(qkv_own.shape, bf16),
+        Across.scratch(small_shape, f32),
+        Across.scratch(output_shape, bf16),
+    ]
+    any_space, vmem = pl.BlockSpec(memory_space=pl.ANY), pl.BlockSpec(memory_space=pltpu.VMEM)
+    return pl.pallas_call(
+        functools.partial(
+            rear_body, shards, groups, (plan, qkv_plan), tuple(len(s) for s in scratch)
+        ),
+        out_shape=[
+            jax.ShapeDtypeStruct(dh.shape, f32),
+            jax.ShapeDtypeStruct(small_shape, f32),
+            jax.ShapeDtypeStruct(qkv_own.shape, bf16),
+            jax.ShapeDtypeStruct(small_shape, f32),
+            jax.ShapeDtypeStruct(output_shape, bf16),
+            jax.ShapeDtypeStruct(held.shape, bf16),
+        ],
+        in_specs=[vmem] * 9 + [any_space] * 3,
+        out_specs=[vmem] * 2 + [any_space] * 4,
+        scratch_shapes=[
+            pltpu.VMEM((sequences, shards, rows, width), bf16),
+            pltpu.VMEM((sequences, shards, rows, width), bf16),
+            pltpu.VMEM(turned.shape, bf16),
+            pltpu.VMEM((length, HEAD_SIZE), f32),
+            pltpu.VMEM((length, HEAD_SIZE), f32),
+            pltpu.VMEM(qkv_own.shape, bf16),
+            pltpu.VMEM(qkv_own.shape, bf16),
+            pltpu.VMEM(output_shape, bf16),
+        ]
+        + [s for some in scratch for s in some],
+        input_output_aliases={11: 5},
+        compiler_params=pltpu.CompilerParams(
+            collective_id=5, has_side_effects=True, vmem_limit_bytes=64 * 1024 * 1024 - 65536
+        ),
+        cost_estimate=pl.CostEstimate(
+            flops=8 * 10**9, bytes_accessed=100 * 10**6, transcendentals=3 * 10**6
+        ),
+    )(
+        dh, w_output, normed, qkv_own, turned, log_sums, mixed, cosine, sine, grad_small, grads,
+        held,
+    )
 
 
 def local(
@@ -1485,7 +1818,6 @@
     w_experts,
 ):
     f32, bf16 = jnp.float32, jnp.bfloat16
-    both = ("expert", "shard")
     shards, groups = lax.axis_size("shard"), lax.axis_size("expert")
     shard, group = lax.axis_index("shard"), lax.axis_index("expert")
     tokens = inputs.shape[0]
@@ -1493,10 +1825,9 @@
     sequences = tokens // DEVICE_TOKENS
     length = shards * DEVICE_TOKENS
     experts_here = E // groups
-    heads = KEY_VALUE_HEADS // shards
+    blocks = groups * shards
     ratio = QUERY_HEADS // KEY_VALUE_HEADS
-    query_width, key_width = heads * ratio * HEAD_SIZE, heads * HEAD_SIZE
-    scale = 1.0 / HEAD_SIZE
+    query_width, key_width = ratio * HEAD_SIZE, HEAD_SIZE
 
     small = jnp.concatenate([w_router, attn_gain[:, None], moe_gain[:, None]], axis=1)
     small = jnp.pad(small, ((0, 0), (0, LANES - E - 2)))
@@ -1511,66 +1842,33 @@
         ),
         (1, 0, 2),
     )
-    group_inputs, small_all, routes_all, qkv_own = gathered(
-        [
-            inputs.reshape(sequences, DEVICE_TOKENS, MODEL_WIDTH),
-            small[None],
-            jnp.transpose(routes)[None],
-        ],
-        (False, False, True),
+    experts_cut = jnp.transpose(w_experts, (1, 0, 2))
+    cosine, sine = angle_tables(jnp.arange(length, dtype=f32))
+    twice = LANES // HEAD_SIZE
+    cosine = jnp.tile(cosine, (1, 2 * twice))
+    sine = jnp.tile(jnp.concatenate([-sine, sine], axis=1), (1, twice))
+    small_all, routes_all, qkv_own, cut_own, normed, turned, log_sums, mixed, attended = front(
+        inputs.reshape(sequences, DEVICE_TOKENS, MODEL_WIDTH),
+        small[None],
+        jnp.transpose(routes)[None],
+        w_output,
+        cosine,
+        sine,
+        qkv_cut,
+        experts_cut,
         shards,
         groups,
-        0,
-        [qkv_cut],
-        [Rows(qkv_cut)],
-    )
-    qkv_own = qkv_own.reshape(MODEL_WIDTH, query_width + 2 * key_width)
+        [Rows(qkv_cut), Experts(experts_cut, shards, experts_here, False, (0, 0), (0, 3))],
+    )
     small = small_all.reshape(MODEL_WIDTH, LANES)
     router_pad = jnp.where(jnp.arange(LANES) < E, small, 0)
     router, gain_one, gain_two = small[:, :E], small[:, E].astype(f32), small[:, E + 1].astype(f32)
-
-    group_wide = group_inputs.reshape(sequences * length, MODEL_WIDTH).astype(f32)
-    r_group = lax.rsqrt(jnp.mean(group_wide * group_wide, axis=-1, keepdims=True) + EPSILON)
-    z_group = group_wide * r_group
-    normed = (z_group * gain_one).astype(bf16)
-    qkv = jnp.dot(normed, qkv_own, preferred_element_type=f32)
-    cosine, sine = angle_tables(jnp.arange(length, dtype=f32))
-    q_shape = (sequences, length, heads, ratio, HEAD_SIZE)
-    k_shape = (sequences, length, heads, HEAD_SIZE)
-    query = rotated(
-        qkv[:, :query_width].reshape(q_shape),
-        cosine[:, None, None, :],
-        sine[:, None, None, :],
-    ).astype(bf16)
-    keys = rotated(
-        qkv[:, query_width : query_width + key_width].reshape(k_shape),
-        cosine[:, None, :],
-        sine[:, None, :],
-    ).astype(bf16)
-    values = qkv[:, query_width + key_width :].reshape(k_shape).astype(bf16)
-    places = jnp.arange(length, dtype=jnp.int32)
-    allowed = places[None, :] <= places[:, None]
-    scores = jnp.einsum("nqjgd,nkjd->njgqk", query, keys, preferred_element_type=f32) * scale
-    scores = jnp.where(allowed, scores, MASKED)
-    top = jnp.max(scores, axis=-1, keepdims=True)
-    log_total = top + jnp.log(jnp.sum(jnp.exp(scores - top), axis=-1, keepdims=True))
-    probs = jnp.exp(scores - log_total)
-    mixed = jnp.einsum(
-        "njgqk,nkjd->nqjgd", probs.astype(bf16), values, preferred_element_type=f32
-    ).astype(bf16)
-    mixed_rows = mixed.reshape(sequences * length, query_width)
-    projected = jnp.dot(mixed_rows, w_output, preferred_element_type=f32).astype(bf16)
-    line_shape = (sequences, shards, DEVICE_TOKENS, MODEL_WIDTH)
-    attended = reduced([projected.reshape(line_shape)], (False,), shards, groups, 1)[0]
-    attended = attended.reshape(tokens, MODEL_WIDTH)
     inputs_wide = inputs.astype(f32)
-    h_one = inputs_wide + attended
+    h_one = inputs_wide + attended.reshape(tokens, MODEL_WIDTH)
     r_two = lax.rsqrt(jnp.mean(h_one * h_one, axis=-1, keepdims=True) + EPSILON)
     z_two = h_one * r_two
     n_two = (z_two * gain_two).astype(bf16)
 
-    blocks = groups * shards
-    experts_cut = jnp.transpose(w_experts, (1, 0, 2))
     n_all, c_all, experts_own = gathered(
         [n_two[None], cotangent[None]],
         (True, True),
@@ -1578,18 +1876,14 @@
         groups,
         2,
         [experts_cut],
-        [Experts(experts_cut, shards, experts_here, False)],
-    )
-    c_all = c_all[0]
-    n_all = n_all[0]
-
+        [Experts(experts_cut, shards, experts_here, False, (0, 3), (0, 0))],
+    )
     whole, extra = divmod(experts_here, shards)
+    cuts = shards // extra
     owned = [(group * experts_here + shard * whole + i, i * 3 * FF, FF) for i in range(whole)]
-    if extra:
-        cuts = shards // extra
-        owned.append(
-            (group * experts_here + whole * shards + shard // cuts, whole * 3 * FF, FF // cuts)
-        )
+    owned.append(
+        (group * experts_here + whole * shards + shard // cuts, whole * 3 * FF, FF // cuts)
+    )
     slots = -(-CAP // 8) * 8
     routes_pairs = jnp.transpose(
         routes_all.reshape(blocks // 2, 2, TOP, tokens), (0, 2, 1, 3)
@@ -1598,9 +1892,10 @@
         jnp.stack([expert for expert, _, _ in owned]).astype(jnp.int32),
         routes_pairs,
         jnp.transpose(router_pad)[: -(-E // 16) * 16],
-        n_all,
-        c_all,
+        n_all[0],
+        c_all[0],
         experts_own,
+        cut_own,
         [(start, width) for _, start, width in owned],
         slots,
         2 * TOP,
@@ -1612,7 +1907,7 @@
         groups,
         3,
         [grads],
-        [Experts(grads, shards, experts_here, True, (0, 2))],
+        [Experts(grads, shards, experts_here, True, (0, 2), (0, 2))],
     )
     back = back[0]
     outputs = (h_one + moe_sum[0]).astype(bf16)
@@ -1625,107 +1920,75 @@
     d_chosen = weights * (d_weights - jnp.sum(weights * d_weights, axis=-1, keepdims=True))
     d_logits = jnp.sum(picks * d_chosen[:, :, None], axis=1).astype(bf16)
     grad_router = jnp.einsum("td,te->de", n_two, d_logits, preferred_element_type=f32)
-    d_n_two = jnp.einsum("te,de->td", d_logits, router, preferred_element_type=f32) + back[
-        :tokens
-    ]
+    d_n_two = jnp.einsum("te,de->td", d_logits, router, preferred_element_type=f32)
+    d_n_two = d_n_two + back[:tokens]
     grad_gain_two = jnp.sum(d_n_two * z_two, axis=0)
     dz_two = d_n_two * gain_two
     dh_one = cotangent.astype(f32) + r_two * (
         dz_two - z_two * jnp.mean(dz_two * z_two, axis=-1, keepdims=True)
     )
-
-    dh_group = gathered(
-        [dh_one.astype(bf16).reshape(sequences, DEVICE_TOKENS, MODEL_WIDTH)],
-        (False,),
+    grad_small = jnp.concatenate([grad_router, grad_gain_two[:, None]], axis=1).astype(bf16)
+    grad_small = jnp.pad(grad_small, ((0, 0), (0, LANES - E - 1)))
+    grad_small = jnp.transpose(
+        grad_small.reshape(shards, groups, own_rows // groups, LANES), (1, 0, 2, 3)
+    )
+    dh_rows = dh_one.astype(bf16).reshape(sequences, DEVICE_TOKENS, MODEL_WIDTH)
+    d_n_one, _, grad_qkv, grad_small, grad_output, grad_experts = rear(
+        dh_rows,
+        w_output,
+        normed,
+        qkv_own,
+        turned,
+        log_sums,
+        mixed,
+        cosine,
+        sine,
+        grad_small,
+        grads,
+        gate_up,
         shards,
         groups,
-        4,
-    )[0].reshape(sequences * length, MODEL_WIDTH)
-    grad_output = jnp.einsum("tk,td->kd", mixed_rows, dh_group, preferred_element_type=f32)
-    d_mixed = (
-        jnp.einsum("td,kd->tk", dh_group, w_output, preferred_element_type=f32)
-        .astype(bf16)
-        .reshape(q_shape)
-    )
-    delta = jnp.sum(d_mixed.astype(f32) * mixed.astype(f32), axis=-1)
-    delta = jnp.transpose(delta, (0, 2, 3, 1))[..., None]
-    d_probs = jnp.einsum("nqjgd,nkjd->njgqk", d_mixed, values, preferred_element_type=f32)
-    d_scores = (probs * (d_probs - delta)).astype(bf16)
-    d_query = jnp.einsum("njgqk,nkjd->nqjgd", d_scores, keys, preferred_element_type=f32) * scale
-    d_keys = jnp.einsum("njgqk,nqjgd->nkjd", d_scores, query, preferred_element_type=f32) * scale
-    d_values = jnp.einsum(
-        "njgqk,nqjgd->nkjd", probs.astype(bf16), d_mixed, preferred_element_type=f32
-    )
-    d_qkv = jnp.concatenate(
-        [
-            rotated(d_query, cosine[:, None, None, :], -sine[:, None, None, :])
-            .astype(bf16)
-            .reshape(sequences * length, query_width),
-            rotated(d_keys, cosine[:, None, :], -sine[:, None, :])
-            .astype(bf16)
-            .reshape(sequences * length, key_width),
-            d_values.astype(bf16).reshape(sequences * length, key_width),
-        ],
-        axis=1,
-    )
-    d_normed = jnp.einsum("tk,dk->td", d_qkv, qkv_own, preferred_element_type=f32)
-    grad_gain_one = jnp.sum(d_normed * z_group, axis=0)
-    grad_qkv = jnp.einsum("td,tk->dk", normed, d_qkv, preferred_element_type=f32)
-    grad_small = jnp.concatenate(
-        [grad_router, grad_gain_one[:, None], grad_gain_two[:, None]], axis=1
-    ).astype(bf16)
-    grad_small = jnp.pad(grad_small, ((0, 0), (0, LANES - E - 2)))
-    grad_qkv = grad_qkv.astype(bf16).reshape(shards, own_rows, -1)
-    d_n_one, _, _, down, grad_qkv, grad_small, grad_output = reduced(
-        [
-            d_normed.astype(bf16).reshape(line_shape),
-            jnp.transpose(
-                grad_small.reshape(shards, groups, own_rows // groups, LANES), (1, 0, 2, 3)
-            ),
-        ],
-        (False, False),
-        shards,
-        groups,
-        5,
-        [grad_qkv, grads],
-        [Rows(grad_qkv), Experts(grads, shards, experts_here, True, (2, 3))],
-        [("swap", 0), ("sum", 1), ("in", 0)],
-        [grad_output.astype(bf16).reshape(groups, own_rows // groups, MODEL_WIDTH)],
-    )
-    grad_experts = jnp.transpose(jnp.concatenate([gate_up, down], axis=2), (1, 0, 2)).astype(f32)
-    grad_output = grad_output.reshape(own_rows, MODEL_WIDTH)
+        Experts(grads, shards, experts_here, True, (2, 3), (2, 3)),
+    )
+    grad_output = grad_output.reshape(own_rows, MODEL_WIDTH).astype(f32)
     grad_small = grad_small.reshape(own_rows, LANES)
-    d_n_one = d_n_one.reshape(tokens, MODEL_WIDTH)
-    grad_small = grad_small.astype(f32)
+    grad_experts = jnp.transpose(grad_experts, (1, 0, 2)).astype(f32)
 
     def columns(start, width):
         part = jnp.transpose(grad_qkv[:, :, start : start + width], (1, 0, 2))
         return part.reshape(own_rows, shards * width).astype(f32)
 
+    grad_query = columns(0, query_width)
+    grad_key = columns(query_width, key_width)
+    grad_value = columns(query_width + key_width, key_width)
+    grad_gain_one = (
+        jnp.sum(grad_query * w_query.astype(f32), axis=1)
+        + jnp.sum(grad_key * key_matrix.astype(f32), axis=1)
+        + jnp.sum(grad_value * value_matrix.astype(f32), axis=1)
+    ) / attn_gain.astype(f32)
     r_one = lax.rsqrt(jnp.mean(inputs_wide * inputs_wide, axis=-1, keepdims=True) + EPSILON)
     z_one = inputs_wide * r_one
-    dz_one = d_n_one * gain_one
+    dz_one = d_n_one.reshape(tokens, MODEL_WIDTH) * gain_one
     grad_inputs = dh_one + r_one * (
         dz_one - z_one * jnp.mean(dz_one * z_one, axis=-1, keepdims=True)
     )
     return (
         outputs,
         grad_inputs,
+        grad_gain_one,
+        grad_query,
+        grad_key,
+        grad_value,
+        grad_output,
         grad_small[:, E],
-        columns(0, query_width),
-        columns(query_width, key_width),
-        columns(query_width + key_width, key_width),
-        grad_output.astype(f32),
-        grad_small[:, E + 1],
         grad_small[:, :E],
         grad_experts,
     )
 
 
 def solution(mesh):
-    fits = divides(mesh.shape["shard"], mesh.shape["expert"])
     return jax.shard_map(
-        local if fits else general,
+        local if fits(mesh.shape["shard"], mesh.shape["expert"]) else general,
         mesh=mesh,
         in_specs=(
             P(("expert", "shard"), None),

time: 803 us -> 747 us (0.930)
  matrix products: 35.1 us -> 2.92 us
  Pallas kernels: 698 us -> 687 us
  local copies, waits for them, and re-layouts: 25.1 us -> 15.6 us
    pallas_call x0 -> x2, Pallas kernels: none -> 287 us  [the longest x1 156 us: rear(): pl.pallas_call(functools.partial(rear_body, shards, groups, (plan, qkv_pl...]
    pallas_call x3 -> x1, Pallas kernels: 353 us -> 174 us  [reduced(): pl.pallas_call(functools.partial(reduce_body, shards, groups, tuple(wides...]
    pallas_call x3 -> x1, Pallas kernels: 272 us -> 158 us  [gathered(): pl.pallas_call(functools.partial(gather_body, shards, groups, tuple(wides...]
    dot_general x12 -> x0, matrix products: 31.7 us -> none  [the longest x1 5.01 us: local(): jnp.einsum('nqjgd,nkjd->njgqk', d_mixed, values, preferred_element_type=f32)]
where the time goes in v3:
time: 747 us; the launch traced here: 739 us
  Pallas kernels  687 us (92%)
  other arithmetic  31.3 us (4%)
  local copies, waits for them, and re-layouts  15.6 us (2%)
    pallas_call x1, Pallas kernels, reduced(): pl.pallas_call(functools.partial(reduce_body, shards, groups, tuple(wides...  174 us
    pallas_call x1, Pallas kernels, gathered(): pl.pallas_call(functools.partial(gather_body, shards, groups, tuple(wides...  158 us
    pallas_call x1, Pallas kernels, rear(): pl.pallas_call(functools.partial(rear_body, shards, groups, (plan, qkv_pl...  156 us
    pallas_call x1, Pallas kernels, front(): pl.pallas_call(functools.partial(front_body, shards, groups, tuple(plans)...  130 us
    pallas_call x1, Pallas kernels, experts(): pl.pallas_call(functools.partial(experts_body, (tuple(units), pairs, slot...  68.7 us

profile of v3, /device:TPU:10, one launch (start us, length us, event | category | flops | bytes accessed | tf_op | source)
XLA Modules:
  0.0 738.6 jit_solution(12693907978963115245)
XLA Ops:
  0.7 0.8 broadcast_in_dim.64
  1.5 0.7 broadcast_in_dim.63
  2.2 0.9 copy.82
  3.1 0.7 fusion.18.refs_1_
  4.2 0.8 copy.90.refs_4_.refs_7_
  5.1 0.8 copy.91.refs_5_.refs_8_
  8.8 1.4 maximum_bitcast_fusion.refs_6_
  10.3 130.4 %shard_map.186 = (bf16[1,8,192,128]{3,2,1,0:T(8,128)(2,1)}, s32[1,32,8,128]{3,2,1,0:T(8,128)}, bf16[8,192,320]{2,1,0:T(8,128)(2,1)}, bf16[8,192,1920]{2,1,0:T(8,...) custom-call(bf16[2,64,1536]{2,1,0:T(8,128)(2,1)} %bitcast.89, ...), custom_call_target="tpu_custom_call" | custom-call | flops 4000000000 | bytes 100000000 | tf_op jit(solution)/shard_map/pallas_call | solution.py:1611
  140.8 1.4 multiply_reduce_fusion.3
  142.8 1.0 convert_reduce_fusion
  145.4 0.9 fusion.30.refs_0_
  146.2 158.0 %shard_map.187 = (bf16[1,32,128,1536]{3,2,1,0:T(8,128)(2,1)}, bf16[1,32,128,1536]{3,2,1,0:T(8,128)(2,1)}, bf16[8,192,1920]{2,1,0:T(8,128)(2,1)}) custom-call(bf16[1,128,1536]{2,1,0:T(8,128)(2,1)} %fusion.30.refs_0_, bf16[1,128,1536]{2,1,0:T(8,128)(2,1)} %bitcast.90, bf16[10,192,1536]{2,1,0:T(8,128)(2,1)} %bitcast.86), custom_call_target="tpu_custom_call" | custom-call | bytes 621281280 | tf_op jit(solution)/shard_map/pallas_call | solution.py:1061
  304.3 68.7 %shard_map.188 = (bf16[32,128,1536]{2,1,0:T(8,128)(2,1)}, bf16[32,144,1536]{2,1,0:T(8,128)(2,1)}, bf16[8,192,1920]{2,1,0:T(8,128)(2,1)}) custom-call(s32[2]{0:T(128)} %pad_add_fusion.ids, s32[16,8,256]{2,1,0:T(8,128)} %bitcast.106, bf16[48,1536]{1,0:T(8,128)(2,1)} %slice.55.router, bf16[32,128,1536]{2,1,0:T(8,128)(2,1)} %bitcast.104, ...), custom_call_target="tpu_custom_call" | custom-call | flops 22649241600 | bytes 62914560 | tf_op jit(solution)/shard_map/pallas_call | solution.py:1439
  373.0 174.0 %shard_map.189 = (f32[1,144,1536]{2,1,0:T(8,128)}, f32[1,128,1536]{2,1,0:T(8,128)}, bf16[10,192,1536]{2,1,0:T(8,128)(2,1)}) custom-call(bf16[1,32,144,1536]{3,2,1,0:T(8,128)(2,1)} %bitcast.79, bf16[1,32,128,1536]{3,2,1,0:T(8,128)(2,1)} %bitcast.80, bf16[8,192,1920]{2,1,0:T(8,128)(2,1)} %get-tuple-element.42.refs_2_.refs_10_), custom_call_target="tpu_custom_call" | custom-call | bytes 652738560 | tf_op jit(solution)/shard_map/pallas_call | solution.py:1176
  547.0 1.4 multiply_convert_fusion
  548.4 1.3 fusion.9
  550.4 0.7 multiply_reduce_fusion.6
  551.2 0.7 subtract_multiply_fusion
  552.7 1.5 multiply_reduce_fusion.1
  554.2 1.0 fusion.25
  555.8 0.8 copy.110
  556.5 156.1 %shard_map.190 = (f32[2,64,1536]{2,1,0:T(8,128)}, f32[4,48,128]{2,1,0:T(8,128)}, bf16[8,192,320]{2,1,0:T(8,128)(2,1)}, f32[4,48,128]{2,1,0:T(8,128)}, bf16[4,48,...) custom-call(bf16[2,64,1536]{2,1,0:T(8,128)(2,1)} %bitcast.101, ...), custom_call_target="tpu_custom_call", output_to_operand_aliasing={{5}: (11, {})} | custom-call | flops 8000000000 | bytes 100000000 | tf_op jit(solution)/shard_map/pallas_call | solution.py:1769
  712.6 1.5 fusion.2
  714.2 3.6 fusion.5
  717.7 1.1 convert_bitcast_fusion.3
  719.4 0.9 copy.97
  720.9 1.7 multiply_reduce_fusion
  722.6 1.5 copy.98
  724.8 0.9 copy.104
  725.7 0.9 copy.105
  726.7 1.2 bitcast_convert_fusion
  729.3 8.8 %convert_bitcast_fusion = f32[192,10,1536]{2,0,1:T(8,128)} fusion(bf16[10,192,1536]{2,1,0:T(8,128)(2,1)} %get-tuple-element.55), kind=kLoop, calls=%fused_computation | loop fusion | flops 2949120 | bytes 17694720 | tf_op jit(solution)/shard_map/convert_element_type | solution.py:1955
  (85 shorter events, 10.6 us)
Async XLA Ops:
  0.6 5.3 copy-start.18
  0.7 6.4 copy-start.19
  2.2 5.9 copy-start.11
  6.1 0.7 copy-start.9
  7.2 0.7 copy-start.7
  10.3 130.5 %copy-start.5 = (bf16[128,1536]{1,0:T(8,128)(2,1)S(1)}, bf16[128,1536]{1,0:T(8,128)(2,1)}, u32[]{:S(2)}) copy-start(bf16[128,1536]{1,0:T(8,128)(2,1)} %param.11) | copy-start | bytes 1179652
  140.7 2.0 copy-start.2
  142.2 162.1 %copy-start = (f32[128,1536]{1,0:T(8,128)}, f32[128,1536]{1,0:T(8,128)S(1)}, u32[]{:S(2)}) copy-start(f32[128,1536]{1,0:T(8,128)S(1)} %get-tuple-element.91) | copy-start | bytes 2359300
  142.8 161.5 %copy-start.20 = (f32[128]{0:T(128)}, f32[128]{0:T(128)S(1)}, u32[]{:S(2)}) copy-start(f32[128]{0:T(128)S(1)} %get-tuple-element.102) | copy-start | bytes 1540
  143.8 160.5 %copy-start.16 = (f32[1536]{0:T(1024)}, f32[1536]{0:T(1024)S(1)}, u32[]{:S(2)}) copy-start(f32[1536]{0:T(1024)S(1)} %get-tuple-element.89) | copy-start | bytes 18436
  546.9 5.7 copy-start.1
  546.9 5.7 copy-start.13
  546.9 7.2 copy-start.6
  547.0 7.2 copy-start.17
  547.0 7.2 copy-start.21
  554.1 1.1 copy-start.3
  554.2 2.4 copy-start.22
  714.1 3.6 copy-start.12
  717.7 1.4 copy-start.10
  720.3 3.8 copy-start.8
  720.9 4.9 copy-start.4
  720.9 3.4 copy-start.23
  722.6 4.1 copy-start.14
  724.1 3.7 copy-start.15

commit v4 on v3

--- a/solution.py
+++ b/solution.py
@@ -563,15 +563,14 @@
 
 
 class Experts:
-    def __init__(self, array, shards, experts_here, back, thirds=(0, 3), cut_thirds=(0, 3)):
-        self.back, self.thirds, self.cut_thirds = back, thirds, cut_thirds
+    def __init__(self, shape, shards, experts_here, back, sixths, shared):
+        self.back, self.sixths = back, sixths
+        self.cut_thirds = (0, 3) if shared else (0, 0)
         self.whole, self.extra = divmod(experts_here, shards)
         self.shards = shards
         self.cuts = shards // self.extra if self.extra else 1
         self.width = FF // self.cuts
-        if not self.extra:
-            self.cut_thirds = (0, 0)
-        rows = array.shape[1]
+        rows = shape[1]
         held = 3 * (FF * self.whole + (self.width if self.extra else 0))
         self.shape = (experts_here, rows, 3 * FF) if back else (shards, rows, held)
         self.block = (rows, held)
@@ -580,9 +579,10 @@
 
     def owner_cuts(self):
         cuts = []
-        first, last = self.thirds
+        first, last = self.sixths
         for i in range(self.whole if last > first else 0):
-            cuts.append((i, pl.ds((3 * i + first) * FF, (last - first) * FF)))
+            start = 3 * i * FF + first * FF // 2
+            cuts.append((i, pl.ds(start, (last - first) * FF // 2)))
         start = self.whole * 3 * FF
         for k in range(*self.cut_thirds):
             cuts.append((k, pl.ds(start + k * self.width, self.width)))
@@ -593,11 +593,10 @@
 
     def outside(self, i):
         cuts = []
-        first, last = self.thirds
+        first, last = self.sixths
         for k in range(self.whole if last > first else 0):
-            cuts.append(
-                (i * self.whole + k, slice(None), pl.ds(first * FF, (last - first) * FF))
-            )
+            here = pl.ds(first * FF // 2, (last - first) * FF // 2)
+            cuts.append((i * self.whole + k, slice(None), here))
         for k in range(*self.cut_thirds):
             expert = self.whole * self.shards + i // self.cuts
             start = pl.multiple_of(k * FF + i % self.cuts * self.width, 128)
@@ -611,75 +610,83 @@
         return self.outside(me) if self.back else self.owner(me)
 
 
+def quarter(ref, group, size, axis):
+    here = pl.ds(pl.multiple_of(group * size, 16) if axis else group * size, size)
+    return ref.at[:, here] if axis else ref.at[here]
+
+
+class Spread:
+    @staticmethod
+    def scratch():
+        return [pltpu.SemaphoreType.DMA((4,)), pltpu.SemaphoreType.DMA((4,))]
+
+    def __init__(self, at, source, target, axis, out, come):
+        self.at, self.source, self.out, self.come = at, source, out, come
+        self.target = quarter(target, at.group, source.shape[axis], axis)
+
+    def copies(self):
+        at = self.at
+        for i, peer in ((3, at.corner), (1, at.first), (2, at.second)):
+            yield sent(
+                self.source, self.target, self.out.at[i], self.come.at[i], peer, at.shard
+            )
+
+    def own(self):
+        return pltpu.make_async_copy(self.source, self.target, self.come.at[0])
+
+    def start(self):
+        self.own().start()
+        for copy in self.copies():
+            copy.start()
+
+    def wait(self):
+        self.own().wait()
+        for copy in self.copies():
+            copy.wait()
+
+
 class Across:
     @staticmethod
-    def scratch(shape, dtype):
-        block = (shape[0] // 4,) + shape[1:]
+    def scratch(shape, dtype, axis=0):
+        block = shape[:axis] + (shape[axis] // 4,) + shape[axis + 1 :]
         dma = pltpu.SemaphoreType.DMA
-        return [pltpu.VMEM((4,) + block, dtype), pltpu.VMEM(block, dtype)] + [
-            dma((4,)) for _ in range(4)
-        ]
-
-    def __init__(self, at, source, target, held, mine, r_out, r_in, g_out, g_in):
-        self.at, self.source, self.target, self.held, self.mine = at, source, target, held, mine
-        self.r_out, self.r_in, self.g_out, self.g_in = r_out, r_in, g_out, g_in
-        self.size = mine.shape[0]
-
-    def part(self, ref, group):
-        return ref.at[pl.ds(group * self.size, self.size)]
-
-    def peer(self, i):
-        return (self.at.first, self.at.second, self.at.corner)[i - 1]
-
-    def out(self, i):
-        return sent(
-            self.part(self.source, self.peer(i)),
-            self.held.at[i],
-            self.r_out.at[i],
-            self.r_in.at[i],
-            self.peer(i),
-            self.at.shard,
-        )
-
-    def back(self, i):
-        return sent(
-            self.mine,
-            self.part(self.target, self.at.group),
-            self.g_out.at[i],
-            self.g_in.at[i],
-            self.peer(i),
-            self.at.shard,
-        )
-
-    def own(self, way):
-        if way == 0:
-            here = self.part(self.source, self.at.group)
-            return pltpu.make_async_copy(here, self.held.at[0], self.r_in.at[0])
-        here = self.part(self.target, self.at.group)
-        return pltpu.make_async_copy(self.mine, here, self.g_in.at[0])
+        return [pltpu.VMEM((4,) + block, dtype), pltpu.VMEM(block, dtype), dma((4,)), dma((4,))]
+
+    def __init__(self, at, source, axis, held, mine, out, come):
+        self.at, self.source, self.axis, self.held, self.mine = at, source, axis, held, mine
+        self.out, self.come = out, come
+
+    def part(self, group):
+        return quarter(self.source, group, self.mine.shape[self.axis], self.axis)
+
+    def copies(self):
+        at = self.at
+        for i, peer in ((3, at.corner), (1, at.first), (2, at.second)):
+            yield sent(
+                self.part(peer),
+                self.held.at[i],
+                self.out.at[i],
+                self.come.at[i],
+                peer,
+                at.shard,
+            )
+
+    def own(self):
+        return pltpu.make_async_copy(self.part(self.at.group), self.held.at[0], self.come.at[0])
 
     def start(self):
-        self.own(0).start()
-        for i in (3, 1, 2):
-            self.out(i).start()
-
-    def turn(self):
-        self.own(0).wait()
-        for i in range(1, 4):
-            self.out(i).wait_recv()
+        self.own().start()
+        for copy in self.copies():
+            copy.start()
+
+    def add(self):
+        self.own().wait()
+        for copy in self.copies():
+            copy.wait()
         total = self.held[0].astype(jnp.float32)
         for i in range(1, 4):
             total = total + self.held[i].astype(jnp.float32)
         self.mine[...] = total.astype(self.mine.dtype)
-        self.own(1).start()
-        for i in (3, 1, 2):
-            self.back(i).start()
-
-    def wait(self):
-        self.own(1).wait()
-        for i in range(1, 4):
-            self.out(i).wait_send()
-            self.back(i).wait()
 
 
 class Gather:
@@ -1072,123 +1079,55 @@
     )(*arrays, *swapped)
 
 
-def halved(array, wide):
-    block = array.size // array.shape[1] * array.dtype.itemsize
-    return not wide and array.shape[0] == 2 and block > 200_000
-
-
-def reduce_body(shards, groups, wides, halves, plans, sums, sizes, *refs):
-    given = len(wides) + len(plans)
-    count = given + sum(1 for kind, _ in sums if kind == "in")
-    results = given + len(sums)
-    ins, outs = refs[:count], refs[count : count + results]
-    scratch = cut_refs(refs[count + results :], sizes)
+def reduce_body(shards, groups, wides, plans, sizes, *refs):
+    count = len(wides) + len(plans)
+    ins, outs = refs[:count], refs[count + len(plans) : 2 * count + len(plans)]
+    scratch = cut_refs(refs[2 * count + len(plans) :], sizes)
     at = Place(shards, groups)
-    at.greet(any(wides) or len(sums) > 0, len(plans) > 0, len(sums) > 0)
-    reductions = []
-    for i, wide in enumerate(wides):
-        if halves[i]:
-            for j in range(2):
-                half = pl.ds(j, 1)
-                reductions.append(
-                    Reduce(at, wide, ins[i].at[half], outs[i].at[half], *scratch.pop(0))
-                )
-        else:
-            reductions.append(Reduce(at, wide, ins[i], outs[i], *scratch.pop(0)))
+    at.greet(any(wides), len(plans) > 0)
+    sums = [Reduce(at, wide, ins[i], outs[i], *scratch[i]) for i, wide in enumerate(wides)]
     moves = [
-        Exchange(at, plan, ins[i], outs[i], *scratch.pop(0))
+        Exchange(at, plan, ins[i], outs[i], *scratch[i])
         for i, plan in enumerate(plans, len(wides))
     ]
-    totals = []
-    for i, (kind, which) in enumerate(sums, given):
-        source = {"in": ins, "sum": outs, "swap": outs}[kind]
-        source = source[which + (0 if kind == "sum" else given if kind == "in" else len(wides))]
-        totals.append(Across(at, source, outs[i], *scratch.pop(0)))
-    flat = [r for r in reductions if not r.wide]
-    wide_ones = [r for r in reductions if r.wide]
-    order = reductions[0].order
-    late = [i for i in range(len(moves)) if flat and ("swap", i) not in sums]
-
-    def swapped_sums():
-        for (kind, which), s in zip(sums, totals):
-            if kind == "swap":
-                moves[which].wait()
-                s.start()
-
-    for r in reductions:
+    for r in sums:
         r.begin()
-    for i, m in enumerate(moves):
-        if i not in late:
-            m.start()
-    for (kind, _), s in zip(sums, totals):
-        if kind == "in":
-            s.start()
-    for r in wide_ones:
-        r.corners()
-    for step, q in enumerate(order):
-        for r in flat:
+    for m in moves:
+        m.start()
+    for r in sums:
+        if r.wide:
+            r.corners()
+    for r in sums:
+        if r.wide:
+            r.sides()
+        for q in r.order:
             r.lines(q)
-        if step == min(1, len(order) - 1):
-            for i in late:
-                moves[i].start()
-        if step == min(2, len(order) - 1):
-            swapped_sums()
-    for r in flat:
+    for r in sums:
         r.finish()
-    for (kind, _), s in zip(sums, totals):
-        if kind == "sum":
-            s.start()
-    for r in wide_ones:
-        r.sides()
-    for s in totals:
-        s.turn()
-    for r in wide_ones:
-        for q in order:
-            r.lines(q)
-    for r in wide_ones:
-        r.finish()
-    for s in totals:
-        s.wait()
-    for i, m in enumerate(moves):
-        if ("swap", i) not in sums:
-            m.wait()
-
-
-def reduced(arrays, wides, shards, groups, identity, swapped=(), plans=(), sums=(), terms=()):
+    for m in moves:
+        m.wait()
+
+
+def reduced(arrays, wides, shards, groups, identity, swapped=(), plans=(), held=()):
     shapes = [
         jax.ShapeDtypeStruct((a.shape[0],) + a.shape[2:], jnp.float32) for a in arrays
     ] + [jax.ShapeDtypeStruct(p.shape, a.dtype) for a, p in zip(swapped, plans)]
-    for kind, which in sums:
-        if kind == "in":
-            source = terms[which]
-        else:
-            source = shapes[which + (0 if kind == "sum" else len(arrays))]
-        shapes.append(jax.ShapeDtypeStruct(source.shape, source.dtype))
-    operands = (*arrays, *swapped, *terms)
+    operands = (*arrays, *swapped, *held)
     moved = sum(a.size * a.dtype.itemsize for a in operands)
-    halves = tuple(halved(a, wide) for a, wide in zip(arrays, wides))
-    scratch = []
-    for a, wide, half in zip(arrays, wides, halves):
-        block = jax.ShapeDtypeStruct((1,) + a.shape[1:] if half else a.shape, a.dtype)
-        scratch += [Reduce.scratch(block, wide, shards)] * (2 if half else 1)
+    scratch = [Reduce.scratch(a, wide, shards) for a, wide in zip(arrays, wides)]
     scratch += [Exchange.scratch(p.block, a.dtype, p.count, shards) for a, p in zip(swapped, plans)]
-    scratch += [Across.scratch(a.shape, a.dtype) for a in shapes[len(arrays) + len(swapped) :]]
     return pl.pallas_call(
         functools.partial(
-            reduce_body,
-            shards,
-            groups,
-            tuple(wides),
-            halves,
-            tuple(plans),
-            tuple(sums),
-            tuple(len(s) for s in scratch),
+            reduce_body, shards, groups, tuple(wides), tuple(plans), tuple(len(s) for s in scratch)
         ),
         out_shape=shapes,
         in_specs=[pl.BlockSpec(memory_space=pl.ANY)] * len(operands),
         out_specs=[pl.BlockSpec(memory_space=pltpu.VMEM)] * len(arrays)
-        + [pl.BlockSpec(memory_space=pl.ANY)] * (len(shapes) - len(arrays)),
+        + [pl.BlockSpec(memory_space=pl.ANY)] * len(swapped),
         scratch_shapes=[s for some in scratch for s in some],
+        input_output_aliases={
+            len(arrays) + len(swapped) + i: len(arrays) + i for i in range(len(held))
+        },
         compiler_params=pltpu.CompilerParams(
             collective_id=identity, has_side_effects=True, vmem_limit_bytes=64 * 1024 * 1024 - 65536
         ),
@@ -1200,67 +1139,42 @@
 TILE = 320
 
 
-def experts_body(
-    shape,
-    ids,
-    routes,
-    router,
-    n_from,
-    c_from,
-    w_from,
-    w_cut,
-    y_to,
-    d_to,
-    g_to,
-    rows_n,
-    rows_c,
-    weights,
-    picks,
-    slot_w,
-    slot_d,
-    act_rows,
-    gu_rows,
-    y_rows,
-    d_rows,
-    n_buf,
-    c_buf,
-    y_buf,
-    d_buf,
-    g_buf,
-    n_sem,
-    c_sem,
-    w_sem,
-    y_sem,
-    d_sem,
-    g_sem,
-):
+def experts_body(shards, groups, plans, shape, sizes, *refs):
+    ids, routes, router, n_block, c_from, w_cut, w_pieces = refs[:7]
+    n_from, y_to, d_to, g_to, g_back = refs[7:12]
+    rows_n, rows_c, weights, picks, slot_w, slot_d, act_rows, gu_rows, y_rows, d_rows = refs[12:22]
+    n_buf, c_buf, y_buf, d_buf, g_buf, n_sem, c_sem, w_sem, y_sem, d_sem, g_sem = refs[22:33]
+    scratch = cut_refs(refs[33:], sizes)
     units, pairs, slots, tokens, extra = shape
     f32, bf16 = jnp.float32, jnp.bfloat16
     whole = 2 * slots
-    chunk = weights.shape[0] // w_from.shape[0]
+    chunk = weights.shape[1]
+    width_all = n_block.shape[2]
+    at = Place(shards, groups)
+    at.greet(True, True)
+    gather = Gather(at, True, n_block, n_from, *scratch[0])
+    bring_weights = Exchange(at, plans[0], w_pieces, weights, *scratch[1])
+    back_cut = Exchange(at, plans[1], g_buf, g_back, *scratch[2])
 
     def bring(p, slot):
         return (
-            pltpu.make_async_copy(n_from.at[pl.ds(2 * p, 2)], n_buf.at[slot], n_sem.at[slot]),
-            pltpu.make_async_copy(c_from.at[pl.ds(2 * p, 2)], c_buf.at[slot], c_sem.at[slot]),
+            pltpu.make_async_copy(n_from.at[0, pl.ds(2 * p, 2)], n_buf.at[slot], n_sem.at[slot]),
+            pltpu.make_async_copy(c_from.at[0, pl.ds(2 * p, 2)], c_buf.at[slot], c_sem.at[slot]),
         )
 
     split = units[-1][0]
-
-    def weight_copies(i):
-        here = pl.ds(i * chunk, chunk)
-        for k, (source, cut) in enumerate(
-            ((w_from, pl.ds(0, split)), (w_cut, pl.ds(split, weights.shape[1] - split)))
-        ):
-            yield pltpu.make_async_copy(
-                source.at[i, :, cut], weights.at[here, cut], w_sem.at[i, k]
-            )
-
+    cut = pl.ds(split, weights.shape[2] - split)
+    cut_copy = pltpu.make_async_copy(w_cut.at[:, :, cut], weights.at[:, :, cut], w_sem.at[0])
+    cut_copy.start()
+    marks = range(len(gather.events))
+    for k in marks:
+        gather.lines(k)
+    bring_weights.start()
+    for step in (Gather.sides, Gather.turns, Gather.finish):
+        for k in marks:
+            step(gather, k)
     for copy in bring(0, 0):
         copy.start()
-    for i in range(w_from.shape[0]):
-        for copy in weight_copies(i):
-            copy.start()
     row = lax.broadcasted_iota(jnp.int32, (PAIR, PAIR), 0)
     column = lax.broadcasted_iota(jnp.int32, (PAIR, PAIR), 1)
     upto = ((row <= column) & (row // tokens == column // tokens)).astype(bf16)
@@ -1310,74 +1224,87 @@
                 -1,
             )
             pick = (places == place).astype(f32)
-            at = pl.ds(pl.multiple_of(p * whole, 16), whole)
-            slot_w[u, at] = jnp.sum(pick * weight, axis=1, keepdims=True)
+            here = pl.ds(pl.multiple_of(p * whole, 16), whole)
+            slot_w[u, here] = jnp.sum(pick * weight, axis=1, keepdims=True)
             picks[p, u * whole : (u + 1) * whole] = pick.astype(bf16)
-        at = pl.ds(pl.multiple_of(p * whole, 16), whole)
+        here = pl.ds(pl.multiple_of(p * whole, 16), whole)
         sent_n = jnp.dot(picks[p], n, preferred_element_type=f32).astype(bf16)
         sent_c = jnp.dot(picks[p], c, preferred_element_type=f32).astype(bf16)
         for u in range(len(units)):
-            rows_n[u, at] = sent_n[u * whole : (u + 1) * whole]
-            rows_c[u, at] = sent_c[u * whole : (u + 1) * whole]
+            rows_n[u, here] = sent_n[u * whole : (u + 1) * whole]
+            rows_c[u, here] = sent_c[u * whole : (u + 1) * whole]
         return 0
 
     lax.fori_loop(0, pairs, dispatch, 0)
-    for i in range(w_from.shape[0]):
-        for copy in weight_copies(i):
-            copy.wait()
     turned = (((1,), (1,)), ((), ()))
     summed = (((0,), (0,)), ((), ()))
-    for u, (start, width) in enumerate(units):
-        gu = pl.ds(start, 2 * width)
-        down = pl.ds(start + 2 * width, width)
-
-        def tile(i, _, u=u, start=start, width=width, gu=gu, down=down):
-            at = pl.ds(pl.multiple_of(i * TILE, 16), TILE)
-            parts = jnp.dot(rows_n[u, at], weights[:, gu], preferred_element_type=f32)
-            plain = jnp.dot(rows_c[u, at], weights[:, down], preferred_element_type=f32)
+    deep = 2 * chunk
+
+    def columns(start, width):
+        return weights[:, :, pl.ds(start, width)].reshape(width_all, width)
+
+    def products(u):
+        start, width = units[u]
+        first = start // 3
+        held_a, held_g = pl.ds(first, width), pl.ds(2 * first, 2 * width)
+
+        def tile(i, _):
+            here = pl.ds(pl.multiple_of(i * TILE, 16), TILE)
+            parts = jnp.dot(rows_n[u, here], columns(start, 2 * width), preferred_element_type=f32)
+            down = columns(start + 2 * width, width)
+            plain = jnp.dot(rows_c[u, here], down, preferred_element_type=f32)
             gate, up = parts[:, :width], parts[:, width:]
             sig = jax.nn.sigmoid(gate)
             act = gate * sig * up
-            w = slot_w[u, at]
-            slot_d[u, at] = jnp.sum(act * plain, axis=1, keepdims=True)
+            w = slot_w[u, here]
+            slot_d[u, here] = jnp.sum(act * plain, axis=1, keepdims=True)
             act_w = (act * w).astype(bf16)
             da = plain * w
             d_gate = (da * up * sig * (1.0 + gate * (1.0 - sig))).astype(bf16)
             d_up = (da * gate * sig).astype(bf16)
-            act_rows[u, at, :width] = act_w
-            gu_rows[u, at, :width] = d_gate
-            gu_rows[u, at, width : 2 * width] = d_up
-            y_rows[u, at] = lax.dot_general(
-                act_w, weights[:, down], turned, preferred_element_type=f32
+            act_rows[here, held_a] = act_w
+            gu_rows[here, pl.ds(2 * first, width)] = d_gate
+            gu_rows[here, pl.ds(2 * first + width, width)] = d_up
+            y_rows[u, here] = lax.dot_general(
+                act_w, down, turned, preferred_element_type=f32
             ).astype(bf16)
-            d_rows[u, at] = lax.dot_general(
-                gu_rows[u, at, : 2 * width], weights[:, gu], turned, preferred_element_type=f32
+            d_rows[u, here] = lax.dot_general(
+                gu_rows[here, held_g],
+                columns(start, 2 * width),
+                turned,
+                preferred_element_type=f32,
             ).astype(bf16)
             return 0
 
         lax.fori_loop(0, pairs * whole // TILE, tile, 0)
 
-    deep = 256
-
-    def grad_copy(i):
-        return pltpu.make_async_copy(
-            g_buf.at[pl.ds(i * chunk, chunk)], g_to.at[i], g_sem.at[i]
-        )
-
-    def grads(i, _):
-        at = pl.ds(pl.multiple_of(i * deep, deep), deep)
-        for u, (start, width) in enumerate(units):
-            g_buf[at, start : start + 2 * width] = lax.dot_general(
-                rows_n[u, :, at], gu_rows[u, :, : 2 * width], summed, preferred_element_type=f32
-            ).astype(bf16)
-            g_buf[at, start + 2 * width : start + 3 * width] = lax.dot_general(
-                rows_c[u, :, at], act_rows[u, :, :width], summed, preferred_element_type=f32
-            ).astype(bf16)
-        return 0
-
-    lax.fori_loop(0, weights.shape[0] // deep, grads, 0)
-    for i in range(g_to.shape[0]):
-        grad_copy(i).start()
+        def grads(i, _):
+            here = pl.ds(pl.multiple_of(i * deep, deep), deep)
+            value = lax.dot_general(
+                rows_n[u, :, here], gu_rows[:, held_g], summed, preferred_element_type=f32
+            )
+            g_buf[pl.ds(2 * i, 2), :, pl.ds(start, 2 * width)] = value.astype(bf16).reshape(
+                2, chunk, 2 * width
+            )
+            value = lax.dot_general(
+                rows_c[u, :, here], act_rows[:, held_a], summed, preferred_element_type=f32
+            )
+            g_buf[pl.ds(2 * i, 2), :, pl.ds(start + 2 * width, width)] = value.astype(
+                bf16
+            ).reshape(2, chunk, width)
+            return 0
+
+        lax.fori_loop(0, width_all // deep, grads, 0)
+
+    cut_copy.wait()
+    products(len(units) - 1)
+    back_cut.start()
+    bring_weights.wait()
+    for u in range(len(units) - 1):
+        products(u)
+    rest = pl.ds(0, split)
+    g_copy = pltpu.make_async_copy(g_buf.at[:, :, rest], g_to.at[:, :, rest], g_sem.at[0])
+    g_copy.start()
 
     def put(p, slot):
         return (
@@ -1395,16 +1322,16 @@
             for copy in put(p - 2, slot):
                 copy.wait()
 
-        at = pl.ds(pl.multiple_of(p * whole, 16), whole)
+        here = pl.ds(pl.multiple_of(p * whole, 16), whole)
         pick = picks[p]
-        both = [y_rows[u, at] for u in range(len(units))]
+        both = [y_rows[u, here] for u in range(len(units))]
         y = lax.dot_general(pick, jnp.concatenate(both), summed, preferred_element_type=f32)
-        both = [d_rows[u, at] for u in range(len(units))]
+        both = [d_rows[u, here] for u in range(len(units))]
         d = lax.dot_general(pick, jnp.concatenate(both), summed, preferred_element_type=f32)
         d_w = jnp.zeros((TOP, PAIR), f32)
         for u in range(len(units)):
             pick = picks[p, u * whole : (u + 1) * whole]
-            back = jnp.sum(pick.astype(f32) * slot_d[u, at], axis=0, keepdims=True)
+            back = jnp.sum(pick.astype(f32) * slot_d[u, here], axis=0, keepdims=True)
             d_w = d_w + jnp.where(routes[p] == ids[u], back, 0.0)
         high = d_w.astype(bf16)
         low = (d_w - high.astype(f32)).astype(bf16)
@@ -1421,58 +1348,79 @@
     for p in range(pairs - 2, pairs):
         for copy in put(p, p % 2):
             copy.wait()
-    for i in range(g_to.shape[0]):
-        grad_copy(i).wait()
-
-
-def experts(ids, routes, router, n_all, c_all, owned, owned_cut, units, slots, extra):
-    blocks, tokens, width = n_all.shape
+    g_copy.wait()
+    back_cut.wait()
+
+
+def experts(
+    ids, routes, router, n_block, c_all, w_cut, w_pieces, units, slots, extra, shards, groups, plans
+):
+    _, tokens, width = n_block.shape
+    blocks = shards * groups
     pairs = blocks // 2
     rows = pairs * 2 * slots
     count = len(units)
-    hidden = max(w for _, w in units)
+    hidden = sum(w for _, w in units)
     bf16, f32 = jnp.bfloat16, jnp.float32
-    shards, own_rows, columns = owned.shape
+    owned = w_cut.shape
     dma = pltpu.SemaphoreType.DMA
     any_space, vmem = pl.BlockSpec(memory_space=pl.ANY), pl.BlockSpec(memory_space=pltpu.VMEM)
-    flops = 2 * rows * width * sum(w for _, w in units) * 9
+    scratch = [
+        Gather.scratch(n_block, True, shards),
+        Exchange.scratch(plans[0].block, bf16, plans[0].count, shards),
+        Exchange.scratch(plans[1].block, bf16, plans[1].count, shards),
+    ]
     return pl.pallas_call(
-        functools.partial(experts_body, (tuple(units), pairs, slots, tokens, extra)),
+        functools.partial(
+            experts_body,
+            shards,
+            groups,
+            tuple(plans),
+            (tuple(units), pairs, slots, tokens, extra),
+            tuple(len(s) for s in scratch),
+        ),
         out_shape=[
+            jax.ShapeDtypeStruct((1, blocks, tokens, width), bf16),
             jax.ShapeDtypeStruct((blocks, tokens, width), bf16),
             jax.ShapeDtypeStruct((blocks, tokens + extra, width), bf16),
-            jax.ShapeDtypeStruct(owned.shape, bf16),
+            jax.ShapeDtypeStruct(owned, bf16),
+            jax.ShapeDtypeStruct(plans[1].shape, bf16),
         ],
-        in_specs=[pl.BlockSpec(memory_space=pltpu.SMEM), vmem, vmem] + [any_space] * 4,
-        out_specs=[any_space] * 3,
+        in_specs=[pl.BlockSpec(memory_space=pltpu.SMEM)] + [vmem] * 3 + [any_space] * 3,
+        out_specs=[any_space] * 5,
         scratch_shapes=[
             pltpu.VMEM((count, rows, width), bf16),
             pltpu.VMEM((count, rows, width), bf16),
-            pltpu.VMEM((shards * own_rows, columns), bf16),
+            pltpu.VMEM(owned, bf16),
             pltpu.VMEM((pairs, count * 2 * slots, PAIR), bf16),
             pltpu.VMEM((count, rows, 1), f32),
             pltpu.VMEM((count, rows, 1), f32),
-            pltpu.VMEM((count, rows, hidden), bf16),
-            pltpu.VMEM((count, rows, 2 * hidden), bf16),
+            pltpu.VMEM((rows, hidden), bf16),
+            pltpu.VMEM((rows, 2 * hidden), bf16),
             pltpu.VMEM((count, rows, width), bf16),
             pltpu.VMEM((count, rows, width), bf16),
             pltpu.VMEM((2, 2, tokens, width), bf16),
             pltpu.VMEM((2, 2, tokens, width), bf16),
             pltpu.VMEM((2, 2, tokens, width), bf16),
             pltpu.VMEM((2, 2, tokens + extra, width), bf16),
-            pltpu.VMEM((shards * own_rows, columns), bf16),
+            pltpu.VMEM(owned, bf16),
             dma((2,)),
             dma((2,)),
-            dma((shards, 2)),
+            dma((1,)),
             dma((2,)),
             dma((2,)),
-            dma((shards,)),
-        ],
-        compiler_params=pltpu.CompilerParams(vmem_limit_bytes=67_000_000),
+            dma((1,)),
+        ]
+        + [s for some in scratch for s in some],
+        compiler_params=pltpu.CompilerParams(
+            collective_id=2, has_side_effects=True, vmem_limit_bytes=67_000_000
+        ),
         cost_estimate=pl.CostEstimate(
-            flops=flops, bytes_accessed=60 * 1024 * 1024, transcendentals=rows * hidden
+            flops=18 * rows * width * hidden,
+            bytes_accessed=200 * 1024 * 1024,
+            transcendentals=rows * hidden,
         ),
-    )(ids, routes, router, n_all, c_all, owned, owned_cut)
+    )(ids, routes, router, n_block, c_all, w_cut, w_pieces)
 
 
 def turned_lanes(values, cosine, sine):
@@ -1500,19 +1448,22 @@
 
 
 def front_body(shards, groups, plans, sizes, *refs):
-    x, small, routes, w_output, cosine, sine, qkv_cut, experts_cut = refs[:8]
-    small_all, routes_all, qkv_own, piece, normed, turned, log_sums, mixed, attended = refs[8:17]
-    x_all, parts = refs[17:19]
-    scratch = cut_refs(refs[19:], sizes)
+    x, small, routes, far, w_output, cosine, sine, qkv_cut, experts_cut = refs[:9]
+    small_all, routes_all, far_all, qkv_own, piece, normed, turned, log_sums, mixed = refs[9:18]
+    attended, x_all, parts, qkv_quarter = refs[18:22]
+    scratch = cut_refs(refs[22:], sizes)
     f32, bf16 = jnp.float32, jnp.bfloat16
     at = Place(shards, groups)
-    at.greet(True, True)
+    at.greet(True, True, True)
     gathers = [
         Gather(at, False, x, x_all, *scratch[0]),
         Gather(at, False, small, small_all, *scratch[1]),
         Gather(at, True, routes, routes_all, *scratch[2]),
     ]
-    qkv_move = Exchange(at, plans[0], qkv_cut, qkv_own, *scratch[3])
+    quarter_cut = quarter(qkv_cut, at.group, qkv_quarter.shape[1], 1)
+    qkv_move = Exchange(at, plans[0], quarter_cut, qkv_quarter, *scratch[3])
+    qkv_spread = Spread(at, qkv_quarter, qkv_own, 1, *scratch[7])
+    beside = Gather(at, True, far, far_all, *scratch[8])
     piece_move = Exchange(at, plans[1], experts_cut, piece, *scratch[4])
     sums = [
         Reduce(at, False, parts.at[pl.ds(j, 1)], attended.at[pl.ds(j, 1)], *scratch[5 + j])
@@ -1524,12 +1475,14 @@
             g.lines(k)
         if k == 0:
             qkv_move.start()
-    piece_move.start()
+    beside.lines(0)
+    qkv_move.wait()
+    qkv_spread.start()
     for step in (Gather.sides, Gather.turns, Gather.finish):
         for k in marks:
             for g in gathers:
                 step(g, k)
-    qkv_move.wait()
+    qkv_spread.wait()
 
     width = x.shape[2]
     length = shards * DEVICE_TOKENS
@@ -1540,13 +1493,13 @@
     gain = product(one_hot, small_all[0].reshape(width, LANES), NT)[0:1]
     per = length // tile
 
-    def project(t, _):
-        j, i = t // per, t % per
+    def project(t):
+        j, i = divmod(t, per)
         count = tile // DEVICE_TOKENS
-        rows = x_all[j, pl.ds(i * count, count)].reshape(tile, width).astype(f32)
+        rows = x_all[j, i * count : (i + 1) * count].reshape(tile, width).astype(f32)
         rate = lax.rsqrt(jnp.mean(rows * rows, axis=-1, keepdims=True) + EPSILON)
         n = (rows * rate * gain).astype(bf16)
-        here = pl.ds(pl.multiple_of(i * tile, tile), tile)
+        here = slice(i * tile, (i + 1) * tile)
         normed[j, here] = n
         qkv = jnp.dot(n, qkv_own[...].reshape(width, -1), preferred_element_type=f32)
         for lanes in (0, LANES):
@@ -1554,9 +1507,17 @@
                 qkv[:, lanes : lanes + LANES], cosine[here], sine[here]
             ).astype(bf16)
         turned[j, here, 2 * LANES :] = qkv[:, 2 * LANES :].astype(bf16)
-        return 0
-
-    lax.fori_loop(0, 2 * per, project, 0)
+
+    waiting = list(marks)[1:]
+    for t in range(2 * per):
+        project(t)
+        for k in waiting[:2]:
+            beside.lines(k)
+        waiting = waiting[2:]
+    for k in waiting:
+        beside.lines(k)
+    piece_move.start()
+    waiting = list(marks)
     ratio = QUERY_HEADS // KEY_VALUE_HEADS
     scale = 1.0 / HEAD_SIZE
     for j in range(2):
@@ -1582,19 +1543,33 @@
             out = jnp.dot(mixed[j, here], w_output[...], preferred_element_type=f32).astype(bf16)
             count = tile // DEVICE_TOKENS
             parts[j, i * count : (i + 1) * count] = out.reshape(count, DEVICE_TOKENS, width)
+            for k in waiting[:2]:
+                beside.sides(k)
+            waiting = waiting[2:]
         sums[j].begin()
+    for k in waiting:
+        beside.sides(k)
     for q in sums[0].order:
         for s in sums:
             s.lines(q)
+    for k in marks:
+        beside.turns(k)
     for s in sums:
         s.finish()
+    for k in marks:
+        beside.finish(k)
     piece_move.wait()
 
 
-def front(x, small, routes, w_output, cosine, sine, qkv_cut, experts_cut, shards, groups, plans):
+def front(
+    x, small, routes, far, w_output, cosine, sine, qkv_cut, experts_cut, shards, groups, plan
+):
     f32, bf16 = jnp.float32, jnp.bfloat16
     sequences, rows, width = x.shape
     length = shards * rows
+    own_rows, columns = qkv_cut.shape[1:]
+    quarter_shape = (shards, own_rows // groups, columns)
+    plans = (Rows(jax.ShapeDtypeStruct(quarter_shape, bf16)), plan)
     block = jax.ShapeDtypeStruct((1, shards, rows, width), bf16)
     scratch = [
         Gather.scratch(x, False, shards),
@@ -1604,30 +1579,33 @@
         Exchange.scratch(plans[1].block, bf16, plans[1].count, shards),
         Reduce.scratch(block, False, shards),
         Reduce.scratch(block, False, shards),
+        Spread.scratch(),
+        Gather.scratch(far, True, shards),
     ]
     any_space, vmem = pl.BlockSpec(memory_space=pl.ANY), pl.BlockSpec(memory_space=pltpu.VMEM)
-    columns = qkv_cut.shape[2]
     queries = w_output.shape[0]
     return pl.pallas_call(
         functools.partial(
-            front_body, shards, groups, tuple(plans), tuple(len(s) for s in scratch)
+            front_body, shards, groups, plans, tuple(len(s) for s in scratch)
         ),
         out_shape=[
             jax.ShapeDtypeStruct((1, shards) + small.shape[1:], bf16),
             jax.ShapeDtypeStruct((1, shards * groups) + routes.shape[1:], routes.dtype),
-            jax.ShapeDtypeStruct(plans[0].shape, bf16),
-            jax.ShapeDtypeStruct(plans[1].shape, bf16),
+            jax.ShapeDtypeStruct((1, shards * groups) + far.shape[1:], bf16),
+            jax.ShapeDtypeStruct(qkv_cut.shape, bf16),
+            jax.ShapeDtypeStruct(plan.shape, bf16),
             jax.ShapeDtypeStruct((sequences, length, width), bf16),
             jax.ShapeDtypeStruct((sequences, length, columns), bf16),
             jax.ShapeDtypeStruct((sequences, length, LANES), f32),
             jax.ShapeDtypeStruct((sequences, length, queries), bf16),
             jax.ShapeDtypeStruct((sequences, rows, width), f32),
         ],
-        in_specs=[vmem] * 6 + [any_space] * 2,
-        out_specs=[vmem, any_space, vmem, any_space, vmem, vmem, vmem, vmem, vmem],
+        in_specs=[vmem] * 7 + [any_space] * 2,
+        out_specs=[vmem, any_space, any_space, vmem, any_space, vmem, vmem, vmem, vmem, vmem],
         scratch_shapes=[
             pltpu.VMEM((sequences, shards, rows, width), bf16),
             pltpu.VMEM((sequences, shards, rows, width), bf16),
+            pltpu.VMEM(quarter_shape, bf16),
         ]
         + [s for some in scratch for s in some],
         compiler_params=pltpu.CompilerParams(
@@ -1636,7 +1614,7 @@
         cost_estimate=pl.CostEstimate(
             flops=4 * 10**9, bytes_accessed=100 * 10**6, transcendentals=3 * 10**6
         ),
-    )(x, small, routes, w_output, cosine, sine, qkv_cut, experts_cut)
+    )(x, small, routes, far, w_output, cosine, sine, qkv_cut, experts_cut)
 
 
 def rear_body(shards, groups, plans, sizes, *refs):
@@ -1649,23 +1627,31 @@
     at = Place(shards, groups)
     at.greet(True, True, True)
     gather = Gather(at, False, dh, dh_all, *scratch[0])
-    experts_move = Exchange(at, plans[0], grads, experts_out, *scratch[1])
-    qkv_move = Exchange(at, plans[1], grad_qkv, swapped, *scratch[2])
+    experts_moves = [
+        Exchange(at, plans[i], grads, experts_out, *scratch[(1, 12)[i]])
+        for i in range(len(plans) - 1)
+    ]
     sums = [
         Reduce(at, False, parts.at[pl.ds(j, 1)], d_normed.at[pl.ds(j, 1)], *scratch[3 + j])
         for j in range(2)
     ]
     small = Reduce(at, False, grad_small, small_line, *scratch[5])
-    of_qkv = Across(at, swapped, qkv_sum, *scratch[6])
-    of_small = Across(at, small_line, small_sum, *scratch[7])
-    of_output = Across(at, grad_output, output_sum, *scratch[8])
+    of_qkv = Across(at, grad_qkv, 1, *scratch[6])
+    of_small = Across(at, small_line, 0, *scratch[7])
+    of_output = Across(at, grad_output, 0, *scratch[8])
+    qkv_move = Exchange(at, plans[-1], of_qkv.mine, swapped, *scratch[2])
+    spreads = [
+        Spread(at, swapped, qkv_sum, 1, *scratch[9]),
+        Spread(at, of_small.mine, small_sum, 0, *scratch[10]),
+        Spread(at, of_output.mine, output_sum, 0, *scratch[11]),
+    ]
     small.begin()
     marks = range(len(gather.events))
     for k in marks:
         gather.lines(k)
     for q in small.order:
         small.lines(q)
-    experts_move.start()
+    experts_moves[0].start()
     small.finish()
     of_small.start()
     for k in marks:
@@ -1723,28 +1709,33 @@
             normed[1, :, here], d_qkv[1], TN
         )
         grad_qkv[2 * i : 2 * i + 2] = value.astype(bf16).reshape(2, cut // 2, -1)
-    qkv_move.start()
+    of_qkv.start()
     order = sums[0].order
     for step, q in enumerate(order):
         for s in sums:
             s.lines(q)
         if step == min(1, len(order) - 1):
-            of_small.turn()
-            of_output.turn()
-        if step == min(2, len(order) - 1):
-            qkv_move.wait()
-            of_qkv.start()
+            of_small.add()
+            spreads[1].start()
+            of_output.add()
+            spreads[2].start()
+            of_qkv.add()
+            qkv_move.start()
+    for m in experts_moves[1:]:
+        m.start()
+    qkv_move.wait()
+    spreads[0].start()
     for s in sums:
         s.finish()
-    of_qkv.turn()
-    for s in (of_small, of_output, of_qkv):
+    for s in spreads:
         s.wait()
-    experts_move.wait()
+    for m in experts_moves:
+        m.wait()
 
 
 def rear(
     dh, w_output, normed, qkv_own, turned, log_sums, mixed, cosine, sine, grad_small, grads, held,
-    shards, groups, plan,
+    shards, groups, plans,
 ):
     f32, bf16 = jnp.float32, jnp.bfloat16
     sequences, rows, width = dh.shape
@@ -1753,22 +1744,27 @@
     block = jax.ShapeDtypeStruct((1, shards, rows, width), bf16)
     small_shape = grad_small.shape[:1] + grad_small.shape[2:]
     output_shape = (groups, queries // groups, width)
-    qkv_plan = Rows(qkv_own)
+    own_rows, columns = qkv_own.shape[1:]
+    quarter_shape = (shards, own_rows // groups, columns)
+    qkv_plan = Rows(jax.ShapeDtypeStruct(quarter_shape, bf16))
     scratch = [
         Gather.scratch(dh, False, shards),
-        Exchange.scratch(plan.block, bf16, plan.count, shards),
+        Exchange.scratch(plans[0].block, bf16, plans[0].count, shards),
         Exchange.scratch(qkv_plan.block, bf16, qkv_plan.count, shards),
         Reduce.scratch(block, False, shards),
         Reduce.scratch(block, False, shards),
         Reduce.scratch(grad_small, False, shards),
-        Across.scratch(qkv_own.shape, bf16),
+        Across.scratch(qkv_own.shape, bf16, 1),
         Across.scratch(small_shape, f32),
         Across.scratch(output_shape, bf16),
-    ]
+        Spread.scratch(),
+        Spread.scratch(),
+        Spread.scratch(),
+    ] + [Exchange.scratch(p.block, bf16, p.count, shards) for p in plans[1:]]
     any_space, vmem = pl.BlockSpec(memory_space=pl.ANY), pl.BlockSpec(memory_space=pltpu.VMEM)
     return pl.pallas_call(
         functools.partial(
-            rear_body, shards, groups, (plan, qkv_plan), tuple(len(s) for s in scratch)
+            rear_body, shards, groups, (*plans, qkv_plan), tuple(len(s) for s in scratch)
         ),
         out_shape=[
             jax.ShapeDtypeStruct(dh.shape, f32),
@@ -1787,7 +1783,7 @@
             pltpu.VMEM((length, HEAD_SIZE), f32),
             pltpu.VMEM((length, HEAD_SIZE), f32),
             pltpu.VMEM(qkv_own.shape, bf16),
-            pltpu.VMEM(qkv_own.shape, bf16),
+            pltpu.VMEM(quarter_shape, bf16),
             pltpu.VMEM(output_shape, bf16),
         ]
         + [s for some in scratch for s in some],
@@ -1847,10 +1843,22 @@
     twice = LANES // HEAD_SIZE
     cosine = jnp.tile(cosine, (1, 2 * twice))
     sine = jnp.tile(jnp.concatenate([-sine, sine], axis=1), (1, twice))
-    small_all, routes_all, qkv_own, cut_own, normed, turned, log_sums, mixed, attended = front(
+    (
+        small_all,
+        routes_all,
+        c_all,
+        qkv_own,
+        cut_own,
+        normed,
+        turned,
+        log_sums,
+        mixed,
+        attended,
+    ) = front(
         inputs.reshape(sequences, DEVICE_TOKENS, MODEL_WIDTH),
         small[None],
         jnp.transpose(routes)[None],
+        cotangent[None],
         w_output,
         cosine,
         sine,
@@ -1858,7 +1866,7 @@
         experts_cut,
         shards,
         groups,
-        [Rows(qkv_cut), Experts(experts_cut, shards, experts_here, False, (0, 0), (0, 3))],
+        Experts(experts_cut.shape, shards, experts_here, False, (0, 0), True),
     )
     small = small_all.reshape(MODEL_WIDTH, LANES)
     router_pad = jnp.where(jnp.arange(LANES) < E, small, 0)
@@ -1869,15 +1877,6 @@
     z_two = h_one * r_two
     n_two = (z_two * gain_two).astype(bf16)
 
-    n_all, c_all, experts_own = gathered(
-        [n_two[None], cotangent[None]],
-        (True, True),
-        shards,
-        groups,
-        2,
-        [experts_cut],
-        [Experts(experts_cut, shards, experts_here, False, (0, 3), (0, 0))],
-    )
     whole, extra = divmod(experts_here, shards)
     cuts = shards // extra
     owned = [(group * experts_here + shard * whole + i, i * 3 * FF, FF) for i in range(whole)]
@@ -1888,26 +1887,33 @@
     routes_pairs = jnp.transpose(
         routes_all.reshape(blocks // 2, 2, TOP, tokens), (0, 2, 1, 3)
     ).reshape(blocks // 2, TOP, 2 * tokens)
-    o_sums, d_sums, grads = experts(
+    _, o_sums, d_sums, grads, grad_experts = experts(
         jnp.stack([expert for expert, _, _ in owned]).astype(jnp.int32),
         routes_pairs,
         jnp.transpose(router_pad)[: -(-E // 16) * 16],
-        n_all[0],
-        c_all[0],
-        experts_own,
+        n_two[None],
+        c_all,
         cut_own,
+        experts_cut,
         [(start, width) for _, start, width in owned],
         slots,
         2 * TOP,
-    )
-    back, moe_sum, gate_up = reduced(
+        shards,
+        groups,
+        [
+            Experts(experts_cut.shape, shards, experts_here, False, (0, 6), False),
+            Experts(cut_own.shape, shards, experts_here, True, (0, 0), True),
+        ],
+    )
+    back, moe_sum, grad_experts = reduced(
         [d_sums[None], o_sums[None]],
         (True, True),
         shards,
         groups,
         3,
         [grads],
-        [Experts(grads, shards, experts_here, True, (0, 2), (0, 2))],
+        [Experts(grads.shape, shards, experts_here, True, (0, 4), False)],
+        [grad_experts],
     )
     back = back[0]
     outputs = (h_one + moe_sum[0]).astype(bf16)
@@ -1945,10 +1951,10 @@
         sine,
         grad_small,
         grads,
-        gate_up,
+        grad_experts,
         shards,
         groups,
-        Experts(grads, shards, experts_here, True, (2, 3), (2, 3)),
+        [Experts(grads.shape, shards, experts_here, True, (4, 6), False)],
     )
     grad_output = grad_output.reshape(own_rows, MODEL_WIDTH).astype(f32)
     grad_small = grad_small.reshape(own_rows, LANES)

time: 747 us -> 666 us (0.89)
  Pallas kernels: 687 us -> 607 us
    pallas_call x4 -> x3, Pallas kernels: 513 us -> 454 us  [the longest x1 176 us: experts(): pl.pallas_call(functools.partial(experts_body, shards, groups, tuple(plan...]
    pallas_call x1, Pallas kernels: 174 us -> 153 us  [reduced(): pl.pallas_call(functools.partial(reduce_body, shards, groups, tuple(wides...]
where the time goes in v4:
time: 666 us; the launch traced here: 658 us
  Pallas kernels  607 us (91%)
  other arithmetic  31.2 us (5%)
  local copies, waits for them, and re-layouts  15.6 us (2%)
    pallas_call x1, Pallas kernels, experts(): pl.pallas_call(functools.partial(experts_body, shards, groups, tuple(plan...  176 us
    pallas_call x1, Pallas kernels, reduced(): pl.pallas_call(functools.partial(reduce_body, shards, groups, tuple(wides...  153 us
    pallas_call x1, Pallas kernels, front(): pl.pallas_call(functools.partial(front_body, shards, groups, plans, tuple...  147 us
    pallas_call x1, Pallas kernels, rear(): pl.pallas_call(functools.partial(rear_body, shards, groups, (*plans, qkv_...  131 us

profile of v4, /device:TPU:10, one launch (start us, length us, event | category | flops | bytes accessed | tf_op | source)
XLA Modules:
  0.0 658.0 jit_solution(2301897835917676286)
XLA Ops:
  0.7 0.8 broadcast_in_dim.64
  1.5 0.7 broadcast_in_dim.63
  2.2 0.9 copy.83
  3.1 0.7 fusion.18.refs_1_
  4.2 0.8 copy.91.refs_5_.refs_7_
  5.1 0.8 copy.92.refs_6_.refs_8_
  7.2 0.7 copy-done.6
  8.9 1.4 maximum_bitcast_fusion.refs_7_
  10.3 147.3 %shard_map.186 = (bf16[1,8,192,128]{3,2,1,0:T(8,128)(2,1)}, s32[1,32,8,128]{3,2,1,0:T(8,128)}, bf16[1,32,128,1536]{3,2,1,0:T(8,128)(2,1)}, bf16[8,192,320]{2,1,0...) custom-call(bf16[2,64,1536]{2,1,0:T(8,128)(2,1)} %bitcast.85, ...), custom_call_target="tpu_custom_call" | custom-call | flops 4000000000 | bytes 100000000 | tf_op jit(solution)/shard_map/pallas_call | solution.py:1587
  157.7 1.4 multiply_reduce_fusion.3
  159.7 1.0 convert_reduce_fusion
  162.3 0.9 fusion.30.refs_3_
  163.2 175.7 %shard_map.187 = (bf16[1,32,128,1536]{3,2,1,0:T(8,128)(2,1)}, bf16[32,128,1536]{2,1,0:T(8,128)(2,1)}, bf16[32,144,1536]{2,1,0:T(8,128)(2,1)}, bf16[8,192,1920]{2,1,0:T(8,128)(2,1)}, bf16[10,192,1536]{2,1,0:T(8,128)(2,1)}) custom-call(s32[2]{0:T(128)} %pad_add_fusion.refs_0_, s32[16,8,256]{2,1,0:T(8,128)} %bitcast.102, bf16[48,1536]{1,0:T(8,128)(2,1)} %slice.55.refs_2_, ...), custom_call_target="tpu_custom_call" | custom-call | flops 22649241600 | bytes 209715200 | tf_op jit(solution)/shard_map/pallas_call | solution.py:1373
  338.8 153.2 %shard_map.188 = (f32[1,144,1536]{2,1,0:T(8,128)}, f32[1,128,1536]{2,1,0:T(8,128)}, bf16[10,192,1536]{2,1,0:T(8,128)(2,1)}) custom-call(bf16[1,32,144,1536]{3,2,1,0:T(8,128)(2,1)} %bitcast.77, bf16[1,32,128,1536]{3,2,1,0:T(8,128)(2,1)} %bitcast.78, bf16[8,192,1920]{2,1,0:T(8,128)(2,1)} %get-tuple-element.39.refs_2_.refs_10_, ...), custom_call_target="tpu_custom_call", output_to_operand_aliasing={{2}: (3, {})} | custom-call | bytes 770703360 | tf_op jit(solution)/shard_map/pallas_call | solution.py:1119
  492.1 1.4 multiply_convert_fusion
  493.5 1.3 fusion.9
  494.8 0.7 select_reduce_fusion.1
  496.9 0.7 select_reduce_fusion
  497.7 1.5 multiply_reduce_fusion.1
  499.2 1.0 fusion.25
  500.8 0.8 copy.111
  501.5 130.8 %shard_map.189 = (f32[2,64,1536]{2,1,0:T(8,128)}, f32[4,48,128]{2,1,0:T(8,128)}, bf16[8,192,320]{2,1,0:T(8,128)(2,1)}, f32[4,48,128]{2,1,0:T(8,128)}, bf16[4,48,...) custom-call(bf16[2,64,1536]{2,1,0:T(8,128)(2,1)} %bitcast.97, ...), custom_call_target="tpu_custom_call", output_to_operand_aliasing={{5}: (11, {})} | custom-call | flops 8000000000 | bytes 100000000 | tf_op jit(solution)/shard_map/pallas_call | solution.py:1765
  632.3 1.5 fusion.2
  633.8 3.6 fusion.5
  637.4 1.1 convert_bitcast_fusion.3
  639.1 0.9 copy.98
  640.6 1.7 multiply_reduce_fusion
  642.3 1.5 copy.99
  644.5 0.9 copy.105
  645.4 0.9 copy.106
  646.4 1.2 bitcast_convert_fusion
  649.0 8.8 %convert_bitcast_fusion = f32[192,10,1536]{2,0,1:T(8,128)} fusion(bf16[10,192,1536]{2,1,0:T(8,128)(2,1)} %get-tuple-element.53), kind=kLoop, calls=%fused_computation | loop fusion | flops 2949120 | bytes 17694720 | tf_op jit(solution)/shard_map/convert_element_type | solution.py:1961
  (84 shorter events, 9.9 us)
Async XLA Ops:
  0.6 5.3 copy-start.18
  0.7 6.4 copy-start.19
  2.2 5.9 copy-start.10
  6.1 0.7 copy-start.8
  7.2 0.7 copy-start.6
  10.3 147.4 %copy-start.5 = (bf16[128,1536]{1,0:T(8,128)(2,1)S(1)}, bf16[128,1536]{1,0:T(8,128)(2,1)}, u32[]{:S(2)}) copy-start(bf16[128,1536]{1,0:T(8,128)(2,1)} %param.11) | copy-start | bytes 1179652
  157.7 2.0 copy-start.2
  159.1 3.2 copy-start
  159.7 3.5 copy-start.20
  160.7 2.4 copy-start.16
  492.0 5.6 copy-start.1
  492.0 5.6 copy-start.13
  492.0 7.1 %copy-start.12 = (bf16[128,1536]{1,0:T(8,128)(2,1)S(1)}, bf16[128,1536]{1,0:T(8,128)(2,1)}, u32[]{:S(2)}) copy-start(bf16[128,1536]{1,0:T(8,128)(2,1)} %param.12) | copy-start | bytes 1179652
  492.1 7.1 %copy-start.17 = (f32[1536]{0:T(1024)S(1)}, f32[1536]{0:T(1024)}, u32[]{:S(2)}) copy-start(f32[1536]{0:T(1024)} %copy-done.16) | copy-start | bytes 18436
  492.1 7.1 %copy-start.21 = (f32[128]{0:T(128)S(1)}, f32[128]{0:T(128)}, u32[]{:S(2)}) copy-start(f32[128]{0:T(128)} %copy-done.20) | copy-start | bytes 1540
  499.1 1.1 copy-start.3
  499.2 2.4 copy-start.22
  633.8 3.6 copy-start.11
  637.4 1.4 copy-start.9
  640.0 3.8 copy-start.7
  640.6 4.9 copy-start.4
  640.6 3.4 copy-start.23
  642.3 4.1 copy-start.14
  643.8 3.7 copy-start.15
